TPU v7x, 8 devices: a whole 2x2x1 slice. The times are simulated.
8 devices in a mesh: dp: 1 (over z), tp: 8 (over x, y, core).
Axes of the slice: x: 2, y: 2, z: 1, core: 2. Of those that a mesh axis runs over, the one named last changes fastest.
Arguments:
- x: bfloat16 [2048, 3072], P('dp')
- dy: bfloat16 [2048, 3072], P('dp')
- gate: bfloat16 [2048, 8192], P('dp', 'tp')
- up: bfloat16 [2048, 8192], P('dp', 'tp')
- w_gate: bfloat16 [3072, 8192], P(None, 'tp')
- w_up: bfloat16 [3072, 8192], P(None, 'tp')
- w_down: bfloat16 [8192, 3072], P('tp')
Outputs:
- output 1: bfloat16 [2048, 3072], P('dp')
- output 2: bfloat16 [3072, 8192], P('dp', 'tp')
- output 3: bfloat16 [3072, 8192], P('dp', 'tp')
- output 4: bfloat16 [8192, 3072], P(('dp', 'tp'))
All inputs are finite; a program needn't handle non-finite values.
Results may differ from a plain program's by a relative error of at most 0.012.
Values are sent between devices in bfloat16 or wider.
A program may use at most 2 GiB of HBM per device.

v0:
```python
import jax
import jax.numpy as jnp
from jax import lax
from jax.sharding import PartitionSpec as P


def act(gate, up):
    return jax.nn.silu(gate) * up


def solution(mesh):
    def step(x, dy, gate, up, w_gate, w_up, w_down):
        hidden, back = jax.vjp(act, gate.astype(jnp.float32), up.astype(jnp.float32))
        d_hidden = jnp.dot(dy, w_down.T, preferred_element_type=jnp.float32)
        d_gate, d_up = (g.astype(jnp.bfloat16) for g in back(d_hidden))
        term = jnp.dot(d_gate, w_gate.T, preferred_element_type=jnp.float32) + jnp.dot(d_up, w_up.T, preferred_element_type=jnp.float32)
        dx = lax.psum(term.astype(jnp.bfloat16), "tp")
        dw_gate = jnp.dot(x.T, d_gate, preferred_element_type=jnp.float32)
        dw_up = jnp.dot(x.T, d_up, preferred_element_type=jnp.float32)
        dw_down = jnp.dot(hidden.astype(jnp.bfloat16).T, dy, preferred_element_type=jnp.float32)
        return dx, *(g.astype(jnp.bfloat16) for g in (dw_gate, dw_up, dw_down))

    tokens, columns, rows = P("dp", None), P(None, "tp"), P("tp", None)
    return jax.shard_map(
        step,
        mesh=mesh,
        in_specs=(tokens, tokens, P("dp", "tp"), P("dp", "tp"), columns, columns, rows),
        out_specs=(tokens, P("dp", "tp"), P("dp", "tp"), P(("dp", "tp"), None)),
        check_vma=False,
    )
```

profile of v0, /device:TPU:0, one launch (start us, length us, event | category | flops | bytes accessed | tf_op | source)
XLA Modules:
  0.0 258.5 jit_solution(6754476675271447647)
XLA Ops:
  7.2 0.0 all-reduce.2.cloned.1.call-start
  7.2 24.7 %fusion.6 = (bf16[2048,1024]{1,0:T(8,128)(2,1)}, f32[2048,1024]{1,0:T(8,128)}) fusion(bf16[2048,1024]{1,0:T(8,128)(2,1)} %param.9, bf16[2048,1024]{1,0:T(8,128)(2,1)} %param.10, bf16[2048,3072]{1,0:T(8,128)(2,1)} %param.8, bf16[1024,3072]{1,0:T(8,128)(2,1)} %param.13), kind=kOutput, calls=%fused_computation.13 | convolution fusion | flops 12912164864 | bytes 39845888 | tf_op jit(solution)/shard_map/dot_general | solution.py:14
  32.0 19.8 %fusion.9 = f32[2048,3072]{1,0:T(8,128)} fusion(bf16[2048,1024]{1,0:T(8,128)(2,1)} %get-tuple-element.8, bf16[3072,1024]{1,0:T(8,128)(2,1)} %param.11), kind=kOutput, calls=%fused_computation.19 | convolution fusion | flops 12884901888 | bytes 35651584 | tf_op jit(solution)/shard_map/dot_general | solution.py:16
  51.8 25.9 %add_convert_fusion = bf16[2048,3072]{1,0:T(8,128)(2,1)} fusion(f32[2048,3072]{1,0:T(8,128)} %fusion.9, bf16[3072,1024]{1,0:T(8,128)(2,1)} %param.12, f32[2048,1024]{1,0:T(8,128)} %get-tuple-element.9, bf16[2048,1024]{1,0:T(8,128)(2,1)} %param.9), kind=kOutput, calls=%fused_computation | convolution fusion | flops 12912164864 | bytes 56623104 | tf_op jit(solution)/shard_map/dot_general | solution.py:16
  77.7 0.0 all-reduce.2.cloned.1.call-update
  77.7 18.6 %convert_bitcast_fusion.1 = bf16[3072,1024]{0,1:T(8,128)(2,1)} fusion(bf16[2048,1024]{1,0:T(8,128)(2,1)} %get-tuple-element.8, bf16[2048,3072]{1,0:T(8,128)(2,1)} %param.7), kind=kOutput, calls=%fused_computation.16 | convolution fusion | flops 12888047616 | bytes 23068672 | tf_op jit(solution)/shard_map/dot_general | solution.py:18
  96.4 8.6 %copy.11 = bf16[3072,1024]{1,0:T(8,128)(2,1)} copy(bf16[3072,1024]{0,1:T(8,128)(2,1)} %convert_bitcast_fusion.1) | data formatting | bytes 12582912
  105.0 22.4 %convert_bitcast_fusion = bf16[3072,1024]{0,1:T(8,128)(2,1)} fusion(bf16[2048,3072]{1,0:T(8,128)(2,1)} %param.7, f32[2048,1024]{1,0:T(8,128)} %get-tuple-element.9, bf16[2048,1024]{1,0:T(8,128)(2,1)} %param.9), kind=kOutput, calls=%fused_computation.15 | convolution fusion | flops 12902727680 | bytes 31457280 | tf_op jit(solution)/shard_map/dot_general | solution.py:19
  127.4 8.6 %copy.12 = bf16[3072,1024]{1,0:T(8,128)(2,1)} copy(bf16[3072,1024]{0,1:T(8,128)(2,1)} %convert_bitcast_fusion) | data formatting | bytes 12582912
  136.0 22.0 %convolution_convert_fusion = bf16[1024,3072]{1,0:T(8,128)(2,1)} fusion(bf16[2048,3072]{1,0:T(8,128)(2,1)} %param.8, bf16[2048,1024]{1,0:T(8,128)(2,1)} %param.10, bf16[2048,1024]{1,0:T(8,128)(2,1)} %param.9), kind=kOutput, calls=%fused_computation.17 | convolution fusion | flops 12904824832 | bytes 27262976 | tf_op jit(solution)/shard_map/dot_general | solution.py:20
  158.0 83.1 %all-reduce.2.cloned.1.call-done = bf16[2048,3072]{1,0:T(8,128)(2,1)} async-done(((bf16[2048,3072]{1,0:T(8,128)(2,1)}), bf16[2048,3072]{1,0:T(8,128)(2,1)}) %all-reduce.2.cloned.1.call-update) | async-done | bytes 12582928 | tf_op jit(solution)/shard_map/psum | solution.py:17
  241.1 10.5 %copy.14 = bf16[2048,3072]{1,0:T(8,128)(2,1)} copy(bf16[2048,3072]{1,0:T(8,128)(2,1)} %all-reduce.2.cloned.1.call-done) | data formatting | bytes 25165824
Async XLA Ops:
  7.2 233.9 %all-reduce.2.cloned.1.call-start = ((), (), s32[]{:S(2)}) async-start(), calls=%async_computation | async-start | bytes 25165824 | tf_op jit(solution)/shard_map/psum | solution.py:17
Sparse Core Ops, SparseCore 0:
  77.8 163.2 all-reduce.1
where the time goes:
time: 259 us; the launch traced here: 258 us
  matrix products  134 us (52%)
  waiting for transfers between devices  83.1 us (32%)
  local copies, waits for them, and re-layouts  27.8 us (11%)
  between operations  14 us (5%)
    psum x1, waiting for transfers between devices, step(): dx = lax.psum(term.astype(jnp.bfloat16), 'tp')  83.1 us
    unnamed x3, local copies, waits for them, and re-layouts  27.8 us
    dot_general x1, matrix products, step(): jnp.dot(d_up, w_up.T, preferred_element_type=jnp.float32)  25.9 us
    dot_general x1, matrix products, step(): d_hidden = jnp.dot(dy, w_down.T, preferred_element_type=jnp.float32)  24.7 us
    dot_general x1, matrix products, step(): dw_up = jnp.dot(x.T, d_up, preferred_element_type=jnp.float32)  22.4 us
    dot_general x1, matrix products, step(): jnp.dot(hidden.astype(jnp.bfloat16).T, dy, preferred_element_type=jnp.flo...  22 us
    dot_general x1, matrix products, step(): jnp.dot(d_gate, w_gate.T, preferred_element_type=jnp.float32)  19.8 us
    dot_general x1, matrix products, step(): dw_gate = jnp.dot(x.T, d_gate, preferred_element_type=jnp.float32)  18.6 us
  transfers between devices with their start and end apart: 1, of which 1 were waited for; matrix products, arithmetic and copies ran while one was open for 31% of the time, Pallas kernels for 0%

commit v1 on v0

v1 whole, which is shorter than its diff:
```python
import functools

import jax
import jax.numpy as jnp
from jax import lax
from jax.experimental import pallas as pl
from jax.experimental.pallas import tpu as pltpu
from jax.sharding import PartitionSpec as P

BF16, F32 = jnp.bfloat16, jnp.float32
ROWS, D, FL = 2048, 3072, 1024
M = 256
HALF = D // 2
W = 768
PIECES = HALF // W
STEPS = ROWS // M
ANY = pl.BlockSpec(memory_space=pl.ANY)


def nt(a, b):
    return lax.dot_general(a, b, (((1,), (1,)), ((), ())), preferred_element_type=F32)


def place():
    me = lax.axis_index("tp")
    core, y, x = me % 2, (me // 2) % 2, me // 4
    return me, core, y, x


def rows_of(p, x, y):
    diag, own = 1 - jnp.minimum(p // 2, 1), p // 6
    mid = 1 - diag - own
    block = diag * p + own * (p - 6) + mid * ((p - 2) // 2)
    flip_x = diag + mid * (p % 2)
    flip_y = diag + mid * (1 - p % 2)
    to_x = x + flip_x - 2 * x * flip_x
    to_y = y + flip_y - 2 * y * flip_y
    return ((to_x * 2 + to_y) * 2 + block) * M, diag, mid, own, block


def scatter_kernel(
    dy, gate, up, w_gate, w_up, w_down,
    shard, d_gate, d_up, hidden,
    wg, wu, wd, dyb, gb, ub, dgb, dub, hb, acc, sum_own, done,
    sib_out, sib_in, one_out, one_in, two_out, two_in,
    w_sem, in_sem, out_sem, done_sem,
    sib_s, sib_r, one_s, one_r, two_s, two_r,
):
    me, core, y, x = place()
    sibling = me + 1 - 2 * core
    near_x, near_y = me + 4 - 8 * x, me + 2 - 4 * y
    first = near_y * (1 - core) + near_x * core
    second = near_x * (1 - core) + near_y * core
    own_col, sib_col = core * HALF, (1 - core) * HALF

    def inputs(p, slot):
        row = rows_of(p, x, y)[0]
        rows = pl.ds(pl.multiple_of(row, M), M)
        return [
            pltpu.make_async_copy(dy.at[rows], dyb.at[slot], in_sem.at[slot, 0]),
            pltpu.make_async_copy(gate.at[rows], gb.at[slot], in_sem.at[slot, 1]),
            pltpu.make_async_copy(up.at[rows], ub.at[slot], in_sem.at[slot, 2]),
        ]

    def outputs(p, slot):
        row = rows_of(p, x, y)[0]
        rows = pl.ds(pl.multiple_of(row, M), M)
        return [
            pltpu.make_async_copy(dgb.at[slot], d_gate.at[rows], out_sem.at[slot, 0]),
            pltpu.make_async_copy(dub.at[slot], d_up.at[rows], out_sem.at[slot, 1]),
            pltpu.make_async_copy(hb.at[slot], hidden.at[rows], out_sem.at[slot, 2]),
        ]

    def columns(base, j):
        return pl.ds(pl.multiple_of(base + j * W, 256), W)

    down = pltpu.make_async_copy(w_down, wd, w_sem.at[0])
    wide = []
    for k, (base, j) in enumerate([(b, j) for b in (sib_col, own_col) for j in range(PIECES)]):
        at = columns(base, j)
        wide.append(pltpu.make_async_copy(w_gate.at[at], wg.at[at], w_sem.at[1 + 2 * k]))
        wide.append(pltpu.make_async_copy(w_up.at[at], wu.at[at], w_sem.at[2 + 2 * k]))

    def remote(src, dst, send, recv, to):
        return pltpu.make_async_remote_copy(
            src_ref=src, dst_ref=dst, send_sem=send, recv_sem=recv,
            device_id={"tp": to}, device_id_type=pl.DeviceIdType.MESH,
        )

    def to_sibling(p, j):
        return remote(sib_out.at[p, j], sib_in.at[p, j], sib_s.at[p, j], sib_r.at[p, j], sibling)

    def to_first(k, j):
        return remote(one_out.at[k, j], one_in.at[k, j], one_s.at[k, j], one_r.at[k, j], first)

    def to_second(k, j):
        return remote(two_out.at[k, j], two_in.at[k, j], two_s.at[k, j], two_r.at[k, j], second)

    for c in inputs(0, 0):
        c.start()
    down.start()
    for c in wide:
        c.start()

    barrier = pltpu.get_barrier_semaphore()
    for other in (sibling, first, second):
        pl.semaphore_signal(barrier, inc=1, device_id={"tp": other}, device_id_type=pl.DeviceIdType.MESH)
    pl.semaphore_wait(barrier, 3)

    def step(p, carry):
        slot = p % 2
        _, diag, mid, own, block = rows_of(p, x, y)
        is_first = diag + mid * (1 - (p + core) % 2)
        is_second = mid * ((p + core) % 2)
        for c in inputs(p, slot):
            c.wait()

        @pl.when(p < STEPS - 1)
        def _():
            for c in inputs(p + 1, 1 - slot):
                c.start()

        @pl.when(p >= 2)
        def _():
            for c in outputs(p - 2, slot):
                c.wait()

        @pl.when(p == 0)
        def _():
            down.wait()

        for n in range(FL // 256):
            at = slice(n * 256, (n + 1) * 256)
            d_hidden = nt(dyb[slot], wd[at, :])
            g, u = gb[slot, :, at].astype(F32), ub[slot, :, at].astype(F32)
            s = jax.nn.sigmoid(g)
            act = g * s
            hb[slot, :, at] = (act * u).astype(BF16)
            dub[slot, :, at] = (d_hidden * act).astype(BF16)
            dgb[slot, :, at] = (d_hidden * u * (s + act * (1 - s))).astype(BF16)
        for c in outputs(p, slot):
            c.start()

        @pl.when(p == 0)
        def _():
            for c in wide:
                c.wait()

        for j in range(PIECES):
            at = columns(sib_col, j)
            sib_out[p, j] = (nt(dgb[slot], wg[at, :]) + nt(dub[slot], wu[at, :])).astype(BF16)
            to_sibling(p, j).start()
        for j in range(PIECES):
            at = columns(own_col, j)
            acc[j] = nt(dgb[slot], wg[at, :]) + nt(dub[slot], wu[at, :])
        for j in range(PIECES):
            to_sibling(p, j).wait_recv()

            @pl.when(is_first == 1)
            def _():
                k = diag * block + mid * (2 + block)
                one_out[k, j] = (acc[j] + sib_in[p, j].astype(F32)).astype(BF16)
                to_first(k, j).start()

            @pl.when(is_second == 1)
            def _():
                to_first(block, j).wait_recv()
                two_out[block, j] = (acc[j] + sib_in[p, j].astype(F32) + one_in[block, j].astype(F32)).astype(BF16)
                to_second(block, j).start()

            @pl.when(own == 1)
            def _():
                sum_own[block, j] = acc[j] + sib_in[p, j].astype(F32)

        return carry

    lax.fori_loop(0, STEPS, step, 0)

    stores = []
    for b in range(2):
        for j in range(PIECES):
            to_first(2 + b, j).wait_recv()
            to_second(b, j).wait_recv()
            done[b, j] = (sum_own[b, j] + one_in[2 + b, j].astype(F32) + two_in[b, j].astype(F32)).astype(BF16)
            stores.append(
                pltpu.make_async_copy(
                    done.at[b, j], shard.at[pl.ds(b * M, M), pl.ds(j * W, W)], done_sem.at[b, j]
                )
            )
            stores[-1].start()
    for p in (STEPS - 2, STEPS - 1):
        for c in outputs(p, p % 2):
            c.wait()
    for j in range(PIECES):
        for p in range(STEPS):
            to_sibling(p, j).wait_send()
        for k in range(4):
            to_first(k, j).wait_send()
        for k in range(2):
            to_second(k, j).wait_send()
    for c in stores:
        c.wait()


def scatter(dy, gate, up, w_gate, w_up, w_down):
    dma = pltpu.SemaphoreType.DMA
    hid = jax.ShapeDtypeStruct((ROWS, FL), BF16)
    piece = lambda n: pltpu.VMEM((n, PIECES, M, W), BF16)
    return pl.pallas_call(
        scatter_kernel,
        out_shape=(jax.ShapeDtypeStruct((2 * M, HALF), BF16), hid, hid, hid),
        in_specs=[ANY] * 6,
        out_specs=(ANY,) * 4,
        scratch_shapes=[
            pltpu.VMEM((D, FL), BF16), pltpu.VMEM((D, FL), BF16), pltpu.VMEM((FL, D), BF16),
            pltpu.VMEM((2, M, D), BF16), pltpu.VMEM((2, M, FL), BF16), pltpu.VMEM((2, M, FL), BF16),
            pltpu.VMEM((2, M, FL), BF16), pltpu.VMEM((2, M, FL), BF16), pltpu.VMEM((2, M, FL), BF16),
            pltpu.VMEM((PIECES, M, W), F32), pltpu.VMEM((2, PIECES, M, W), F32), piece(2),
            piece(STEPS), piece(STEPS), piece(4), piece(4), piece(2), piece(2),
            dma((1 + 4 * PIECES,)), dma((2, 3)), dma((2, 3)), dma((2, PIECES)),
            dma((STEPS, PIECES)), dma((STEPS, PIECES)), dma((4, PIECES)), dma((4, PIECES)),
            dma((2, PIECES)), dma((2, PIECES)),
        ],
        compiler_params=pltpu.CompilerParams(
            collective_id=0, has_side_effects=True, vmem_limit_bytes=63 * 1024 * 1024
        ),
        cost_estimate=pl.CostEstimate(
            flops=6 * 2 * ROWS * D * FL // 2, bytes_accessed=60 * 2**20, transcendentals=2 * ROWS * FL
        ),
        name="scatter",
    )(dy, gate, up, w_gate, w_up, w_down)


def turned(a, b):
    return lax.dot_general(a, b, (((0,), (0,)), ((), ())), preferred_element_type=F32)


def wide_kernel(x, d_gate, d_up, dw_gate, dw_up, xt):
    xt[...] = x[...].T
    dw_gate[...] = jnp.dot(xt[...], d_gate[...], preferred_element_type=F32).astype(BF16)
    dw_up[...] = jnp.dot(xt[...], d_up[...], preferred_element_type=F32).astype(BF16)


def wide_grads(x, d_gate, d_up, bm=512):
    whole = pl.BlockSpec((ROWS, FL), lambda i: (0, 0))
    out = pl.BlockSpec((bm, FL), lambda i: (i, 0))
    shape = jax.ShapeDtypeStruct((D, FL), BF16)
    return pl.pallas_call(
        wide_kernel,
        grid=(D // bm,),
        out_shape=(shape, shape),
        in_specs=[pl.BlockSpec((ROWS, bm), lambda i: (0, i)), whole, whole],
        out_specs=(out, out),
        scratch_shapes=[pltpu.VMEM((bm, ROWS), BF16)],
        compiler_params=pltpu.CompilerParams(vmem_limit_bytes=50 * 1024 * 1024),
        cost_estimate=pl.CostEstimate(flops=4 * ROWS * D * FL, bytes_accessed=34 * 2**20, transcendentals=0),
        name="wide_grads",
    )(x, d_gate, d_up)


def down_kernel(hidden, dy, out, ht):
    @pl.when(pl.program_id(0) == 0)
    def _():
        ht[...] = hidden[...].T

    out[...] = jnp.dot(ht[...], dy[...], preferred_element_type=F32).astype(BF16)


def down_grad(hidden, dy, bn=512):
    return pl.pallas_call(
        down_kernel,
        grid=(D // bn,),
        out_shape=jax.ShapeDtypeStruct((FL, D), BF16),
        in_specs=[pl.BlockSpec((ROWS, FL), lambda i: (0, 0)), pl.BlockSpec((ROWS, bn), lambda i: (0, i))],
        out_specs=pl.BlockSpec((FL, bn), lambda i: (0, i)),
        scratch_shapes=[pltpu.VMEM((FL, ROWS), BF16)],
        compiler_params=pltpu.CompilerParams(vmem_limit_bytes=50 * 1024 * 1024),
        cost_estimate=pl.CostEstimate(flops=2 * ROWS * D * FL, bytes_accessed=24 * 2**20, transcendentals=0),
        name="down_grad",
    )(hidden, dy)


def assemble_kernel(*refs):
    parts, out, buf, in_sem, out_sem = refs[:8], refs[8], refs[9], refs[10], refs[11]
    me, core, y, x = place()
    reads, writes = [], []
    for k in range(8):
        c, f, s = k % 2, (k // 2) % 2, k // 4
        half = core + c - 2 * core * c
        flip_y = f * (1 - half) + s * half
        flip_x = f * half + s * (1 - half)
        to_x, to_y = x + flip_x - 2 * x * flip_x, y + flip_y - 2 * y * flip_y
        rows = pl.ds(pl.multiple_of((to_x * 2 + to_y) * 2 * M, 2 * M), 2 * M)
        cols = pl.ds(pl.multiple_of(half * HALF, HALF), HALF)
        reads.append(pltpu.make_async_copy(parts[k], buf.at[k], in_sem.at[k]))
        writes.append(pltpu.make_async_copy(buf.at[k], out.at[rows, cols], out_sem.at[k]))
    for c in reads:
        c.start()
    for r, w in zip(reads, writes):
        r.wait()
        w.start()
    for c in writes:
        c.wait()


def assemble(parts):
    return pl.pallas_call(
        assemble_kernel,
        out_shape=jax.ShapeDtypeStruct((ROWS, D), BF16),
        in_specs=[ANY] * 8,
        out_specs=ANY,
        scratch_shapes=[
            pltpu.VMEM((8, 2 * M, HALF), BF16), pltpu.SemaphoreType.DMA((8,)), pltpu.SemaphoreType.DMA((8,)),
        ],
        compiler_params=pltpu.CompilerParams(vmem_limit_bytes=20 * 1024 * 1024),
        cost_estimate=pl.CostEstimate(flops=10**9, bytes_accessed=24 * 2**20, transcendentals=0),
        name="assemble",
    )(*parts)


def index(x, y, core):
    return (x * 2 + y) * 2 + core


def pairs(to):
    return [(index(x, y, c), index(*to(x, y, c))) for x in (0, 1) for y in (0, 1) for c in (0, 1)]


FIRST = pairs(lambda x, y, c: (x, 1 - y, c) if c == 0 else (1 - x, y, c))
SECOND = pairs(lambda x, y, c: (1 - x, y, c) if c == 0 else (x, 1 - y, c))
SIBLING = pairs(lambda x, y, c: (x, y, 1 - c))


def solution(mesh):
    def step(x, dy, gate, up, w_gate, w_up, w_down):
        shard, d_gate, d_up, hidden = scatter(dy, gate, up, w_gate, w_up, w_down)
        send = functools.partial(lax.ppermute, axis_name="tp")
        from_first, from_second = send(shard, perm=FIRST), send(shard, perm=SECOND)
        own_twin = send(shard, perm=SIBLING)
        from_both = send(from_first, perm=SECOND)
        first_twin, second_twin = send(from_first, perm=SIBLING), send(from_second, perm=SIBLING)
        both_twin = send(from_both, perm=SIBLING)
        dw_gate, dw_up = wide_grads(x, d_gate, d_up)
        dw_down = down_grad(hidden, dy)
        dx = assemble(
            (shard, own_twin, from_first, first_twin, from_second, second_twin, from_both, both_twin)
        )
        return dx, dw_gate, dw_up, dw_down

    tokens, columns, rows = P("dp", None), P(None, "tp"), P("tp", None)
    return jax.shard_map(
        step,
        mesh=mesh,
        in_specs=(tokens, tokens, P("dp", "tp"), P("dp", "tp"), columns, columns, rows),
        out_specs=(tokens, P("dp", "tp"), P("dp", "tp"), P(("dp", "tp"), None)),
        check_vma=False,
    )
```

time: 259 us -> 187 us (0.72)
  matrix products: 134 us -> 0 us
  Pallas kernels: 0 us -> 130 us
  waiting for transfers between devices: 83.1 us -> 52 us
  local copies, waits for them, and re-layouts: 27.8 us -> 0.01 us
  between operations: 14 us -> 0.67 us
  starting transfers between devices: 0.04 us -> 4.31 us
    dot_general x6 -> x0, matrix products: 134 us -> none  [the longest x1 25.9 us: step(): jnp.dot(d_up, w_up.T, preferred_element_type=jnp.float32)]
    pallas_call x0 -> x4, Pallas kernels: none -> 130 us  [the longest x1 72.6 us: scatter(): pl.pallas_call(scatter_kernel, out_shape=(jax.ShapeDtypeStruct((2 * M, HA...]
    psum x1 -> x0, waiting for transfers between devices: 83.1 us -> none  [step(): dx = lax.psum(term.astype(jnp.bfloat16), 'tp')]
    ppermute x0 -> x7, waiting for transfers between devices: none -> 52 us  [the longest x1 33.7 us: step(): send(shard, perm=FIRST)]
    unnamed x3 -> x2, local copies, waits for them, and re-layouts: 27.8 us -> 0.01 us
    ppermute x0 -> x7, starting transfers between devices: none -> 4.31 us  [the longest x1 1.59 us: step(): from_both = send(from_first, perm=SECOND)]
  transfers between devices with their start and end apart: 1 -> 7, of which waited for: 1 -> 2; matrix products, arithmetic and copies ran while one was open for 31% -> 0% of each run, Pallas kernels for 0% -> 28%
where the time goes in v1:
time: 187 us
  Pallas kernels  130 us (70%)
  waiting for transfers between devices  52 us (28%)
  starting transfers between devices  4.31 us (2%)
    pallas_call x1, Pallas kernels, scatter(): pl.pallas_call(scatter_kernel, out_shape=(jax.ShapeDtypeStruct((2 * M, HA...  72.6 us
    ppermute x1, waiting for transfers between devices, step(): send(shard, perm=FIRST)  33.7 us
    pallas_call x1, Pallas kernels, wide_grads(): pl.pallas_call(wide_kernel, grid=(D // bm,), out_shape=(shape, shape), in...  32.3 us
    pallas_call x1, Pallas kernels, down_grad(): pl.pallas_call(down_kernel, grid=(D // bn,), out_shape=jax.ShapeDtypeStru...  19.2 us
    ppermute x1, waiting for transfers between devices, step(): from_both = send(from_first, perm=SECOND)  18.3 us
    pallas_call x1, Pallas kernels, assemble(): pl.pallas_call(assemble_kernel, out_shape=jax.ShapeDtypeStruct((ROWS, D),...  5.61 us
  transfers between devices with their start and end apart: 7, of which 2 were waited for; matrix products, arithmetic and copies ran while one was open for 0% of the time, Pallas kernels for 28%

profile of v1, /device:TPU:0, one launch (start us, length us, event | category | flops | bytes accessed | tf_op | source)
XLA Modules:
  0.0 186.6 jit_solution(14243454978948006539)
XLA Ops:
  0.6 72.6 %scatter.1 = (bf16[512,1536]{1,0:T(8,128)(2,1)}, bf16[2048,1024]{1,0:T(8,128)(2,1)}, bf16[2048,1024]{1,0:T(8,128)(2,1)}, bf16[2048,1024]{1,0:T(8,128)(2,1)}) custom-call(bf16[2048,3072]{1,0:T(8,128)(2,1)} %dy.3, bf16[2048,1024]{1,0:T(8,128)(2,1)} %gate.1, bf16[2048,1024]{1,0:T(8,128)(2,1)} %up.1, bf16[3072,1024]{1,0:T(8,128)(2,1)} %w_gate.1, ...), custom_call_target="tpu_custom_call" | custom-call | flops 38654705664 | bytes 62914560 | tf_op jit(solution)/shard_map/scatter/pallas_call | solution.py:209
  73.2 1.5 collective-permute-start.1
  74.8 0.7 collective-permute-start.3
  75.4 33.7 %collective-permute-done.1.refs_2_ = bf16[512,1536]{1,0:T(8,128)(2,1)S(1)} collective-permute-done((bf16[512,1536]{1,0:T(8,128)(2,1)}, bf16[512,1536]{1,0:T(8,128)(2,1)S(1)}, u32[]{:S(2)}, u32[]{:S(2)}) %collective-permute-start.1) | collective-permute-done | bytes 1572896 | tf_op jit(solution)/shard_map/ppermute | solution.py:338
  109.1 1.6 collective-permute-start.5
  110.7 0.0 collective-permute-start
  110.7 0.5 collective-permute-start.2
  111.2 0.0 collective-permute-done.3.refs_4_
  111.2 0.0 collective-permute-start.4
  111.2 18.3 %collective-permute-done.5.refs_6_ = bf16[512,1536]{1,0:T(8,128)(2,1)S(1)} collective-permute-done((bf16[512,1536]{1,0:T(8,128)(2,1)S(1)}, bf16[512,1536]{1,0:T(8,128)(2,1)S(1)}, u32[]{:S(2)}, u32[]{:S(2)}) %collective-permute-start.5) | collective-permute-done | bytes 1572896 | tf_op jit(solution)/shard_map/ppermute | solution.py:340
  129.5 0.0 collective-permute-start.6
  129.5 32.3 %wide_grads.1 = (bf16[3072,1024]{1,0:T(8,128)(2,1)}, bf16[3072,1024]{1,0:T(8,128)(2,1)}) custom-call(bf16[2048,3072]{1,0:T(8,128)(2,1)} %x.1, bf16[2048,1024]{1,0:T(8,128)(2,1)} %get-tuple-element.11.d_gate, bf16[2048,1024]{1,0:T(8,128)(2,1)} %get-tuple-element.12.d_up), custom_call_target="tpu_custom_call" | custom-call | flops 25769803776 | bytes 35651584 | tf_op jit(solution)/shard_map/wide_grads/pallas_call | solution.py:248
  161.8 0.0 copy-start
  161.8 19.2 %down_grad.1 = bf16[1024,3072]{1,0:T(8,128)(2,1)} custom-call(bf16[2048,1024]{1,0:T(8,128)(2,1)} %get-tuple-element.15.hidden, bf16[2048,3072]{1,0:T(8,128)(2,1)} %dy.3), custom_call_target="tpu_custom_call" | custom-call | flops 12884901888 | bytes 25165824 | tf_op jit(solution)/shard_map/down_grad/pallas_call | solution.py:270
  181.0 0.0 collective-permute-done.refs_1_
  181.0 0.0 collective-permute-done.4.refs_5_
  181.0 0.0 collective-permute-done.2.refs_3_
  181.0 0.0 collective-permute-done.6.refs_7_
  181.0 0.0 copy-done
  181.0 5.6 %assemble.1 = bf16[2048,3072]{1,0:T(8,128)(2,1)} custom-call(bf16[512,1536]{1,0:T(8,128)(2,1)S(1)} %copy-done, bf16[512,1536]{1,0:T(8,128)(2,1)S(1)} %collective-permute-done.refs_1_, bf16[512,1536]{1,0:T(8,128)(2,1)S(1)} %collective-permute-done.1.refs_2_, bf16[512,1536]{1,0:T(8,128)(2,1)S(1)} %collective-permute-done.2.refs_3_, ...), custom_call_target="tpu_custom_call" | custom-call | flops 1000000000 | bytes 25165824 | tf_op jit(solution)/shard_map/assemble/pallas_call | solution.py:307
Async XLA Ops:
  73.2 35.9 %collective-permute-start.1 = (bf16[512,1536]{1,0:T(8,128)(2,1)}, bf16[512,1536]{1,0:T(8,128)(2,1)S(1)}, u32[]{:S(2)}, u32[]{:S(2)}) collective-permute-start(bf16[512,1536]{1,0:T(8,128)(2,1)} %get-tuple-element.10.refs_0_), channel_id=1, source_target_pairs={{0,2},{1,5},{2,0},{3,7},{4,6},{5,1},{6,4},{7,3}} | collective-permute-start | bytes 4718600 | tf_op jit(solution)/shard_map/ppermute | solution.py:338
  74.8 36.4 %collective-permute-start.3 = (bf16[512,1536]{1,0:T(8,128)(2,1)}, bf16[512,1536]{1,0:T(8,128)(2,1)S(1)}, u32[]{:S(2)}, u32[]{:S(2)}) collective-permute-start(bf16[512,1536]{1,0:T(8,128)(2,1)} %get-tuple-element.10.refs_0_), channel_id=1, source_target_pairs={{0,4},{1,3},{2,6},{3,1},{4,0},{5,7},{6,2},{7,5}} | collective-permute-start | bytes 4718600 | tf_op jit(solution)/shard_map/ppermute | solution.py:338
  109.1 20.4 %collective-permute-start.5 = (bf16[512,1536]{1,0:T(8,128)(2,1)S(1)}, bf16[512,1536]{1,0:T(8,128)(2,1)S(1)}, u32[]{:S(2)}, u32[]{:S(2)}) collective-permute-start(bf16[512,1536]{1,0:T(8,128)(2,1)S(1)} %collective-permute-done.1.refs_2_), channel_id=1, source_target_pairs={{0,4},{1,3},{2,6},{3,1},{4,0},{5,7},{6,2},{7,5}} | collective-permute-start | bytes 4718600 | tf_op jit(solution)/shard_map/ppermute | solution.py:340
  110.7 70.3 %collective-permute-start = (bf16[512,1536]{1,0:T(8,128)(2,1)}, bf16[512,1536]{1,0:T(8,128)(2,1)S(1)}, u32[]{:S(2)}, u32[]{:S(2)}) collective-permute-start(bf16[512,1536]{1,0:T(8,128)(2,1)} %get-tuple-element.10.refs_0_), channel_id=1, source_target_pairs={{0,1},{1,0},{2,3},{3,2},{4,5},{5,4},{6,7},{7,6}} | collective-permute-start | bytes 4718600 | tf_op jit(solution)/shard_map/ppermute | solution.py:339
  110.7 70.3 %collective-permute-start.2 = (bf16[512,1536]{1,0:T(8,128)(2,1)S(1)}, bf16[512,1536]{1,0:T(8,128)(2,1)S(1)}, u32[]{:S(2)}, u32[]{:S(2)}) collective-permute-start(bf16[512,1536]{1,0:T(8,128)(2,1)S(1)} %collective-permute-done.1.refs_2_), channel_id=1, source_target_pairs={{0,1},{1,0},{2,3},{3,2},{4,5},{5,4},{6,7},{7,6}} | collective-permute-start | bytes 4718600 | tf_op jit(solution)/shard_map/ppermute | solution.py:341
  111.2 69.8 %collective-permute-start.4 = (bf16[512,1536]{1,0:T(8,128)(2,1)S(1)}, bf16[512,1536]{1,0:T(8,128)(2,1)S(1)}, u32[]{:S(2)}, u32[]{:S(2)}) collective-permute-start(bf16[512,1536]{1,0:T(8,128)(2,1)S(1)} %collective-permute-done.3.refs_4_), channel_id=1, source_target_pairs={{0,1},{1,0},{2,3},{3,2},{4,5},{5,4},{6,7},{7,6}} | collective-permute-start | bytes 4718600 | tf_op jit(solution)/shard_map/ppermute | solution.py:341
  129.5 51.5 %collective-permute-start.6 = (bf16[512,1536]{1,0:T(8,128)(2,1)S(1)}, bf16[512,1536]{1,0:T(8,128)(2,1)S(1)}, u32[]{:S(2)}, u32[]{:S(2)}) collective-permute-start(bf16[512,1536]{1,0:T(8,128)(2,1)S(1)} %collective-permute-done.5.refs_6_), channel_id=1, source_target_pairs={{0,1},{1,0},{2,3},{3,2},{4,5},{5,4},{6,7},{7,6}} | collective-permute-start | bytes 4718600 | tf_op jit(solution)/shard_map/ppermute | solution.py:342
  161.8 19.2 %copy-start = (bf16[512,1536]{1,0:T(8,128)(2,1)S(1)}, bf16[512,1536]{1,0:T(8,128)(2,1)}, u32[]{:S(2)}) copy-start(bf16[512,1536]{1,0:T(8,128)(2,1)} %get-tuple-element.10.refs_0_) | copy-start | bytes 4718596

commit v2 on v1

--- a/solution.py
+++ b/solution.py
@@ -1,11 +1,10 @@
-import functools
-
 import jax
 import jax.numpy as jnp
 from jax import lax
 from jax.experimental import pallas as pl
 from jax.experimental.pallas import tpu as pltpu
 from jax.sharding import PartitionSpec as P
+
 
 BF16, F32 = jnp.bfloat16, jnp.float32
 ROWS, D, FL = 2048, 3072, 1024
@@ -231,10 +230,6 @@
     )(dy, gate, up, w_gate, w_up, w_down)
 
 
-def turned(a, b):
-    return lax.dot_general(a, b, (((0,), (0,)), ((), ())), preferred_element_type=F32)
-
-
 def wide_kernel(x, d_gate, d_up, dw_gate, dw_up, xt):
     xt[...] = x[...].T
     dw_gate[...] = jnp.dot(xt[...], d_gate[...], preferred_element_type=F32).astype(BF16)
@@ -282,7 +277,7 @@
 
 def assemble_kernel(*refs):
     parts, out, buf, in_sem, out_sem = refs[:8], refs[8], refs[9], refs[10], refs[11]
-    me, core, y, x = place()
+    _, core, y, x = place()
     reads, writes = [], []
     for k in range(8):
         c, f, s = k % 2, (k // 2) % 2, k // 4
@@ -332,14 +327,17 @@
 
 
 def solution(mesh):
+    def send(value, perm):
+        return lax.ppermute(value, "tp", perm)
+
     def step(x, dy, gate, up, w_gate, w_up, w_down):
         shard, d_gate, d_up, hidden = scatter(dy, gate, up, w_gate, w_up, w_down)
-        send = functools.partial(lax.ppermute, axis_name="tp")
-        from_first, from_second = send(shard, perm=FIRST), send(shard, perm=SECOND)
-        own_twin = send(shard, perm=SIBLING)
-        from_both = send(from_first, perm=SECOND)
-        first_twin, second_twin = send(from_first, perm=SIBLING), send(from_second, perm=SIBLING)
-        both_twin = send(from_both, perm=SIBLING)
+        from_first, from_second = send(shard, FIRST), send(shard, SECOND)
+        own_twin = send(shard, SIBLING)
+        from_both = send(from_first, SECOND)
+        first_twin = send(from_first, SIBLING)
+        second_twin = send(from_second, SIBLING)
+        both_twin = send(from_both, SIBLING)
         dw_gate, dw_up = wide_grads(x, d_gate, d_up)
         dw_down = down_grad(hidden, dy)
         dx = assemble(

time: 187 us -> 187 us (level)
  no operation moved by 1% of the time
where the time goes in v2:
time: 187 us
  Pallas kernels  130 us (70%)
  waiting for transfers between devices  52.2 us (28%)
  starting transfers between devices  4.16 us (2%)
    pallas_call x1, Pallas kernels, scatter(): pl.pallas_call(scatter_kernel, out_shape=(jax.ShapeDtypeStruct((2 * M, HA...  72.6 us
    ppermute x7, waiting for transfers between devices, send(): return lax.ppermute(value, 'tp', perm)  52.2 us
    pallas_call x1, Pallas kernels, wide_grads(): pl.pallas_call(wide_kernel, grid=(D // bm,), out_shape=(shape, shape), in...  32.3 us
    pallas_call x1, Pallas kernels, down_grad(): pl.pallas_call(down_kernel, grid=(D // bn,), out_shape=jax.ShapeDtypeStru...  19.2 us
    pallas_call x1, Pallas kernels, assemble(): pl.pallas_call(assemble_kernel, out_shape=jax.ShapeDtypeStruct((ROWS, D),...  5.61 us
    ppermute x7, starting transfers between devices, send(): return lax.ppermute(value, 'tp', perm)  4.16 us
  transfers between devices with their start and end apart: 7, of which 2 were waited for; matrix products, arithmetic and copies ran while one was open for 0% of the time, Pallas kernels for 28%

profile of v2, /device:TPU:0, one launch (start us, length us, event | category | flops | bytes accessed | tf_op | source)
XLA Modules:
  0.0 186.7 jit_solution(14243454978948006539)
XLA Ops:
  0.6 72.6 %scatter.1 = (bf16[512,1536]{1,0:T(8,128)(2,1)}, bf16[2048,1024]{1,0:T(8,128)(2,1)}, bf16[2048,1024]{1,0:T(8,128)(2,1)}, bf16[2048,1024]{1,0:T(8,128)(2,1)}) custom-call(bf16[2048,3072]{1,0:T(8,128)(2,1)} %dy.3, bf16[2048,1024]{1,0:T(8,128)(2,1)} %gate.1, bf16[2048,1024]{1,0:T(8,128)(2,1)} %up.1, bf16[3072,1024]{1,0:T(8,128)(2,1)} %w_gate.1, ...), custom_call_target="tpu_custom_call" | custom-call | flops 38654705664 | bytes 62914560 | tf_op jit(solution)/shard_map/scatter/pallas_call | solution.py:208
  73.2 1.5 collective-permute-start.1
  74.8 0.6 collective-permute-start.3
  75.3 33.9 %collective-permute-done.1.refs_2_ = bf16[512,1536]{1,0:T(8,128)(2,1)S(1)} collective-permute-done((bf16[512,1536]{1,0:T(8,128)(2,1)}, bf16[512,1536]{1,0:T(8,128)(2,1)S(1)}, u32[]{:S(2)}, u32[]{:S(2)}) %collective-permute-start.1) | collective-permute-done | bytes 1572896 | tf_op jit(solution)/shard_map/ppermute | solution.py:331
  109.2 1.5 collective-permute-start.5
  110.7 0.0 collective-permute-start
  110.7 0.5 collective-permute-start.2
  111.3 0.0 collective-permute-done.3.refs_4_
  111.3 0.0 collective-permute-start.4
  111.3 18.4 %collective-permute-done.5.refs_6_ = bf16[512,1536]{1,0:T(8,128)(2,1)S(1)} collective-permute-done((bf16[512,1536]{1,0:T(8,128)(2,1)S(1)}, bf16[512,1536]{1,0:T(8,128)(2,1)S(1)}, u32[]{:S(2)}, u32[]{:S(2)}) %collective-permute-start.5) | collective-permute-done | bytes 1572896 | tf_op jit(solution)/shard_map/ppermute | solution.py:331
  129.6 0.0 collective-permute-start.6
  129.6 32.3 %wide_grads.1 = (bf16[3072,1024]{1,0:T(8,128)(2,1)}, bf16[3072,1024]{1,0:T(8,128)(2,1)}) custom-call(bf16[2048,3072]{1,0:T(8,128)(2,1)} %x.1, bf16[2048,1024]{1,0:T(8,128)(2,1)} %get-tuple-element.11.d_gate, bf16[2048,1024]{1,0:T(8,128)(2,1)} %get-tuple-element.12.d_up), custom_call_target="tpu_custom_call" | custom-call | flops 25769803776 | bytes 35651584 | tf_op jit(solution)/shard_map/wide_grads/pallas_call | solution.py:243
  161.9 0.0 copy-start
  161.9 19.2 %down_grad.1 = bf16[1024,3072]{1,0:T(8,128)(2,1)} custom-call(bf16[2048,1024]{1,0:T(8,128)(2,1)} %get-tuple-element.15.hidden, bf16[2048,3072]{1,0:T(8,128)(2,1)} %dy.3), custom_call_target="tpu_custom_call" | custom-call | flops 12884901888 | bytes 25165824 | tf_op jit(solution)/shard_map/down_grad/pallas_call | solution.py:265
  181.1 0.0 collective-permute-done.refs_1_
  181.1 0.0 collective-permute-done.4.refs_5_
  181.1 0.0 collective-permute-done.2.refs_3_
  181.1 0.0 collective-permute-done.6.refs_7_
  181.1 0.0 copy-done
  181.1 5.6 %assemble.1 = bf16[2048,3072]{1,0:T(8,128)(2,1)} custom-call(bf16[512,1536]{1,0:T(8,128)(2,1)S(1)} %copy-done, bf16[512,1536]{1,0:T(8,128)(2,1)S(1)} %collective-permute-done.refs_1_, bf16[512,1536]{1,0:T(8,128)(2,1)S(1)} %collective-permute-done.1.refs_2_, bf16[512,1536]{1,0:T(8,128)(2,1)S(1)} %collective-permute-done.2.refs_3_, ...), custom_call_target="tpu_custom_call" | custom-call | flops 1000000000 | bytes 25165824 | tf_op jit(solution)/shard_map/assemble/pallas_call | solution.py:302
Async XLA Ops:
  73.2 36.0 %collective-permute-start.1 = (bf16[512,1536]{1,0:T(8,128)(2,1)}, bf16[512,1536]{1,0:T(8,128)(2,1)S(1)}, u32[]{:S(2)}, u32[]{:S(2)}) collective-permute-start(bf16[512,1536]{1,0:T(8,128)(2,1)} %get-tuple-element.10.refs_0_), channel_id=1, source_target_pairs={{0,2},{1,5},{2,0},{3,7},{4,6},{5,1},{6,4},{7,3}} | collective-permute-start | bytes 4718600 | tf_op jit(solution)/shard_map/ppermute | solution.py:331
  74.8 36.5 %collective-permute-start.3 = (bf16[512,1536]{1,0:T(8,128)(2,1)}, bf16[512,1536]{1,0:T(8,128)(2,1)S(1)}, u32[]{:S(2)}, u32[]{:S(2)}) collective-permute-start(bf16[512,1536]{1,0:T(8,128)(2,1)} %get-tuple-element.10.refs_0_), channel_id=1, source_target_pairs={{0,4},{1,3},{2,6},{3,1},{4,0},{5,7},{6,2},{7,5}} | collective-permute-start | bytes 4718600 | tf_op jit(solution)/shard_map/ppermute | solution.py:331
  109.2 20.4 %collective-permute-start.5 = (bf16[512,1536]{1,0:T(8,128)(2,1)S(1)}, bf16[512,1536]{1,0:T(8,128)(2,1)S(1)}, u32[]{:S(2)}, u32[]{:S(2)}) collective-permute-start(bf16[512,1536]{1,0:T(8,128)(2,1)S(1)} %collective-permute-done.1.refs_2_), channel_id=1, source_target_pairs={{0,4},{1,3},{2,6},{3,1},{4,0},{5,7},{6,2},{7,5}} | collective-permute-start | bytes 4718600 | tf_op jit(solution)/shard_map/ppermute | solution.py:331
  110.7 70.4 %collective-permute-start = (bf16[512,1536]{1,0:T(8,128)(2,1)}, bf16[512,1536]{1,0:T(8,128)(2,1)S(1)}, u32[]{:S(2)}, u32[]{:S(2)}) collective-permute-start(bf16[512,1536]{1,0:T(8,128)(2,1)} %get-tuple-element.10.refs_0_), channel_id=1, source_target_pairs={{0,1},{1,0},{2,3},{3,2},{4,5},{5,4},{6,7},{7,6}} | collective-permute-start | bytes 4718600 | tf_op jit(solution)/shard_map/ppermute | solution.py:331
  110.7 70.4 %collective-permute-start.2 = (bf16[512,1536]{1,0:T(8,128)(2,1)S(1)}, bf16[512,1536]{1,0:T(8,128)(2,1)S(1)}, u32[]{:S(2)}, u32[]{:S(2)}) collective-permute-start(bf16[512,1536]{1,0:T(8,128)(2,1)S(1)} %collective-permute-done.1.refs_2_), channel_id=1, source_target_pairs={{0,1},{1,0},{2,3},{3,2},{4,5},{5,4},{6,7},{7,6}} | collective-permute-start | bytes 4718600 | tf_op jit(solution)/shard_map/ppermute | solution.py:331
  111.3 69.8 %collective-permute-start.4 = (bf16[512,1536]{1,0:T(8,128)(2,1)S(1)}, bf16[512,1536]{1,0:T(8,128)(2,1)S(1)}, u32[]{:S(2)}, u32[]{:S(2)}) collective-permute-start(bf16[512,1536]{1,0:T(8,128)(2,1)S(1)} %collective-permute-done.3.refs_4_), channel_id=1, source_target_pairs={{0,1},{1,0},{2,3},{3,2},{4,5},{5,4},{6,7},{7,6}} | collective-permute-start | bytes 4718600 | tf_op jit(solution)/shard_map/ppermute | solution.py:331
  129.6 51.5 %collective-permute-start.6 = (bf16[512,1536]{1,0:T(8,128)(2,1)S(1)}, bf16[512,1536]{1,0:T(8,128)(2,1)S(1)}, u32[]{:S(2)}, u32[]{:S(2)}) collective-permute-start(bf16[512,1536]{1,0:T(8,128)(2,1)S(1)} %collective-permute-done.5.refs_6_), channel_id=1, source_target_pairs={{0,1},{1,0},{2,3},{3,2},{4,5},{5,4},{6,7},{7,6}} | collective-permute-start | bytes 4718600 | tf_op jit(solution)/shard_map/ppermute | solution.py:331
  161.9 19.2 %copy-start = (bf16[512,1536]{1,0:T(8,128)(2,1)S(1)}, bf16[512,1536]{1,0:T(8,128)(2,1)}, u32[]{:S(2)}) copy-start(bf16[512,1536]{1,0:T(8,128)(2,1)} %get-tuple-element.10.refs_0_) | copy-start | bytes 4718596

commit v3 on v0

v3 whole, which is shorter than its diff:
```python
import functools

import jax
import jax.numpy as jnp
from jax import lax
from jax.experimental import pallas as pl
from jax.experimental.pallas import tpu as pltpu
from jax.sharding import PartitionSpec as P


BF16, F32 = jnp.bfloat16, jnp.float32
ROWS, D, FL = 2048, 3072, 1024
M = 256
U = M // 2
HALF = D // 2
W = 512
PIECES = HALF // W
STEPS = ROWS // M
ANY = pl.BlockSpec(memory_space=pl.ANY)


def nt(a, b):
    return lax.dot_general(a, b, (((1,), (1,)), ((), ())), preferred_element_type=F32)


def place():
    me = lax.axis_index("tp")
    core, y, x = me % 2, (me // 2) % 2, me // 4
    return me, core, y, x


def rows_of(p, x, y):
    diag, own = 1 - jnp.minimum(p // 2, 1), p // 6
    mid = 1 - diag - own
    at = diag * p * M + own * (p - 6) * M + mid * (p - 2) * U

    def run(flip_x, flip_y):
        to_x, to_y = x + flip_x - 2 * x * flip_x, y + flip_y - 2 * y * flip_y
        return (to_x * 2 + to_y) * 2 * M + at

    return run(diag, diag + mid), run(diag + mid, diag) + (1 - mid) * U


def scatter_kernel(
    dy, gate, up, w_gate, w_up, w_down,
    shard, d_gate, d_up, hidden,
    wg, wu, wd, dyb, gb, ub, dgb, dub, hb, acc, sum_own, done,
    sib_out, sib_in, one_out, one_in, two_out, two_in,
    down_sem, wide_sem, in_sem, out_sem, done_sem,
    sib_s, sib_r, one_s, one_r, two_s, two_r,
):
    me, core, y, x = place()
    sibling = me + 1 - 2 * core
    near_x, near_y = me + 4 - 8 * x, me + 2 - 4 * y
    first = near_y * (1 - core) + near_x * core
    second = near_x * (1 - core) + near_y * core
    own_col, sib_col = core * HALF, (1 - core) * HALF

    def copies(p, slot, outward):
        made = []
        arrays = ((dgb, d_gate), (dub, d_up), (hb, hidden)) if outward else ((dyb, dy), (gb, gate), (ub, up))
        for h, row in enumerate(rows_of(p, x, y)):
            rows = pl.ds(pl.multiple_of(row, U), U)
            for k, (near, far) in enumerate(arrays):
                near, far = near.at[slot, pl.ds(h * U, U)], far.at[rows]
                if outward:
                    made.append(pltpu.make_async_copy(near, far, out_sem.at[slot, h, k]))
                else:
                    made.append(pltpu.make_async_copy(far, near, in_sem.at[slot, h, k]))
        return made

    def columns(base, j):
        return pl.ds(pl.multiple_of(base + j * W, 256), W)

    down = []
    for n in range(FL // 256):
        at = pl.ds(n * 256, 256)
        down.append(pltpu.make_async_copy(w_down.at[at], wd.at[at], down_sem.at[n]))
    wide = {}
    for j in range(PIECES):
        for side, base in ((0, sib_col), (1, own_col)):
            at = columns(base, j)
            wide[side, j] = (
                pltpu.make_async_copy(w_gate.at[at], wg.at[at], wide_sem.at[side, j, 0]),
                pltpu.make_async_copy(w_up.at[at], wu.at[at], wide_sem.at[side, j, 1]),
            )

    def remote(src, dst, send, recv, to):
        return pltpu.make_async_remote_copy(
            src_ref=src, dst_ref=dst, send_sem=send, recv_sem=recv,
            device_id={"tp": to}, device_id_type=pl.DeviceIdType.MESH,
        )

    def to_sibling(p, j):
        return remote(sib_out.at[p, j], sib_in.at[p, j], sib_s, sib_r.at[p, j], sibling)

    def to_first(k, j):
        return remote(one_out.at[k, j], one_in.at[k, j], one_s, one_r.at[k, j], first)

    def to_second(k, j):
        return remote(two_out.at[k, j], two_in.at[k, j], two_s, two_r.at[k, j], second)

    for c in copies(0, 0, False):
        c.start()
    for c in down:
        c.start()

    barrier = pltpu.get_barrier_semaphore()
    for other in (sibling, first, second):
        pl.semaphore_signal(barrier, inc=1, device_id={"tp": other}, device_id_type=pl.DeviceIdType.MESH)
    pl.semaphore_wait(barrier, 3)

    def hidden_grads(slot, n):
        at = slice(n * 256, (n + 1) * 256)
        d_hidden = nt(dyb[slot], wd[at, :])
        g, u = gb[slot, :, at].astype(F32), ub[slot, :, at].astype(F32)
        s = jax.nn.sigmoid(g)
        act = g * s
        hb[slot, :, at] = (act * u).astype(BF16)
        dub[slot, :, at] = (d_hidden * act).astype(BF16)
        dgb[slot, :, at] = (d_hidden * u * (s + act * (1 - s))).astype(BF16)

    def term(slot, base, j):
        at = columns(base, j)
        return (nt(dgb[slot], wg[at, :]) + nt(dub[slot], wu[at, :])).reshape(2, U, W)

    def for_sibling(p, slot, j):
        sib_out[p, j] = term(slot, sib_col, j).astype(BF16)
        to_sibling(p, j).start()

    def chip_sum(p, j, h):
        return acc[j, h] + sib_in[p, j, h].astype(F32)

    def send_diagonal(p, j):
        for h in range(2):
            one_out[2 * p + h, j] = chip_sum(p, j, h).astype(BF16)
            to_first(2 * p + h, j).start()

    def send_middle(p):
        q = p - 2
        for j in range(PIECES):
            to_sibling(p, j).wait_recv()
            one_out[4 + q, j] = chip_sum(p, j, core).astype(BF16)
            to_first(4 + q, j).start()
        for j in range(PIECES):
            to_first(q, j).wait_recv()
            two_out[q, j] = (chip_sum(p, j, 1 - core) + one_in[q, j].astype(F32)).astype(BF16)
            to_second(q, j).start()

    def keep_own(p):
        for j in range(PIECES):
            to_sibling(p, j).wait_recv()
            for h in range(2):
                sum_own[2 * (p - 6) + h, j] = chip_sum(p, j, h)

    def diagonal_step(p, ready):
        for n in range(FL // 256):
            hidden_grads(p, n)
        for c in copies(p, p, True):
            c.start()
        for j in range(PIECES + 1):
            if j < PIECES:
                ready(0, j)
                for_sibling(p, p, j)
            if j:
                ready(1, j - 1)
                acc[j - 1] = term(p, own_col, j - 1)
                to_sibling(p, j - 1).wait_recv()
                send_diagonal(p, j - 1)

    def arrived(side, j):
        for c in wide[side, j]:
            c.wait()

    for c in copies(0, 0, False):
        c.wait()
    for j in range(PIECES):
        for side in range(2):
            for c in wide[side, j]:
                c.start()
    for c in copies(1, 1, False):
        c.start()
    for c in down:
        c.wait()
    diagonal_step(0, arrived)
    for c in copies(1, 1, False):
        c.wait()
    for c in copies(0, 0, True):
        c.wait()
    for c in copies(2, 0, False):
        c.start()
    diagonal_step(1, lambda side, j: None)

    def step(p, carry):
        slot = p % 2
        for c in copies(p, slot, False):
            c.wait()

        @pl.when(p < STEPS - 1)
        def _():
            for c in copies(p + 1, 1 - slot, False):
                c.start()

        @pl.when(p >= 3)
        def _():
            for c in copies(p - 2, slot, True):
                c.wait()

        for n in range(FL // 256):
            hidden_grads(slot, n)
        for c in copies(p, slot, True):
            c.start()

        @pl.when(jnp.logical_and(p >= 3, p < 7))
        def _():
            send_middle(p - 1)

        @pl.when(p == 7)
        def _():
            keep_own(6)

        for j in range(PIECES):
            for_sibling(p, slot, j)
        for j in range(PIECES):
            acc[j] = term(slot, own_col, j)
        return carry

    lax.fori_loop(2, STEPS, step, 0)
    keep_own(STEPS - 1)

    for q in range(4):
        for j in range(PIECES):
            to_first(4 + q, j).wait_recv()
            to_second(q, j).wait_recv()
            done[q, j] = (sum_own[q, j] + one_in[4 + q, j].astype(F32) + two_in[q, j].astype(F32)).astype(BF16)
            pltpu.make_async_copy(
                done.at[q, j], shard.at[pl.ds(q * U, U), pl.ds(j * W, W)], done_sem
            ).start()
    for p in (STEPS - 2, STEPS - 1):
        for c in copies(p, p % 2, True):
            c.wait()
    remote(sib_out, sib_in, sib_s, sib_r.at[0, 0], sibling).wait_send()
    remote(one_out, one_in, one_s, one_r.at[0, 0], first).wait_send()
    remote(two_out, two_in, two_s, two_r.at[0, 0], second).wait_send()
    pltpu.make_async_copy(shard, shard, done_sem).wait()


def scatter(dy, gate, up, w_gate, w_up, w_down):
    dma = pltpu.SemaphoreType.DMA
    hid = jax.ShapeDtypeStruct((ROWS, FL), BF16)
    units = lambda n: pltpu.VMEM((n, PIECES, U, W), BF16)
    steps = pltpu.VMEM((STEPS, PIECES, 2, U, W), BF16)
    return pl.pallas_call(
        scatter_kernel,
        out_shape=(jax.ShapeDtypeStruct((2 * M, HALF), BF16), hid, hid, hid),
        in_specs=[ANY] * 6,
        out_specs=(ANY,) * 4,
        scratch_shapes=[
            pltpu.VMEM((D, FL), BF16), pltpu.VMEM((D, FL), BF16), pltpu.VMEM((FL, D), BF16),
            pltpu.VMEM((2, M, D), BF16), pltpu.VMEM((2, M, FL), BF16), pltpu.VMEM((2, M, FL), BF16),
            pltpu.VMEM((2, M, FL), BF16), pltpu.VMEM((2, M, FL), BF16), pltpu.VMEM((2, M, FL), BF16),
            pltpu.VMEM((PIECES, 2, U, W), F32), pltpu.VMEM((4, PIECES, U, W), F32), units(4),
            steps, steps, units(8), units(8), units(4), units(4),
            dma((FL // 256,)), dma((2, PIECES, 2)), dma((2, 2, 3)), dma((2, 2, 3)), dma,
            dma, dma((STEPS, PIECES)), dma, dma((8, PIECES)), dma, dma((4, PIECES)),
        ],
        compiler_params=pltpu.CompilerParams(
            collective_id=0, has_side_effects=True, vmem_limit_bytes=63 * 1024 * 1024
        ),
        cost_estimate=pl.CostEstimate(
            flops=6 * ROWS * D * FL, bytes_accessed=60 * 2**20, transcendentals=2 * ROWS * FL
        ),
        name="scatter",
    )(dy, gate, up, w_gate, w_up, w_down)


def turned(a, b):
    return lax.dot_general(a, b, (((0,), (0,)), ((), ())), preferred_element_type=F32)


def wide_kernel(x, d_gate, d_up, *refs):
    dw_gate, dw_up, xt = refs[-3:]
    xt[...] = x[...].T
    dw_gate[...] = jnp.dot(xt[...], d_gate[...], preferred_element_type=F32).astype(BF16)
    dw_up[...] = jnp.dot(xt[...], d_up[...], preferred_element_type=F32).astype(BF16)


def wide_grads(x, d_gate, d_up, start, count, into=(), bm=512):
    whole = pl.BlockSpec((ROWS, FL), lambda i: (0, 0), pipeline_mode=pl.Buffered(1))
    out = pl.BlockSpec((bm, FL), lambda i: (start + i, 0))
    shape = jax.ShapeDtypeStruct((D, FL), BF16)
    return pl.pallas_call(
        wide_kernel,
        grid=(count,),
        out_shape=(shape, shape),
        in_specs=[pl.BlockSpec((ROWS, bm), lambda i: (0, start + i)), whole, whole] + [ANY] * len(into),
        out_specs=(out, out),
        scratch_shapes=[pltpu.VMEM((bm, ROWS), BF16)],
        input_output_aliases={3 + k: k for k in range(len(into))},
        compiler_params=pltpu.CompilerParams(vmem_limit_bytes=36 * 1024 * 1024),
        cost_estimate=pl.CostEstimate(flops=4 * ROWS * bm * count * FL, bytes_accessed=20 * 2**20, transcendentals=0),
        name="wide_grads",
    )(x, d_gate, d_up, *into)


def down_kernel(hidden, dy, out):
    out[...] = turned(hidden[...], dy[...]).astype(BF16)


def down_grad(hidden, dy, bn=512):
    return pl.pallas_call(
        down_kernel,
        grid=(D // bn,),
        out_shape=jax.ShapeDtypeStruct((FL, D), BF16),
        in_specs=[
            pl.BlockSpec((ROWS, FL), lambda i: (0, 0), pipeline_mode=pl.Buffered(1)),
            pl.BlockSpec((ROWS, bn), lambda i: (0, i)),
        ],
        out_specs=pl.BlockSpec((FL, bn), lambda i: (0, i)),
        compiler_params=pltpu.CompilerParams(vmem_limit_bytes=40 * 1024 * 1024),
        cost_estimate=pl.CostEstimate(flops=2 * ROWS * D * FL, bytes_accessed=24 * 2**20, transcendentals=0),
        name="down_grad",
    )(hidden, dy)


def write_kernel(spots, *refs):
    parts, out, sem = refs[: len(spots)], refs[-2], refs[-1]
    _, core, y, x = place()
    writes = []
    for k, (twin, along_first, along_second, row, count) in enumerate(spots):
        half = core + twin - 2 * core * twin
        flip_y = along_first * (1 - half) + along_second * half
        flip_x = along_first * half + along_second * (1 - half)
        to_x, to_y = x + flip_x - 2 * x * flip_x, y + flip_y - 2 * y * flip_y
        cols = pl.ds(pl.multiple_of(half * HALF, HALF), HALF)
        for i in range(0, count, U):
            rows = pl.ds(pl.multiple_of((to_x * 2 + to_y) * 2 * M + row + i, U), U)
            writes.append(pltpu.make_async_copy(parts[k].at[pl.ds(i, U)], out.at[rows, cols], sem.at[k, i // U]))
            writes[-1].start()
    for c in writes:
        c.wait()


def write(parts, spots, into=None):
    n = len(parts)
    given = () if into is None else (into,)
    return pl.pallas_call(
        functools.partial(write_kernel, spots),
        out_shape=jax.ShapeDtypeStruct((ROWS, D), BF16),
        in_specs=[pl.BlockSpec(memory_space=pltpu.VMEM)] * n + [ANY] * len(given),
        out_specs=ANY,
        scratch_shapes=[pltpu.SemaphoreType.DMA((n, 2 * M // U))],
        input_output_aliases={n: 0} if given else {},
        compiler_params=pltpu.CompilerParams(vmem_limit_bytes=16 * 1024 * 1024),
        cost_estimate=pl.CostEstimate(flops=10**9, bytes_accessed=24 * 2**20, transcendentals=0),
        name="write",
    )(*parts, *given)


def index(x, y, core):
    return (x * 2 + y) * 2 + core


def pairs(to):
    return [(index(x, y, c), index(*to(x, y, c))) for x in (0, 1) for y in (0, 1) for c in (0, 1)]


FIRST = pairs(lambda x, y, c: (x, 1 - y, c) if c == 0 else (1 - x, y, c))
SECOND = pairs(lambda x, y, c: (1 - x, y, c) if c == 0 else (x, 1 - y, c))
SIBLING = pairs(lambda x, y, c: (x, y, 1 - c))


def solution(mesh):
    def send(value, perm):
        return lax.ppermute(value, "tp", perm)

    def step(x, dy, gate, up, w_gate, w_up, w_down):
        shard, d_gate, d_up, hidden = scatter(dy, gate, up, w_gate, w_up, w_down)
        from_first, from_second = send(shard, FIRST), send(shard, SECOND)
        own_twin = send(shard, SIBLING)
        both_a = send(from_first[:M], SECOND)
        both_b = send(from_first[M:], SECOND)
        first_twin = send(from_first, SIBLING)
        second_twin = send(from_second, SIBLING)
        twin_a, twin_b = send(both_a, SIBLING), send(both_b, SIBLING)
        dw_down = down_grad(hidden, dy)
        wide = wide_grads(x, d_gate, d_up, 0, 3)
        dw_gate, dw_up = wide_grads(x, d_gate, d_up, 3, 3, wide)
        dx = write(
            (shard, own_twin, from_first, first_twin, from_second, second_twin),
            tuple((t, f, s, 0, 2 * M) for f, s in ((0, 0), (1, 0), (0, 1)) for t in (0, 1)),
        )
        dx = write(
            (both_a, both_b, twin_a, twin_b),
            tuple((t, 1, 1, r, M) for t in (0, 1) for r in (0, M)),
            dx,
        )
        return dx, dw_gate, dw_up, dw_down

    tokens, columns, rows = P("dp", None), P(None, "tp"), P("tp", None)
    return jax.shard_map(
        step,
        mesh=mesh,
        in_specs=(tokens, tokens, P("dp", "tp"), P("dp", "tp"), columns, columns, rows),
        out_specs=(tokens, P("dp", "tp"), P("dp", "tp"), P(("dp", "tp"), None)),
        check_vma=False,
    )
```

time: 259 us -> 147 us (0.57)
  matrix products: 134 us -> 0 us
  Pallas kernels: 0 us -> 120 us
  waiting for transfers between devices: 83.1 us -> 16.4 us
  local copies, waits for them, and re-layouts: 27.8 us -> 4.49 us
  between operations: 14 us -> 0.89 us
  starting transfers between devices: 0.04 us -> 5.08 us
    dot_general x6 -> x0, matrix products: 134 us -> none  [the longest x1 25.9 us: step(): jnp.dot(d_up, w_up.T, preferred_element_type=jnp.float32)]
    pallas_call x0 -> x6, Pallas kernels: none -> 120 us  [the longest x1 65.1 us: scatter(): pl.pallas_call(scatter_kernel, out_shape=(jax.ShapeDtypeStruct((2 * M, HA...]
    psum x1 -> x0, waiting for transfers between devices: 83.1 us -> none  [step(): dx = lax.psum(term.astype(jnp.bfloat16), 'tp')]
    unnamed x3 -> x8, local copies, waits for them, and re-layouts: 27.8 us -> 4.38 us
    ppermute x0 -> x9, waiting for transfers between devices: none -> 16.4 us  [send(): return lax.ppermute(value, 'tp', perm)]
    ppermute x0 -> x9, starting transfers between devices: none -> 5.08 us  [send(): return lax.ppermute(value, 'tp', perm)]
  transfers between devices with their start and end apart: 1 -> 9, of which waited for: 1 -> 1; matrix products, arithmetic and copies ran while one was open for 31% -> 0% of each run, Pallas kernels for 0% -> 36%
where the time goes in v3:
time: 147 us
  Pallas kernels  120 us (82%)
  waiting for transfers between devices  16.4 us (11%)
  starting transfers between devices  5.08 us (3%)
  local copies, waits for them, and re-layouts  4.49 us (3%)
    pallas_call x1, Pallas kernels, scatter(): pl.pallas_call(scatter_kernel, out_shape=(jax.ShapeDtypeStruct((2 * M, HA...  65.1 us
    pallas_call x2, Pallas kernels, wide_grads(): pl.pallas_call(wide_kernel, grid=(count,), out_shape=(shape, shape), in_s...  32.4 us
    pallas_call x1, Pallas kernels, down_grad(): pl.pallas_call(down_kernel, grid=(D // bn,), out_shape=jax.ShapeDtypeStru...  17 us
    ppermute x9, waiting for transfers between devices, send(): return lax.ppermute(value, 'tp', perm)  16.4 us
    pallas_call x2, Pallas kernels, write(): pl.pallas_call(functools.partial(write_kernel, spots), out_shape=jax.Shap...  5.64 us
    ppermute x9, starting transfers between devices, send(): return lax.ppermute(value, 'tp', perm)  5.08 us
    unnamed x8, local copies, waits for them, and re-layouts  4.38 us
  transfers between devices with their start and end apart: 9, of which 1 were waited for; matrix products, arithmetic and copies ran while one was open for 0% of the time, Pallas kernels for 36%

profile of v3, /device:TPU:0, one launch (start us, length us, event | category | flops | bytes accessed | tf_op | source)
XLA Modules:
  0.0 146.9 jit_solution(11723185317463158711)
XLA Ops:
  0.6 65.1 %scatter.1 = (bf16[512,1536]{1,0:T(8,128)(2,1)}, bf16[2048,1024]{1,0:T(8,128)(2,1)}, bf16[2048,1024]{1,0:T(8,128)(2,1)}, bf16[2048,1024]{1,0:T(8,128)(2,1)}) custom-call(bf16[2048,3072]{1,0:T(8,128)(2,1)} %dy.3, bf16[2048,1024]{1,0:T(8,128)(2,1)} %gate.1, bf16[2048,1024]{1,0:T(8,128)(2,1)} %up.1, bf16[3072,1024]{1,0:T(8,128)(2,1)} %w_gate.1, ...), custom_call_target="tpu_custom_call" | custom-call | flops 38654705664 | bytes 62914560 | tf_op jit(solution)/shard_map/scatter/pallas_call | solution.py:253
  65.7 1.4 collective-permute-start
  67.1 0.6 collective-permute-start.7
  67.7 0.0 collective-permute-start.5
  67.7 0.0 copy-start.3
  67.8 2.2 %copy-done.3 = bf16[2048,1024]{1,0:T(8,128)(2,1)S(1)} copy-done((bf16[2048,1024]{1,0:T(8,128)(2,1)S(1)}, bf16[2048,1024]{1,0:T(8,128)(2,1)}, u32[]{:S(2)}) %copy-start.3) | copy-done | bytes 4194328
  69.9 0.0 copy-start.1
  69.9 17.0 %down_grad.1 = bf16[1024,3072]{1,0:T(8,128)(2,1)} custom-call(bf16[2048,1024]{1,0:T(8,128)(2,1)S(1)} %copy-done.3, bf16[2048,3072]{1,0:T(8,128)(2,1)} %dy.3), custom_call_target="tpu_custom_call" | custom-call | flops 12884901888 | bytes 25165824 | tf_op jit(solution)/shard_map/down_grad/pallas_call | solution.py:311
  86.9 16.3 %collective-permute-done.refs_2_ = bf16[512,1536]{1,0:T(8,128)(2,1)S(1)} collective-permute-done((bf16[512,1536]{1,0:T(8,128)(2,1)}, bf16[512,1536]{1,0:T(8,128)(2,1)S(1)}, u32[]{:S(2)}, u32[]{:S(2)}) %collective-permute-start) | collective-permute-done | bytes 1572896 | tf_op jit(solution)/shard_map/ppermute | solution.py:375
  103.2 0.1 fusion
  103.3 0.4 collective-permute-start.1
  103.7 1.7 %collective-permute-start.2 = (bf16[256,1536]{1,0:T(8,128)(2,1)S(1)}, bf16[256,1536]{1,0:T(8,128)(2,1)S(1)}, u32[]{:S(2)}, u32[]{:S(2)}) collective-permute-start(bf16[256,1536]{1,0:T(8,128)(2,1)S(1)} %get-tuple-element.20), channel_id=1, source_target_pairs={{0,4},{1,3},{2,6},{3,1},{4,0},{5,7},{6,2},{7,5}} | collective-permute-start | bytes 2359304 | tf_op jit(solution)/shard_map/ppermute | solution.py:375
  105.4 0.0 collective-permute-start.6
  105.4 0.0 collective-permute-done.7.refs_4_
  105.4 0.5 collective-permute-start.8
  105.9 0.0 copy-done.1
  105.9 0.0 copy-start.2
  105.9 2.2 %copy-done.2 = bf16[2048,1024]{1,0:T(8,128)(2,1)S(1)} copy-done((bf16[2048,1024]{1,0:T(8,128)(2,1)S(1)}, bf16[2048,1024]{1,0:T(8,128)(2,1)}, u32[]{:S(2)}) %copy-start.2) | copy-done | bytes 4194328
  108.1 16.1 %wide_grads.2 = (bf16[3072,1024]{1,0:T(8,128)(2,1)}, bf16[3072,1024]{1,0:T(8,128)(2,1)}) custom-call(bf16[2048,3072]{1,0:T(8,128)(2,1)} %x.3, bf16[2048,1024]{1,0:T(8,128)(2,1)S(1)} %copy-done.1, bf16[2048,1024]{1,0:T(8,128)(2,1)S(1)} %copy-done.2), custom_call_target="tpu_custom_call" | custom-call | flops 12884901888 | bytes 20971520 | tf_op jit(solution)/shard_map/wide_grads/pallas_call | solution.py:292
  124.2 0.0 collective-permute-done.1.refs_0_
  124.2 0.0 collective-permute-start.3
  124.2 0.0 collective-permute-done.2.refs_1_
  124.2 0.5 collective-permute-start.4
  124.7 0.0 copy-start
  124.7 16.3 %wide_grads.3 = (bf16[3072,1024]{1,0:T(8,128)(2,1)}, bf16[3072,1024]{1,0:T(8,128)(2,1)}) custom-call(bf16[2048,3072]{1,0:T(8,128)(2,1)} %x.3, bf16[2048,1024]{1,0:T(8,128)(2,1)S(1)} %copy-done.1, bf16[2048,1024]{1,0:T(8,128)(2,1)S(1)} %copy-done.2, bf16[3072,1024]{1,0:T(8,128)(2,1)} %get-tuple-element.15.refs_0_, ...), custom_call_target="tpu_custom_call", output_to_operand_aliasing={{0}: (3, {}), {1}: (4, {})} | custom-call | flops 12884901888 | bytes 20971520 | tf_op jit(solution)/shard_map/wide_grads/pallas_call | solution.py:292
  141.0 0.0 collective-permute-done.5.refs_1_
  141.0 0.0 collective-permute-done.6.refs_3_
  141.0 0.0 collective-permute-done.8.refs_5_
  141.0 0.0 copy-done
  141.0 3.8 %write.2.refs_4_ = bf16[2048,3072]{1,0:T(8,128)(2,1)} custom-call(bf16[512,1536]{1,0:T(8,128)(2,1)S(1)} %copy-done, bf16[512,1536]{1,0:T(8,128)(2,1)S(1)} %collective-permute-done.5.refs_1_, bf16[512,1536]{1,0:T(8,128)(2,1)S(1)} %collective-permute-done.refs_2_, bf16[512,1536]{1,0:T(8,128)(2,1)S(1)} %collective-permute-done.6.refs_3_, ...), custom_call_target="tpu_custom_call" | custom-call | flops 1000000000 | bytes 25165824 | tf_op jit(solution)/shard_map/write/pallas_call | solution.py:347
  144.9 0.0 collective-permute-done.3.refs_2_
  144.9 0.0 collective-permute-done.4.refs_3_
  144.9 1.8 %write.3 = bf16[2048,3072]{1,0:T(8,128)(2,1)} custom-call(bf16[256,1536]{1,0:T(8,128)(2,1)S(1)} %collective-permute-done.1.refs_0_, bf16[256,1536]{1,0:T(8,128)(2,1)S(1)} %collective-permute-done.2.refs_1_, bf16[256,1536]{1,0:T(8,128)(2,1)S(1)} %collective-permute-done.3.refs_2_, ...), custom_call_target="tpu_custom_call", output_to_operand_aliasing={{}: (4, {})} | custom-call | flops 1000000000 | bytes 25165824 | tf_op jit(solution)/shard_map/write/pallas_call | solution.py:347
Async XLA Ops:
  65.7 37.5 %collective-permute-start = (bf16[512,1536]{1,0:T(8,128)(2,1)}, bf16[512,1536]{1,0:T(8,128)(2,1)S(1)}, u32[]{:S(2)}, u32[]{:S(2)}) collective-permute-start(bf16[512,1536]{1,0:T(8,128)(2,1)} %get-tuple-element.12.refs_0_), channel_id=1, source_target_pairs={{0,2},{1,5},{2,0},{3,7},{4,6},{5,1},{6,4},{7,3}} | collective-permute-start | bytes 4718600 | tf_op jit(solution)/shard_map/ppermute | solution.py:375
  67.1 38.2 %collective-permute-start.7 = (bf16[512,1536]{1,0:T(8,128)(2,1)}, bf16[512,1536]{1,0:T(8,128)(2,1)S(1)}, u32[]{:S(2)}, u32[]{:S(2)}) collective-permute-start(bf16[512,1536]{1,0:T(8,128)(2,1)} %get-tuple-element.12.refs_0_), channel_id=1, source_target_pairs={{0,4},{1,3},{2,6},{3,1},{4,0},{5,7},{6,2},{7,5}} | collective-permute-start | bytes 4718600 | tf_op jit(solution)/shard_map/ppermute | solution.py:375
  67.7 73.3 %collective-permute-start.5 = (bf16[512,1536]{1,0:T(8,128)(2,1)}, bf16[512,1536]{1,0:T(8,128)(2,1)S(1)}, u32[]{:S(2)}, u32[]{:S(2)}) collective-permute-start(bf16[512,1536]{1,0:T(8,128)(2,1)} %get-tuple-element.12.refs_0_), channel_id=1, source_target_pairs={{0,1},{1,0},{2,3},{3,2},{4,5},{5,4},{6,7},{7,6}} | collective-permute-start | bytes 4718600 | tf_op jit(solution)/shard_map/ppermute | solution.py:375
  67.7 2.2 %copy-start.3 = (bf16[2048,1024]{1,0:T(8,128)(2,1)S(1)}, bf16[2048,1024]{1,0:T(8,128)(2,1)}, u32[]{:S(2)}) copy-start(bf16[2048,1024]{1,0:T(8,128)(2,1)} %get-tuple-element.19.hidden) | copy-start | bytes 12582916
  69.9 36.0 %copy-start.1 = (bf16[2048,1024]{1,0:T(8,128)(2,1)S(1)}, bf16[2048,1024]{1,0:T(8,128)(2,1)}, u32[]{:S(2)}) copy-start(bf16[2048,1024]{1,0:T(8,128)(2,1)} %get-tuple-element.13.d_gate) | copy-start | bytes 12582916
  103.3 20.9 %collective-permute-start.1 = (bf16[256,1536]{1,0:T(8,128)(2,1)S(1)}, bf16[256,1536]{1,0:T(8,128)(2,1)S(1)}, u32[]{:S(2)}, u32[]{:S(2)}) collective-permute-start(bf16[256,1536]{1,0:T(8,128)(2,1)S(1)} %get-tuple-element.21), channel_id=1, source_target_pairs={{0,4},{1,3},{2,6},{3,1},{4,0},{5,7},{6,2},{7,5}} | collective-permute-start | bytes 2359304 | tf_op jit(solution)/shard_map/ppermute | solution.py:375
  103.7 20.5 %collective-permute-start.2 = (bf16[256,1536]{1,0:T(8,128)(2,1)S(1)}, bf16[256,1536]{1,0:T(8,128)(2,1)S(1)}, u32[]{:S(2)}, u32[]{:S(2)}) collective-permute-start(bf16[256,1536]{1,0:T(8,128)(2,1)S(1)} %get-tuple-element.20), channel_id=1, source_target_pairs={{0,4},{1,3},{2,6},{3,1},{4,0},{5,7},{6,2},{7,5}} | collective-permute-start | bytes 2359304 | tf_op jit(solution)/shard_map/ppermute | solution.py:375
  105.4 35.6 %collective-permute-start.6 = (bf16[512,1536]{1,0:T(8,128)(2,1)S(1)}, bf16[512,1536]{1,0:T(8,128)(2,1)S(1)}, u32[]{:S(2)}, u32[]{:S(2)}) collective-permute-start(bf16[512,1536]{1,0:T(8,128)(2,1)S(1)} %collective-permute-done.refs_2_), channel_id=1, source_target_pairs={{0,1},{1,0},{2,3},{3,2},{4,5},{5,4},{6,7},{7,6}} | collective-permute-start | bytes 4718600 | tf_op jit(solution)/shard_map/ppermute | solution.py:375
  105.4 35.6 %collective-permute-start.8 = (bf16[512,1536]{1,0:T(8,128)(2,1)S(1)}, bf16[512,1536]{1,0:T(8,128)(2,1)S(1)}, u32[]{:S(2)}, u32[]{:S(2)}) collective-permute-start(bf16[512,1536]{1,0:T(8,128)(2,1)S(1)} %collective-permute-done.7.refs_4_), channel_id=1, source_target_pairs={{0,1},{1,0},{2,3},{3,2},{4,5},{5,4},{6,7},{7,6}} | collective-permute-start | bytes 4718600 | tf_op jit(solution)/shard_map/ppermute | solution.py:375
  105.9 2.2 %copy-start.2 = (bf16[2048,1024]{1,0:T(8,128)(2,1)S(1)}, bf16[2048,1024]{1,0:T(8,128)(2,1)}, u32[]{:S(2)}) copy-start(bf16[2048,1024]{1,0:T(8,128)(2,1)} %get-tuple-element.14.d_up) | copy-start | bytes 12582916
  124.2 20.6 %collective-permute-start.3 = (bf16[256,1536]{1,0:T(8,128)(2,1)S(1)}, bf16[256,1536]{1,0:T(8,128)(2,1)S(1)}, u32[]{:S(2)}, u32[]{:S(2)}) collective-permute-start(bf16[256,1536]{1,0:T(8,128)(2,1)S(1)} %collective-permute-done.1.refs_0_), channel_id=1, source_target_pairs={{0,1},{1,0},{2,3},{3,2},{4,5},{5,4},{6,7},{7,6}} | collective-permute-start | bytes 2359304 | tf_op jit(solution)/shard_map/ppermute | solution.py:375
  124.2 20.6 %collective-permute-start.4 = (bf16[256,1536]{1,0:T(8,128)(2,1)S(1)}, bf16[256,1536]{1,0:T(8,128)(2,1)S(1)}, u32[]{:S(2)}, u32[]{:S(2)}) collective-permute-start(bf16[256,1536]{1,0:T(8,128)(2,1)S(1)} %collective-permute-done.2.refs_1_), channel_id=1, source_target_pairs={{0,1},{1,0},{2,3},{3,2},{4,5},{5,4},{6,7},{7,6}} | collective-permute-start | bytes 2359304 | tf_op jit(solution)/shard_map/ppermute | solution.py:375
  124.7 16.3 %copy-start = (bf16[512,1536]{1,0:T(8,128)(2,1)S(1)}, bf16[512,1536]{1,0:T(8,128)(2,1)}, u32[]{:S(2)}) copy-start(bf16[512,1536]{1,0:T(8,128)(2,1)} %get-tuple-element.12.refs_0_) | copy-start | bytes 4718596

commit v4 on v3

v4 whole, which is shorter than its diff:
```python
import functools

import jax
import jax.numpy as jnp
from jax import lax
from jax.experimental import pallas as pl
from jax.experimental.pallas import tpu as pltpu
from jax.sharding import PartitionSpec as P


SCATTER_MIB, WIDE_MIB, DOWN_MIB = 47, 26, 26

BF16, F32 = jnp.bfloat16, jnp.float32
ROWS, D, FL = 2048, 3072, 1024
M = 256
U = M // 2
HALF = D // 2
W = 512
PIECES = HALF // W
BN = 512
PARTS = D // BN
STEPS = ROWS // M
ANY = pl.BlockSpec(memory_space=pl.ANY)


def nt(a, b):
    return lax.dot_general(a, b, (((1,), (1,)), ((), ())), preferred_element_type=F32)


def turned(a, b):
    return lax.dot_general(a, b, (((0,), (0,)), ((), ())), preferred_element_type=F32)


def places(parts, spots, out, sem):
    _, core, y, x = place()
    copies = []
    for k, (part, (twin, along_first, along_second, row, count)) in enumerate(zip(parts, spots)):
        half = core + twin - 2 * core * twin
        flip_y = along_first * (1 - half) + along_second * half
        flip_x = along_first * half + along_second * (1 - half)
        to_x, to_y = x + flip_x - 2 * x * flip_x, y + flip_y - 2 * y * flip_y
        cols = pl.ds(pl.multiple_of(half * HALF, HALF), HALF)
        for i in range(0, count, U):
            rows = pl.ds(pl.multiple_of((to_x * 2 + to_y) * 2 * M + row + i, U), U)
            copies.append(pltpu.make_async_copy(part.at[pl.ds(i, U)], out.at[rows, cols], sem.at[k, i // U]))
    return copies


def place():
    me = lax.axis_index("tp")
    core, y, x = me % 2, (me // 2) % 2, me // 4
    return me, core, y, x


def rows_of(p, x, y):
    diag, own = 1 - jnp.minimum(p // 2, 1), p // 6
    mid = 1 - diag - own
    at = diag * p * M + own * (p - 6) * M + mid * (p - 2) * U

    def run(flip_x, flip_y):
        to_x, to_y = x + flip_x - 2 * x * flip_x, y + flip_y - 2 * y * flip_y
        return (to_x * 2 + to_y) * 2 * M + at

    return run(diag, diag + mid), run(diag + mid, diag) + (1 - mid) * U


def scatter_kernel(
    dy, gate, up, w_gate, w_up, w_down,
    shard, d_gate, d_up, hidden, block,
    wg, wu, wd, dyb, gb, ub, dgb, dub, acc, sum_own,
    sib_out, sib_in, one_out, one_in, two_out, two_in,
    down_sem, wide_sem, in_sem,
    sib_s, sib_r, one_s, one_r, two_s, two_r,
):
    me, core, y, x = place()
    sibling = me + 1 - 2 * core
    near_x, near_y = me + 4 - 8 * x, me + 2 - 4 * y
    first = near_y * (1 - core) + near_x * core
    second = near_x * (1 - core) + near_y * core
    own_col, sib_col = core * HALF, (1 - core) * HALF

    def inputs(p, slot):
        made = []
        for h, row in enumerate(rows_of(p, x, y)):
            rows = pl.ds(pl.multiple_of(row, U), U)
            for k, (near, far) in enumerate(((dyb, dy), (gb, gate), (ub, up))):
                made.append(pltpu.make_async_copy(far.at[rows], near.at[slot, pl.ds(h * U, U)], in_sem.at[slot, h, k]))
        return made

    def columns(base, j):
        return pl.ds(pl.multiple_of(base + j * W, 256), W)

    down = []
    for n in range(FL // 256):
        at = pl.ds(n * 256, 256)
        down.append(pltpu.make_async_copy(w_down.at[at], wd.at[at], down_sem.at[n]))
    wide = {}
    for j in range(PIECES):
        for side, base in ((0, sib_col), (1, own_col)):
            at = columns(base, j)
            wide[side, j] = (
                pltpu.make_async_copy(w_gate.at[at], wg.at[at], wide_sem.at[side, j, 0]),
                pltpu.make_async_copy(w_up.at[at], wu.at[at], wide_sem.at[side, j, 1]),
            )

    def remote(src, dst, send, recv, to):
        return pltpu.make_async_remote_copy(
            src_ref=src, dst_ref=dst, send_sem=send, recv_sem=recv,
            device_id={"tp": to}, device_id_type=pl.DeviceIdType.MESH,
        )

    def to_sibling(p, j):
        return remote(sib_out.at[p % 2, j], sib_in.at[p % 2, j], sib_s.at[p % 2, j], sib_r.at[p % 2, j], sibling)

    def to_first(k, j):
        return remote(one_out.at[k, j], one_in.at[k, j], one_s, one_r.at[k, j], first)

    def to_second(k, j):
        return remote(two_out.at[k, j], two_in.at[k, j], two_s, two_r.at[k, j], second)

    for c in inputs(0, 0):
        c.start()
    for c in down:
        c.start()

    barrier = pltpu.get_barrier_semaphore()
    for other in (sibling, first, second):
        pl.semaphore_signal(barrier, inc=1, device_id={"tp": other}, device_id_type=pl.DeviceIdType.MESH)
    pl.semaphore_wait(barrier, 3)

    def keep(to, p, at, value):
        value = value.astype(BF16)
        for h, row in enumerate(rows_of(p, x, y)):
            to[pl.ds(pl.multiple_of(row, U), U), at] = value[h * U : (h + 1) * U]
        return value

    def hidden_grads(p, slot, n):
        at = slice(n * 256, (n + 1) * 256)
        d_hidden = nt(dyb[slot], wd[at, :])
        g, u = gb[slot, :, at].astype(F32), ub[slot, :, at].astype(F32)
        s = jax.nn.sigmoid(g)
        act = g * s
        keep(hidden, p, at, act * u)
        dub[:, at] = keep(d_up, p, at, d_hidden * act)
        dgb[:, at] = keep(d_gate, p, at, d_hidden * u * (s + act * (1 - s)))

    def term(base, j):
        at = columns(base, j)
        return (nt(dgb[...], wg[at, :]) + nt(dub[...], wu[at, :])).reshape(2, U, W)

    def for_sibling(p, j, reused):
        if reused:
            to_sibling(p, j).wait_send()
        sib_out[p % 2, j] = term(sib_col, j).astype(BF16)
        to_sibling(p, j).start()

    def chip_sum(p, j, h):
        return acc[j, h] + sib_in[p % 2, j, h].astype(F32)

    def send_diagonal(p, j):
        for h in range(2):
            one_out[2 * p + h, j] = chip_sum(p, j, h).astype(BF16)
            to_first(2 * p + h, j).start()

    def send_middle(p):
        q = p - 2
        for j in range(PIECES):
            to_sibling(p, j).wait_recv()
            one_out[4 + q, j] = chip_sum(p, j, core).astype(BF16)
            to_first(4 + q, j).start()
        for j in range(PIECES):
            to_first(q, j).wait_recv()
            two_out[q, j] = (chip_sum(p, j, 1 - core) + one_in[q, j].astype(F32)).astype(BF16)
            to_second(q, j).start()

    def keep_own(p):
        for j in range(PIECES):
            to_sibling(p, j).wait_recv()
            for h in range(2):
                sum_own[2 * (p - 6) + h, j] = chip_sum(p, j, h)

    def diagonal_step(p, ready):
        for n in range(FL // 256):
            hidden_grads(p, p, n)
        for j in range(PIECES + 1):
            if j < PIECES:
                ready(0, j)
                for_sibling(p, j, False)
            if j:
                ready(1, j - 1)
                acc[j - 1] = term(own_col, j - 1)
                to_sibling(p, j - 1).wait_recv()
                send_diagonal(p, j - 1)

    def arrived(side, j):
        for c in wide[side, j]:
            c.wait()

    down_inputs = []
    for k in range(ROWS // M):
        near = dyb.at[k // PARTS, :, pl.ds(k % PARTS * BN, BN)]
        down_inputs.append(
            pltpu.make_async_copy(dy.at[pl.ds(k * M, M), pl.ds(0, BN)], near, in_sem.at[k // 6, k % 6 // 3, k % 3])
        )

    for c in inputs(0, 0):
        c.wait()
    for j in range(PIECES):
        for side in range(2):
            for c in wide[side, j]:
                c.start()
    for c in inputs(1, 1):
        c.start()
    for c in down:
        c.wait()
    diagonal_step(0, arrived)
    for c in inputs(1, 1):
        c.wait()
    for c in inputs(2, 0):
        c.start()
    diagonal_step(1, lambda side, j: None)

    def step(p, carry):
        slot = p % 2
        for c in inputs(p, slot):
            c.wait()

        @pl.when(p < STEPS - 1)
        def _():
            for c in inputs(p + 1, 1 - slot):
                c.start()

        for n in range(FL // 256):
            hidden_grads(p, slot, n)

        @pl.when(jnp.logical_and(p >= 4, p < 7))
        def _():
            send_middle(p - 1)

        @pl.when(p == 7)
        def _():
            for c in down_inputs:
                c.start()
            keep_own(6)

        for j in range(PIECES):
            for_sibling(p, j, True)
        for j in range(PIECES):
            acc[j] = term(own_col, j)

        @pl.when(p == 2)
        def _():
            send_middle(2)

        return carry

    lax.fori_loop(2, STEPS, step, 0)
    keep_own(STEPS - 1)

    for c in down_inputs:
        c.wait()
    for n in range(0, BN, 256):
        right = jnp.concatenate([dyb[k // PARTS, :, pl.ds(k % PARTS * BN + n, 256)] for k in range(ROWS // M)])
        block[:, pl.ds(n, 256)] = turned(hidden[...], right).astype(BF16)

    for q in range(4):
        for j in range(PIECES):
            to_first(4 + q, j).wait_recv()
            to_second(q, j).wait_recv()
            total = sum_own[q, j] + one_in[4 + q, j].astype(F32) + two_in[q, j].astype(F32)
            shard[pl.ds(q * U, U), pl.ds(j * W, W)] = total.astype(BF16)
    for p in (STEPS - 2, STEPS - 1):
        for j in range(PIECES):
            to_sibling(p, j).wait_send()
    remote(one_out, one_in, one_s, one_r.at[0, 0], first).wait_send()
    remote(two_out, two_in, two_s, two_r.at[0, 0], second).wait_send()


def scatter(dy, gate, up, w_gate, w_up, w_down):
    dma = pltpu.SemaphoreType.DMA
    hid = pltpu.VMEM((ROWS, FL), BF16)
    units = lambda n: pltpu.VMEM((n, PIECES, U, W), BF16)
    twin = pltpu.VMEM((2, PIECES, 2, U, W), BF16)
    return pl.pallas_call(
        scatter_kernel,
        out_shape=(pltpu.VMEM((2 * M, HALF), BF16), hid, hid, hid, pltpu.VMEM((FL, BN), BF16)),
        in_specs=[ANY] * 6,
        out_specs=(pl.BlockSpec(memory_space=pltpu.VMEM),) * 5,
        scratch_shapes=[
            pltpu.VMEM((D, FL), BF16), pltpu.VMEM((D, FL), BF16), pltpu.VMEM((FL, D), BF16),
            pltpu.VMEM((2, M, D), BF16), pltpu.VMEM((2, M, FL), BF16), pltpu.VMEM((2, M, FL), BF16),
            pltpu.VMEM((M, FL), BF16), pltpu.VMEM((M, FL), BF16),
            pltpu.VMEM((PIECES, 2, U, W), F32), pltpu.VMEM((4, PIECES, U, W), F32),
            twin, twin, units(8), units(8), units(4), units(4),
            dma((FL // 256,)), dma((2, PIECES, 2)), dma((2, 2, 3)),
            dma((2, PIECES)), dma((2, PIECES)), dma, dma((8, PIECES)), dma, dma((4, PIECES)),
        ],
        compiler_params=pltpu.CompilerParams(
            collective_id=0, has_side_effects=True, vmem_limit_bytes=SCATTER_MIB * 2**20
        ),
        cost_estimate=pl.CostEstimate(
            flops=6 * ROWS * D * FL, bytes_accessed=60 * 2**20, transcendentals=2 * ROWS * FL
        ),
        name="scatter",
    )(dy, gate, up, w_gate, w_up, w_down)


def placed(value, space):
    return pltpu.with_memory_space_constraint(value, space)


def wide_kernel(x, d_gate, d_up, *refs):
    dw_gate, dw_up = refs[-2:]
    xt = x[...].T
    dw_gate[...] = jnp.dot(xt, d_gate[...], preferred_element_type=F32).astype(BF16)
    dw_up[...] = jnp.dot(xt, d_up[...], preferred_element_type=F32).astype(BF16)


def wide_grads(x, d_gate, d_up, start, count, into=(), bm=512):
    whole = pl.BlockSpec((ROWS, FL), lambda i: (0, 0), pipeline_mode=pl.Buffered(1))
    out = pl.BlockSpec((bm, FL), lambda i: (start + i, 0))
    shape = jax.ShapeDtypeStruct((D, FL), BF16)
    return pl.pallas_call(
        wide_kernel,
        grid=(count,),
        out_shape=(shape, shape),
        in_specs=[pl.BlockSpec((ROWS, bm), lambda i: (0, start + i)), whole, whole] + [ANY] * len(into),
        out_specs=(out, out),
        input_output_aliases={3 + k: k for k in range(len(into))},
        compiler_params=pltpu.CompilerParams(vmem_limit_bytes=WIDE_MIB * 2**20),
        cost_estimate=pl.CostEstimate(flops=4 * ROWS * bm * count * FL, bytes_accessed=20 * 2**20, transcendentals=0),
        name="wide_grads",
    )(placed(x, pltpu.HBM), placed(d_gate, pltpu.VMEM), placed(d_up, pltpu.VMEM), *into)


def down_kernel(spots, hidden, dy, block, *refs):
    n = len(spots)
    parts, out, dx, sem = refs[:n], refs[n], refs[n + 1], refs[n + 2]
    step, last = pl.program_id(0), pl.num_programs(0) - 1

    @pl.when(step == 0)
    def _():
        for c in places(parts, spots, dx, sem):
            c.start()

    @pl.when(step < last)
    def _():
        out[...] = turned(hidden[...], dy[...]).astype(BF16)

    @pl.when(step == last)
    def _():
        out[...] = block[...]
        for c in places(parts, spots, dx, sem):
            c.wait()


def down_grad(hidden, dy, block, parts, spots):
    n = len(parts)
    whole = lambda *shape: pl.BlockSpec(shape, lambda i: (0, 0), pipeline_mode=pl.Buffered(1))
    return pl.pallas_call(
        functools.partial(down_kernel, spots),
        grid=(PARTS,),
        out_shape=(jax.ShapeDtypeStruct((FL, D), BF16), jax.ShapeDtypeStruct((ROWS, D), BF16)),
        in_specs=[
            whole(ROWS, FL), pl.BlockSpec((ROWS, BN), lambda i: (0, jnp.minimum(i + 1, PARTS - 1))), whole(FL, BN),
        ]
        + [ANY] * n,
        out_specs=(pl.BlockSpec((FL, BN), lambda i: (0, (i + 1) % PARTS)), ANY),
        scratch_shapes=[pltpu.SemaphoreType.DMA((n, 2 * M // U))],
        compiler_params=pltpu.CompilerParams(vmem_limit_bytes=DOWN_MIB * 2**20),
        cost_estimate=pl.CostEstimate(flops=2 * ROWS * D * FL, bytes_accessed=24 * 2**20, transcendentals=0),
        name="down_grad",
    )(placed(hidden, pltpu.VMEM), placed(dy, pltpu.HBM), placed(block, pltpu.VMEM), *parts)


def write_kernel(spots, *refs):
    copies = places(refs[: len(spots)], spots, refs[-2], refs[-1])
    for c in copies:
        c.start()
    for c in copies:
        c.wait()


def write(parts, spots, into=None):
    n = len(parts)
    given = () if into is None else (into,)
    return pl.pallas_call(
        functools.partial(write_kernel, spots),
        out_shape=jax.ShapeDtypeStruct((ROWS, D), BF16),
        in_specs=[pl.BlockSpec(memory_space=pltpu.VMEM)] * n + [ANY] * len(given),
        out_specs=ANY,
        scratch_shapes=[pltpu.SemaphoreType.DMA((n, 2 * M // U))],
        input_output_aliases={n: 0} if given else {},
        compiler_params=pltpu.CompilerParams(vmem_limit_bytes=16 * 1024 * 1024),
        cost_estimate=pl.CostEstimate(flops=10**9, bytes_accessed=24 * 2**20, transcendentals=0),
        name="write",
    )(*parts, *given)


def index(x, y, core):
    return (x * 2 + y) * 2 + core


def pairs(to):
    return [(index(x, y, c), index(*to(x, y, c))) for x in (0, 1) for y in (0, 1) for c in (0, 1)]


FIRST = pairs(lambda x, y, c: (x, 1 - y, c) if c == 0 else (1 - x, y, c))
SECOND = pairs(lambda x, y, c: (1 - x, y, c) if c == 0 else (x, 1 - y, c))
SIBLING = pairs(lambda x, y, c: (x, y, 1 - c))


def solution(mesh):
    def send(value, perm):
        return lax.ppermute(value, "tp", perm)

    def step(x, dy, gate, up, w_gate, w_up, w_down):
        shard, d_gate, d_up, hidden, block = scatter(dy, gate, up, w_gate, w_up, w_down)
        first_a, first_b = send(shard[:M], FIRST), send(shard[M:], FIRST)
        second = send(shard, SECOND)
        own_twin = send(shard, SIBLING)
        both_a, both_b = send(first_a, SECOND), send(first_b, SECOND)
        first_a_twin, first_b_twin = send(first_a, SIBLING), send(first_b, SIBLING)
        second_twin = send(second, SIBLING)
        both_a_twin, both_b_twin = send(both_a, SIBLING), send(both_b, SIBLING)
        wide = wide_grads(x, d_gate, d_up, 0, 3)
        dw_gate, dw_up = wide_grads(x, d_gate, d_up, 3, 3, wide)
        dw_down, dx = down_grad(
            hidden, dy, block, (shard, own_twin, first_a, first_a_twin, first_b, second),
            ((0, 0, 0, 0, 2 * M), (1, 0, 0, 0, 2 * M), (0, 1, 0, 0, M), (1, 1, 0, 0, M), (0, 1, 0, M, M), (0, 0, 1, 0, 2 * M)),
        )
        dx = write(
            (first_b_twin, second_twin, both_a, both_b),
            ((1, 1, 0, M, M), (1, 0, 1, 0, 2 * M), (0, 1, 1, 0, M), (0, 1, 1, M, M)),
            dx,
        )
        dx = write((both_a_twin, both_b_twin), ((1, 1, 1, 0, M), (1, 1, 1, M, M)), dx)
        return dx, dw_gate, dw_up, dw_down

    tokens, columns, rows = P("dp", None), P(None, "tp"), P("tp", None)
    return jax.shard_map(
        step,
        mesh=mesh,
        in_specs=(tokens, tokens, P("dp", "tp"), P("dp", "tp"), columns, columns, rows),
        out_specs=(tokens, P("dp", "tp"), P("dp", "tp"), P(("dp", "tp"), None)),
        check_vma=False,
    )
```

time: 147 us -> 142 us (0.966)
  Pallas kernels: 120 us -> 115 us
  local copies, waits for them, and re-layouts: 4.49 us -> 0.1 us
  waiting for transfers between devices: 16.4 us -> 19 us
  starting transfers between devices: 5.08 us -> 6.68 us
    unnamed x8 -> x0, local copies, waits for them, and re-layouts: 4.38 us -> none
    ppermute x9 -> x11, waiting for transfers between devices: 16.4 us -> 19 us  [send(): return lax.ppermute(value, 'tp', perm)]
    pallas_call x2, Pallas kernels: 82 us -> 79.5 us  [the longest x1 64.2 us: scatter(): pl.pallas_call(scatter_kernel, out_shape=(pltpu.VMEM((2 * M, HALF), BF16)...]
    pallas_call x2, Pallas kernels: 5.64 us -> 3.31 us  [write(): pl.pallas_call(functools.partial(write_kernel, spots), out_shape=jax.Shap...]
    ppermute x9 -> x11, starting transfers between devices: 5.08 us -> 6.68 us  [send(): return lax.ppermute(value, 'tp', perm)]
  transfers between devices with their start and end apart: 9 -> 11, of which waited for: 1 -> 2; matrix products, arithmetic and copies ran while one was open for 0% -> 0% of each run, Pallas kernels for 36% -> 35%
where the time goes in v4:
time: 142 us
  Pallas kernels  115 us (81%)
  waiting for transfers between devices  19 us (13%)
  starting transfers between devices  6.68 us (5%)
    pallas_call x1, Pallas kernels, scatter(): pl.pallas_call(scatter_kernel, out_shape=(pltpu.VMEM((2 * M, HALF), BF16)...  64.2 us
    pallas_call x2, Pallas kernels, wide_grads(): pl.pallas_call(wide_kernel, grid=(count,), out_shape=(shape, shape), in_s...  32.5 us
    ppermute x11, waiting for transfers between devices, send(): return lax.ppermute(value, 'tp', perm)  19 us
    pallas_call x1, Pallas kernels, down_grad(): pl.pallas_call(functools.partial(down_kernel, spots), grid=(PARTS,), out_...  15.2 us
    ppermute x11, starting transfers between devices, send(): return lax.ppermute(value, 'tp', perm)  6.68 us
    pallas_call x2, Pallas kernels, write(): pl.pallas_call(functools.partial(write_kernel, spots), out_shape=jax.Shap...  3.31 us
  transfers between devices with their start and end apart: 11, of which 2 were waited for; matrix products, arithmetic and copies ran while one was open for 0% of the time, Pallas kernels for 35%

profile of v4, /device:TPU:0, one launch (start us, length us, event | category | flops | bytes accessed | tf_op | source)
XLA Modules:
  0.0 142.0 jit_solution(5075017173968255757)
XLA Ops:
  0.6 64.2 %scatter.1 = (bf16[512,1536]{1,0:T(8,128)(2,1)S(1)}, bf16[2048,1024]{1,0:T(8,128)(2,1)S(1)}, bf16[2048,1024]{1,0:T(8,128)(2,1)S(1)}, bf16[2048,1024]{1,0:T(8,128)(2,1)S(1)}, bf16[1024,512]{1,0:T(8,128)(2,1)S(1)}) custom-call(bf16[2048,3072]{1,0:T(8,128)(2,1)} %dy.3, bf16[2048,1024]{1,0:T(8,128)(2,1)} %gate.1, bf16[2048,1024]{1,0:T(8,128)(2,1)} %up.1, ...), custom_call_target="tpu_custom_call" | custom-call | flops 38654705664 | bytes 62914560 | tf_op jit(solution)/shard_map/scatter/pallas_call | solution.py:284
  64.9 0.0 collective-permute-start.9
  64.9 1.5 %collective-permute-start.7 = (bf16[512,1536]{1,0:T(8,128)(2,1)S(1)}, bf16[512,1536]{1,0:T(8,128)(2,1)S(1)}, u32[]{:S(2)}, u32[]{:S(2)}) collective-permute-start(bf16[512,1536]{1,0:T(8,128)(2,1)S(1)} %get-tuple-element.15.refs_0_), channel_id=1, source_target_pairs={{0,4},{1,3},{2,6},{3,1},{4,0},{5,7},{6,2},{7,5}} | collective-permute-start | bytes 4718600 | tf_op jit(solution)/shard_map/ppermute | solution.py:415
  66.4 0.1 fusion
  66.5 0.5 collective-permute-start.3
  67.1 1.5 %collective-permute-start = (bf16[256,1536]{1,0:T(8,128)(2,1)S(1)}, bf16[256,1536]{1,0:T(8,128)(2,1)S(1)}, u32[]{:S(2)}, u32[]{:S(2)}) collective-permute-start(bf16[256,1536]{1,0:T(8,128)(2,1)S(1)} %get-tuple-element.27), channel_id=1, source_target_pairs={{0,2},{1,5},{2,0},{3,7},{4,6},{5,1},{6,4},{7,3}} | collective-permute-start | bytes 2359304 | tf_op jit(solution)/shard_map/ppermute | solution.py:415
  68.6 16.1 %wide_grads.2 = (bf16[3072,1024]{1,0:T(8,128)(2,1)}, bf16[3072,1024]{1,0:T(8,128)(2,1)}) custom-call(bf16[2048,3072]{1,0:T(8,128)(2,1)} %x.3, bf16[2048,1024]{1,0:T(8,128)(2,1)S(1)} %get-tuple-element.19.d_gate, bf16[2048,1024]{1,0:T(8,128)(2,1)S(1)} %get-tuple-element.20.d_up), custom_call_target="tpu_custom_call" | custom-call | flops 12884901888 | bytes 20971520 | tf_op jit(solution)/shard_map/wide_grads/pallas_call | solution.py:323
  84.7 17.0 %collective-permute-done.refs_2_ = bf16[256,1536]{1,0:T(8,128)(2,1)S(1)} collective-permute-done((bf16[256,1536]{1,0:T(8,128)(2,1)S(1)}, bf16[256,1536]{1,0:T(8,128)(2,1)S(1)}, u32[]{:S(2)}, u32[]{:S(2)}) %collective-permute-start) | collective-permute-done | bytes 786464 | tf_op jit(solution)/shard_map/ppermute | solution.py:415
  101.7 0.5 collective-permute-start.10
  102.3 1.3 collective-permute-start.1
  103.5 0.0 collective-permute-done.3.refs_4_
  103.5 0.7 collective-permute-start.4
  104.3 0.0 collective-permute-done.7.refs_5_
  104.3 0.0 collective-permute-start.8
  104.3 16.4 %wide_grads.3 = (bf16[3072,1024]{1,0:T(8,128)(2,1)}, bf16[3072,1024]{1,0:T(8,128)(2,1)}) custom-call(bf16[2048,3072]{1,0:T(8,128)(2,1)} %x.3, bf16[2048,1024]{1,0:T(8,128)(2,1)S(1)} %get-tuple-element.19.d_gate, bf16[2048,1024]{1,0:T(8,128)(2,1)S(1)} %get-tuple-element.20.d_up, ...), custom_call_target="tpu_custom_call", output_to_operand_aliasing={{0}: (3, {}), {1}: (4, {})} | custom-call | flops 12884901888 | bytes 20971520 | tf_op jit(solution)/shard_map/wide_grads/pallas_call | solution.py:323
  120.7 2.0 %collective-permute-done.4.refs_3_ = bf16[256,1536]{1,0:T(8,128)(2,1)S(1)} collective-permute-done((bf16[256,1536]{1,0:T(8,128)(2,1)S(1)}, bf16[256,1536]{1,0:T(8,128)(2,1)S(1)}, u32[]{:S(2)}, u32[]{:S(2)}) %collective-permute-start.4) | collective-permute-done | bytes 786464 | tf_op jit(solution)/shard_map/ppermute | solution.py:415
  122.7 0.0 collective-permute-start.6
  122.7 0.0 collective-permute-done.10.refs_3_
  122.7 0.5 collective-permute-start.5
  123.2 0.0 collective-permute-done.1.refs_2_
  123.2 0.0 collective-permute-start.2
  123.2 0.0 collective-permute-done.9.refs_1_
  123.2 15.2 %down_grad.1 = (bf16[1024,3072]{1,0:T(8,128)(2,1)}, bf16[2048,3072]{1,0:T(8,128)(2,1)}) custom-call(bf16[2048,1024]{1,0:T(8,128)(2,1)S(1)} %get-tuple-element.16.hidden, bf16[2048,3072]{1,0:T(8,128)(2,1)} %dy.3, bf16[1024,512]{1,0:T(8,128)(2,1)S(1)} %get-tuple-element.17.block, bf16[512,1536]{1,0:T(8,128)(2,1)S(1)} %get-tuple-element.15.refs_0_, ...), custom_call_target="tpu_custom_call" | custom-call | flops 12884901888 | bytes 25165824 | tf_op jit(solution)/shard_map/down_grad/pallas_call | solution.py:360
  138.5 0.0 collective-permute-done.6.refs_0_
  138.5 0.0 collective-permute-done.8.refs_1_
  138.5 2.1 %write.2.refs_2_ = bf16[2048,3072]{1,0:T(8,128)(2,1)} custom-call(bf16[256,1536]{1,0:T(8,128)(2,1)S(1)} %collective-permute-done.6.refs_0_, bf16[512,1536]{1,0:T(8,128)(2,1)S(1)} %collective-permute-done.8.refs_1_, bf16[256,1536]{1,0:T(8,128)(2,1)S(1)} %collective-permute-done.1.refs_2_, ...), custom_call_target="tpu_custom_call", output_to_operand_aliasing={{}: (4, {})} | custom-call | flops 1000000000 | bytes 25165824 | tf_op jit(solution)/shard_map/write/pallas_call | solution.py:387
  140.6 0.0 collective-permute-done.5.refs_1_
  140.6 0.0 collective-permute-done.2.refs_0_
  140.6 1.2 write.3
Async XLA Ops:
  64.9 58.3 %collective-permute-start.9 = (bf16[512,1536]{1,0:T(8,128)(2,1)S(1)}, bf16[512,1536]{1,0:T(8,128)(2,1)S(1)}, u32[]{:S(2)}, u32[]{:S(2)}) collective-permute-start(bf16[512,1536]{1,0:T(8,128)(2,1)S(1)} %get-tuple-element.15.refs_0_), channel_id=1, source_target_pairs={{0,1},{1,0},{2,3},{3,2},{4,5},{5,4},{6,7},{7,6}} | collective-permute-start | bytes 4718600 | tf_op jit(solution)/shard_map/ppermute | solution.py:415
  64.9 39.4 %collective-permute-start.7 = (bf16[512,1536]{1,0:T(8,128)(2,1)S(1)}, bf16[512,1536]{1,0:T(8,128)(2,1)S(1)}, u32[]{:S(2)}, u32[]{:S(2)}) collective-permute-start(bf16[512,1536]{1,0:T(8,128)(2,1)S(1)} %get-tuple-element.15.refs_0_), channel_id=1, source_target_pairs={{0,4},{1,3},{2,6},{3,1},{4,0},{5,7},{6,2},{7,5}} | collective-permute-start | bytes 4718600 | tf_op jit(solution)/shard_map/ppermute | solution.py:415
  66.5 37.0 %collective-permute-start.3 = (bf16[256,1536]{1,0:T(8,128)(2,1)S(1)}, bf16[256,1536]{1,0:T(8,128)(2,1)S(1)}, u32[]{:S(2)}, u32[]{:S(2)}) collective-permute-start(bf16[256,1536]{1,0:T(8,128)(2,1)S(1)} %get-tuple-element.26), channel_id=1, source_target_pairs={{0,2},{1,5},{2,0},{3,7},{4,6},{5,1},{6,4},{7,3}} | collective-permute-start | bytes 2359304 | tf_op jit(solution)/shard_map/ppermute | solution.py:415
  67.1 34.7 %collective-permute-start = (bf16[256,1536]{1,0:T(8,128)(2,1)S(1)}, bf16[256,1536]{1,0:T(8,128)(2,1)S(1)}, u32[]{:S(2)}, u32[]{:S(2)}) collective-permute-start(bf16[256,1536]{1,0:T(8,128)(2,1)S(1)} %get-tuple-element.27), channel_id=1, source_target_pairs={{0,2},{1,5},{2,0},{3,7},{4,6},{5,1},{6,4},{7,3}} | collective-permute-start | bytes 2359304 | tf_op jit(solution)/shard_map/ppermute | solution.py:415
  101.7 21.0 %collective-permute-start.10 = (bf16[256,1536]{1,0:T(8,128)(2,1)S(1)}, bf16[256,1536]{1,0:T(8,128)(2,1)S(1)}, u32[]{:S(2)}, u32[]{:S(2)}) collective-permute-start(bf16[256,1536]{1,0:T(8,128)(2,1)S(1)} %collective-permute-done.refs_2_), channel_id=1, source_target_pairs={{0,1},{1,0},{2,3},{3,2},{4,5},{5,4},{6,7},{7,6}} | collective-permute-start | bytes 2359304 | tf_op jit(solution)/shard_map/ppermute | solution.py:415
  102.3 20.9 %collective-permute-start.1 = (bf16[256,1536]{1,0:T(8,128)(2,1)S(1)}, bf16[256,1536]{1,0:T(8,128)(2,1)S(1)}, u32[]{:S(2)}, u32[]{:S(2)}) collective-permute-start(bf16[256,1536]{1,0:T(8,128)(2,1)S(1)} %collective-permute-done.refs_2_), channel_id=1, source_target_pairs={{0,4},{1,3},{2,6},{3,1},{4,0},{5,7},{6,2},{7,5}} | collective-permute-start | bytes 2359304 | tf_op jit(solution)/shard_map/ppermute | solution.py:415
  103.5 19.1 %collective-permute-start.4 = (bf16[256,1536]{1,0:T(8,128)(2,1)S(1)}, bf16[256,1536]{1,0:T(8,128)(2,1)S(1)}, u32[]{:S(2)}, u32[]{:S(2)}) collective-permute-start(bf16[256,1536]{1,0:T(8,128)(2,1)S(1)} %collective-permute-done.3.refs_4_), channel_id=1, source_target_pairs={{0,4},{1,3},{2,6},{3,1},{4,0},{5,7},{6,2},{7,5}} | collective-permute-start | bytes 2359304 | tf_op jit(solution)/shard_map/ppermute | solution.py:415
  104.3 34.2 %collective-permute-start.8 = (bf16[512,1536]{1,0:T(8,128)(2,1)S(1)}, bf16[512,1536]{1,0:T(8,128)(2,1)S(1)}, u32[]{:S(2)}, u32[]{:S(2)}) collective-permute-start(bf16[512,1536]{1,0:T(8,128)(2,1)S(1)} %collective-permute-done.7.refs_5_), channel_id=1, source_target_pairs={{0,1},{1,0},{2,3},{3,2},{4,5},{5,4},{6,7},{7,6}} | collective-permute-start | bytes 4718600 | tf_op jit(solution)/shard_map/ppermute | solution.py:415
  122.7 15.8 %collective-permute-start.6 = (bf16[256,1536]{1,0:T(8,128)(2,1)S(1)}, bf16[256,1536]{1,0:T(8,128)(2,1)S(1)}, u32[]{:S(2)}, u32[]{:S(2)}) collective-permute-start(bf16[256,1536]{1,0:T(8,128)(2,1)S(1)} %collective-permute-done.3.refs_4_), channel_id=1, source_target_pairs={{0,1},{1,0},{2,3},{3,2},{4,5},{5,4},{6,7},{7,6}} | collective-permute-start | bytes 2359304 | tf_op jit(solution)/shard_map/ppermute | solution.py:415
  122.7 17.9 %collective-permute-start.5 = (bf16[256,1536]{1,0:T(8,128)(2,1)S(1)}, bf16[256,1536]{1,0:T(8,128)(2,1)S(1)}, u32[]{:S(2)}, u32[]{:S(2)}) collective-permute-start(bf16[256,1536]{1,0:T(8,128)(2,1)S(1)} %collective-permute-done.4.refs_3_), channel_id=1, source_target_pairs={{0,1},{1,0},{2,3},{3,2},{4,5},{5,4},{6,7},{7,6}} | collective-permute-start | bytes 2359304 | tf_op jit(solution)/shard_map/ppermute | solution.py:415
  123.2 17.4 %collective-permute-start.2 = (bf16[256,1536]{1,0:T(8,128)(2,1)S(1)}, bf16[256,1536]{1,0:T(8,128)(2,1)S(1)}, u32[]{:S(2)}, u32[]{:S(2)}) collective-permute-start(bf16[256,1536]{1,0:T(8,128)(2,1)S(1)} %collective-permute-done.1.refs_2_), channel_id=1, source_target_pairs={{0,1},{1,0},{2,3},{3,2},{4,5},{5,4},{6,7},{7,6}} | collective-permute-start | bytes 2359304 | tf_op jit(solution)/shard_map/ppermute | solution.py:415

commit v5 on v4

--- a/solution.py
+++ b/solution.py
@@ -8,7 +8,7 @@
 from jax.sharding import PartitionSpec as P
 
 
-SCATTER_MIB, WIDE_MIB, DOWN_MIB = 47, 26, 26
+SCATTER_MIB, WIDE_MIB, DOWN_MIB = 44, 26, 26
 
 BF16, F32 = jnp.bfloat16, jnp.float32
 ROWS, D, FL = 2048, 3072, 1024
@@ -18,7 +18,8 @@
 W = 512
 PIECES = HALF // W
 BN = 512
-PARTS = D // BN
+EARLY = 3 * BN
+LATE = (D - EARLY) // BN
 STEPS = ROWS // M
 ANY = pl.BlockSpec(memory_space=pl.ANY)
 
@@ -66,8 +67,8 @@
 
 def scatter_kernel(
     dy, gate, up, w_gate, w_up, w_down,
-    shard, d_gate, d_up, hidden, block,
-    wg, wu, wd, dyb, gb, ub, dgb, dub, acc, sum_own,
+    shard, upper, lower, d_gate, d_up, hidden, block,
+    wide, wd, inb, dgb, dub, acc, sum_own,
     sib_out, sib_in, one_out, one_in, two_out, two_in,
     down_sem, wide_sem, in_sem,
     sib_s, sib_r, one_s, one_r, two_s, two_r,
@@ -82,10 +83,15 @@
     def inputs(p, slot):
         made = []
         for h, row in enumerate(rows_of(p, x, y)):
-            rows = pl.ds(pl.multiple_of(row, U), U)
-            for k, (near, far) in enumerate(((dyb, dy), (gb, gate), (ub, up))):
-                made.append(pltpu.make_async_copy(far.at[rows], near.at[slot, pl.ds(h * U, U)], in_sem.at[slot, h, k]))
+            rows, at = pl.ds(pl.multiple_of(row, U), U), 0
+            for far in (dy, gate, up):
+                near = inb.at[slot, pl.ds(h * U, U), pl.ds(at, far.shape[1])]
+                made.append(pltpu.make_async_copy(far.at[rows], near, in_sem.at[slot]))
+                at += far.shape[1]
         return made
+
+    def inputs_here(slot):
+        pltpu.make_async_copy(inb.at[slot], inb.at[slot], in_sem.at[slot]).wait()
 
     def columns(base, j):
         return pl.ds(pl.multiple_of(base + j * W, 256), W)
@@ -94,14 +100,14 @@
     for n in range(FL // 256):
         at = pl.ds(n * 256, 256)
         down.append(pltpu.make_async_copy(w_down.at[at], wd.at[at], down_sem.at[n]))
-    wide = {}
+    slices = {}
     for j in range(PIECES):
         for side, base in ((0, sib_col), (1, own_col)):
             at = columns(base, j)
-            wide[side, j] = (
-                pltpu.make_async_copy(w_gate.at[at], wg.at[at], wide_sem.at[side, j, 0]),
-                pltpu.make_async_copy(w_up.at[at], wu.at[at], wide_sem.at[side, j, 1]),
-            )
+            slices[side, j] = [
+                pltpu.make_async_copy(w.at[at], wide.at[k, at], wide_sem.at[side, j])
+                for k, w in enumerate((w_gate, w_up))
+            ]
 
     def remote(src, dst, send, recv, to):
         return pltpu.make_async_remote_copy(
@@ -118,15 +124,15 @@
     def to_second(k, j):
         return remote(two_out.at[k, j], two_in.at[k, j], two_s, two_r.at[k, j], second)
 
-    for c in inputs(0, 0):
-        c.start()
-    for c in down:
+    for c in inputs(0, 0) + down[:2]:
         c.start()
 
     barrier = pltpu.get_barrier_semaphore()
     for other in (sibling, first, second):
         pl.semaphore_signal(barrier, inc=1, device_id={"tp": other}, device_id_type=pl.DeviceIdType.MESH)
     pl.semaphore_wait(barrier, 3)
+    for c in down[2:]:
+        c.start()
 
     def keep(to, p, at, value):
         value = value.astype(BF16)
@@ -136,8 +142,9 @@
 
     def hidden_grads(p, slot, n):
         at = slice(n * 256, (n + 1) * 256)
-        d_hidden = nt(dyb[slot], wd[at, :])
-        g, u = gb[slot, :, at].astype(F32), ub[slot, :, at].astype(F32)
+        d_hidden = nt(inb[slot, :, :D], wd[at, :])
+        g = inb[slot, :, D + n * 256 : D + (n + 1) * 256].astype(F32)
+        u = inb[slot, :, D + FL + n * 256 : D + FL + (n + 1) * 256].astype(F32)
         s = jax.nn.sigmoid(g)
         act = g * s
         keep(hidden, p, at, act * u)
@@ -146,13 +153,13 @@
 
     def term(base, j):
         at = columns(base, j)
-        return (nt(dgb[...], wg[at, :]) + nt(dub[...], wu[at, :])).reshape(2, U, W)
-
-    def for_sibling(p, j, reused):
-        if reused:
-            to_sibling(p, j).wait_send()
-        sib_out[p % 2, j] = term(sib_col, j).astype(BF16)
-        to_sibling(p, j).start()
+        return (nt(dgb[...], wide[0, at, :]) + nt(dub[...], wide[1, at, :])).reshape(2, U, W)
+
+    def for_sibling(p, pieces):
+        for j in pieces:
+            sib_out[p % 2, j] = term(sib_col, j).astype(BF16)
+        for j in pieces:
+            to_sibling(p, j).start()
 
     def chip_sum(p, j, h):
         return acc[j, h] + sib_in[p % 2, j, h].astype(F32)
@@ -180,12 +187,10 @@
                 sum_own[2 * (p - 6) + h, j] = chip_sum(p, j, h)
 
     def diagonal_step(p, ready):
-        for n in range(FL // 256):
-            hidden_grads(p, p, n)
         for j in range(PIECES + 1):
             if j < PIECES:
                 ready(0, j)
-                for_sibling(p, j, False)
+                for_sibling(p, (j,))
             if j:
                 ready(1, j - 1)
                 acc[j - 1] = term(own_col, j - 1)
@@ -193,37 +198,41 @@
                 send_diagonal(p, j - 1)
 
     def arrived(side, j):
-        for c in wide[side, j]:
-            c.wait()
+        here = wide.at[:, columns((sib_col, own_col)[side], j)]
+        pltpu.make_async_copy(here, here, wide_sem.at[side, j]).wait()
 
     down_inputs = []
-    for k in range(ROWS // M):
-        near = dyb.at[k // PARTS, :, pl.ds(k % PARTS * BN, BN)]
-        down_inputs.append(
-            pltpu.make_async_copy(dy.at[pl.ds(k * M, M), pl.ds(0, BN)], near, in_sem.at[k // 6, k % 6 // 3, k % 3])
-        )
-
-    for c in inputs(0, 0):
+    for k in range(ROWS // FL):
+        near = wd.at[:, pl.ds(k * EARLY, EARLY)]
+        down_inputs.append(pltpu.make_async_copy(dy.at[pl.ds(k * FL, FL), pl.ds(0, EARLY)], near, down_sem.at[k]))
+
+    inputs_here(0)
+    for c in down[:2]:
         c.wait()
-    for j in range(PIECES):
-        for side in range(2):
-            for c in wide[side, j]:
-                c.start()
+    for c in slices[0, 0] + slices[0, 1]:
+        c.start()
+    for n in range(2):
+        hidden_grads(0, 0, n)
+    for c in down[2:]:
+        c.wait()
+    for k in ((1, 0), (0, 2), (1, 1), (1, 2)):
+        for c in slices[k]:
+            c.start()
     for c in inputs(1, 1):
         c.start()
-    for c in down:
-        c.wait()
+    for n in range(2, 4):
+        hidden_grads(0, 0, n)
     diagonal_step(0, arrived)
-    for c in inputs(1, 1):
-        c.wait()
+    inputs_here(1)
     for c in inputs(2, 0):
         c.start()
+    for n in range(FL // 256):
+        hidden_grads(1, 1, n)
     diagonal_step(1, lambda side, j: None)
 
     def step(p, carry):
         slot = p % 2
-        for c in inputs(p, slot):
-            c.wait()
+        inputs_here(slot)
 
         @pl.when(p < STEPS - 1)
         def _():
@@ -244,7 +253,8 @@
             keep_own(6)
 
         for j in range(PIECES):
-            for_sibling(p, j, True)
+            to_sibling(p, j).wait_send()
+        for_sibling(p, range(PIECES))
         for j in range(PIECES):
             acc[j] = term(own_col, j)
 
@@ -259,8 +269,8 @@
 
     for c in down_inputs:
         c.wait()
-    for n in range(0, BN, 256):
-        right = jnp.concatenate([dyb[k // PARTS, :, pl.ds(k % PARTS * BN + n, 256)] for k in range(ROWS // M)])
+    for n in range(0, EARLY, 256):
+        right = jnp.concatenate([wd[:, pl.ds(k * EARLY + n, 256)] for k in range(ROWS // FL)])
         block[:, pl.ds(n, 256)] = turned(hidden[...], right).astype(BF16)
 
     for q in range(4):
@@ -268,7 +278,8 @@
             to_first(4 + q, j).wait_recv()
             to_second(q, j).wait_recv()
             total = sum_own[q, j] + one_in[4 + q, j].astype(F32) + two_in[q, j].astype(F32)
-            shard[pl.ds(q * U, U), pl.ds(j * W, W)] = total.astype(BF16)
+            for to, row in ((upper, lower)[q // 2], q % 2), (shard, q):
+                to[pl.ds(row * U, U), pl.ds(j * W, W)] = total.astype(BF16)
     for p in (STEPS - 2, STEPS - 1):
         for j in range(PIECES):
             to_sibling(p, j).wait_send()
@@ -278,21 +289,20 @@
 
 def scatter(dy, gate, up, w_gate, w_up, w_down):
     dma = pltpu.SemaphoreType.DMA
-    hid = pltpu.VMEM((ROWS, FL), BF16)
+    hid, part = pltpu.VMEM((ROWS, FL), BF16), pltpu.VMEM((M, HALF), BF16)
     units = lambda n: pltpu.VMEM((n, PIECES, U, W), BF16)
     twin = pltpu.VMEM((2, PIECES, 2, U, W), BF16)
     return pl.pallas_call(
         scatter_kernel,
-        out_shape=(pltpu.VMEM((2 * M, HALF), BF16), hid, hid, hid, pltpu.VMEM((FL, BN), BF16)),
+        out_shape=(pltpu.VMEM((2 * M, HALF), BF16), part, part, hid, hid, hid, pltpu.VMEM((FL, EARLY), BF16)),
         in_specs=[ANY] * 6,
-        out_specs=(pl.BlockSpec(memory_space=pltpu.VMEM),) * 5,
+        out_specs=(pl.BlockSpec(memory_space=pltpu.VMEM),) * 7,
         scratch_shapes=[
-            pltpu.VMEM((D, FL), BF16), pltpu.VMEM((D, FL), BF16), pltpu.VMEM((FL, D), BF16),
-            pltpu.VMEM((2, M, D), BF16), pltpu.VMEM((2, M, FL), BF16), pltpu.VMEM((2, M, FL), BF16),
+            pltpu.VMEM((2, D, FL), BF16), pltpu.VMEM((FL, D), BF16), pltpu.VMEM((2, M, D + 2 * FL), BF16),
             pltpu.VMEM((M, FL), BF16), pltpu.VMEM((M, FL), BF16),
             pltpu.VMEM((PIECES, 2, U, W), F32), pltpu.VMEM((4, PIECES, U, W), F32),
             twin, twin, units(8), units(8), units(4), units(4),
-            dma((FL // 256,)), dma((2, PIECES, 2)), dma((2, 2, 3)),
+            dma((FL // 256,)), dma((2, PIECES)), dma((2,)),
             dma((2, PIECES)), dma((2, PIECES)), dma, dma((8, PIECES)), dma, dma((4, PIECES)),
         ],
         compiler_params=pltpu.CompilerParams(
@@ -335,38 +345,49 @@
 
 def down_kernel(spots, hidden, dy, block, *refs):
     n = len(spots)
-    parts, out, dx, sem = refs[:n], refs[n], refs[n + 1], refs[n + 2]
+    parts, (out, dx, made, part_sem, block_sem, made_sem) = refs[:n], refs[n:]
     step, last = pl.program_id(0), pl.num_programs(0) - 1
+
+    def save(i):
+        cols = pl.ds(pl.multiple_of(EARLY + i * BN, BN), BN)
+        return pltpu.make_async_copy(made.at[i % 2], out.at[:, cols], made_sem.at[i % 2])
+
+    early = pltpu.make_async_copy(block, out.at[:, pl.ds(0, EARLY)], block_sem)
 
     @pl.when(step == 0)
     def _():
-        for c in places(parts, spots, dx, sem):
+        early.start()
+        for c in places(parts, spots, dx, part_sem):
             c.start()
 
-    @pl.when(step < last)
+    @pl.when(step >= 2)
     def _():
-        out[...] = turned(hidden[...], dy[...]).astype(BF16)
+        save(step - 2).wait()
+
+    made[step % 2] = turned(hidden[...], dy[...]).astype(BF16)
+    save(step).start()
 
     @pl.when(step == last)
     def _():
-        out[...] = block[...]
-        for c in places(parts, spots, dx, sem):
+        early.wait()
+        for c in places(parts, spots, dx, part_sem):
             c.wait()
+        save(step - 1).wait()
+        save(step).wait()
 
 
 def down_grad(hidden, dy, block, parts, spots):
     n = len(parts)
+    dma = pltpu.SemaphoreType.DMA
     whole = lambda *shape: pl.BlockSpec(shape, lambda i: (0, 0), pipeline_mode=pl.Buffered(1))
     return pl.pallas_call(
         functools.partial(down_kernel, spots),
-        grid=(PARTS,),
+        grid=(LATE,),
         out_shape=(jax.ShapeDtypeStruct((FL, D), BF16), jax.ShapeDtypeStruct((ROWS, D), BF16)),
-        in_specs=[
-            whole(ROWS, FL), pl.BlockSpec((ROWS, BN), lambda i: (0, jnp.minimum(i + 1, PARTS - 1))), whole(FL, BN),
-        ]
+        in_specs=[whole(ROWS, FL), pl.BlockSpec((ROWS, BN), lambda i: (0, i + EARLY // BN)), whole(FL, EARLY)]
         + [ANY] * n,
-        out_specs=(pl.BlockSpec((FL, BN), lambda i: (0, (i + 1) % PARTS)), ANY),
-        scratch_shapes=[pltpu.SemaphoreType.DMA((n, 2 * M // U))],
+        out_specs=(ANY, ANY),
+        scratch_shapes=[pltpu.VMEM((2, FL, BN), BF16), dma((n, 2 * M // U)), dma, dma((2,))],
         compiler_params=pltpu.CompilerParams(vmem_limit_bytes=DOWN_MIB * 2**20),
         cost_estimate=pl.CostEstimate(flops=2 * ROWS * D * FL, bytes_accessed=24 * 2**20, transcendentals=0),
         name="down_grad",
@@ -415,26 +436,31 @@
         return lax.ppermute(value, "tp", perm)
 
     def step(x, dy, gate, up, w_gate, w_up, w_down):
-        shard, d_gate, d_up, hidden, block = scatter(dy, gate, up, w_gate, w_up, w_down)
-        first_a, first_b = send(shard[:M], FIRST), send(shard[M:], FIRST)
+        shard, upper, lower, d_gate, d_up, hidden, block = scatter(dy, gate, up, w_gate, w_up, w_down)
+        first_a, first_b = send(upper, FIRST), send(lower, FIRST)
         second = send(shard, SECOND)
         own_twin = send(shard, SIBLING)
-        both_a, both_b = send(first_a, SECOND), send(first_b, SECOND)
+        both_a = send(first_a, SECOND)
+        both_b, both_c = send(first_b[:U], SECOND), send(first_b[U:], SECOND)
         first_a_twin, first_b_twin = send(first_a, SIBLING), send(first_b, SIBLING)
         second_twin = send(second, SIBLING)
         both_a_twin, both_b_twin = send(both_a, SIBLING), send(both_b, SIBLING)
+        both_c_twin = send(both_c, SIBLING)
         wide = wide_grads(x, d_gate, d_up, 0, 3)
         dw_gate, dw_up = wide_grads(x, d_gate, d_up, 3, 3, wide)
         dw_down, dx = down_grad(
-            hidden, dy, block, (shard, own_twin, first_a, first_a_twin, first_b, second),
-            ((0, 0, 0, 0, 2 * M), (1, 0, 0, 0, 2 * M), (0, 1, 0, 0, M), (1, 1, 0, 0, M), (0, 1, 0, M, M), (0, 0, 1, 0, 2 * M)),
+            hidden, dy, block, (shard, own_twin, first_a, first_b, second),
+            ((0, 0, 0, 0, 2 * M), (1, 0, 0, 0, 2 * M), (0, 1, 0, 0, M), (0, 1, 0, M, M), (0, 0, 1, 0, 2 * M)),
         )
         dx = write(
-            (first_b_twin, second_twin, both_a, both_b),
-            ((1, 1, 0, M, M), (1, 0, 1, 0, 2 * M), (0, 1, 1, 0, M), (0, 1, 1, M, M)),
+            (first_a_twin, first_b_twin, second_twin, both_a),
+            ((1, 1, 0, 0, M), (1, 1, 0, M, M), (1, 0, 1, 0, 2 * M), (0, 1, 1, 0, M)),
             dx,
         )
-        dx = write((both_a_twin, both_b_twin), ((1, 1, 1, 0, M), (1, 1, 1, M, M)), dx)
+        dx = write(
+            (both_a_twin, both_b, both_c), ((1, 1, 1, 0, M), (0, 1, 1, M, U), (0, 1, 1, M + U, U)), dx
+        )
+        dx = write((both_b_twin, both_c_twin), ((1, 1, 1, M, U), (1, 1, 1, M + U, U)), dx)
         return dx, dw_gate, dw_up, dw_down
 
     tokens, columns, rows = P("dp", None), P(None, "tp"), P("tp", None)

time: 142 us -> 140 us (0.986)
  Pallas kernels: 115 us -> 111 us
  starting transfers between devices: 6.68 us -> 9.01 us
    pallas_call x1, Pallas kernels: 15.2 us -> 10.1 us  [down_grad(): pl.pallas_call(functools.partial(down_kernel, spots), grid=(LATE,), out_s...]
    ppermute x11 -> x13, starting transfers between devices: 6.68 us -> 9.01 us  [send(): return lax.ppermute(value, 'tp', perm)]
    pallas_call x2 -> x3, Pallas kernels: 3.31 us -> 4.32 us  [write(): pl.pallas_call(functools.partial(write_kernel, spots), out_shape=jax.Shap...]
    ppermute x11 -> x13, waiting for transfers between devices: 19 us -> 18.4 us  [send(): return lax.ppermute(value, 'tp', perm)]
  transfers between devices with their start and end apart: 11 -> 13, of which waited for: 2 -> 2; matrix products, arithmetic and copies ran while one was open for 0% -> 0% of each run, Pallas kernels for 35% -> 33%
where the time goes in v5:
time: 140 us; the launch traced here: 139 us
  Pallas kernels  111 us (79%)
  waiting for transfers between devices  18.4 us (13%)
  starting transfers between devices  9.01 us (6%)
    pallas_call x1, Pallas kernels, scatter(): pl.pallas_call(scatter_kernel, out_shape=(pltpu.VMEM((2 * M, HALF), BF16)...  64.3 us
    pallas_call x2, Pallas kernels, wide_grads(): pl.pallas_call(wide_kernel, grid=(count,), out_shape=(shape, shape), in_s...  32.3 us
    ppermute x13, waiting for transfers between devices, send(): return lax.ppermute(value, 'tp', perm)  18.4 us
    pallas_call x1, Pallas kernels, down_grad(): pl.pallas_call(functools.partial(down_kernel, spots), grid=(LATE,), out_s...  10.1 us
    ppermute x13, starting transfers between devices, send(): return lax.ppermute(value, 'tp', perm)  9.01 us
    pallas_call x3, Pallas kernels, write(): pl.pallas_call(functools.partial(write_kernel, spots), out_shape=jax.Shap...  4.32 us
  transfers between devices with their start and end apart: 13, of which 2 were waited for; matrix products, arithmetic and copies ran while one was open for 0% of the time, Pallas kernels for 33%

profile of v5, /device:TPU:0, one launch (start us, length us, event | category | flops | bytes accessed | tf_op | source)
XLA Modules:
  0.0 139.4 jit_solution(4433011193401606504)
XLA Ops:
  0.6 64.3 %scatter.1 = (bf16[512,1536]{1,0:T(8,128)(2,1)S(1)}, bf16[256,1536]{1,0:T(8,128)(2,1)S(1)}, bf16[256,1536]{1,0:T(8,128)(2,1)}, bf16[2048,1024]{1,0:T(8,128)(2,1)...) custom-call(bf16[2048,3072]{1,0:T(8,128)(2,1)} %dy.3, ...), custom_call_target="tpu_custom_call" | custom-call | flops 38654705664 | bytes 62914560 | tf_op jit(solution)/shard_map/scatter/pallas_call | solution.py:295
  64.9 1.1 collective-permute-start
  66.0 0.0 collective-permute-start.12
  66.0 1.5 %collective-permute-start.10 = (bf16[512,1536]{1,0:T(8,128)(2,1)S(1)}, bf16[512,1536]{1,0:T(8,128)(2,1)S(1)}, u32[]{:S(2)}, u32[]{:S(2)}) collective-permute-start(bf16[512,1536]{1,0:T(8,128)(2,1)S(1)} %get-tuple-element.19.refs_0_), channel_id=1, source_target_pairs={{0,4},{1,3},{2,6},{3,1},{4,0},{5,7},{6,2},{7,5}} | collective-permute-start | bytes 4718600 | tf_op jit(solution)/shard_map/ppermute | solution.py:436
  67.5 1.0 collective-permute-start.5
  68.5 16.7 %collective-permute-done.refs_3_ = bf16[256,1536]{1,0:T(8,128)(2,1)S(1)} collective-permute-done((bf16[256,1536]{1,0:T(8,128)(2,1)}, bf16[256,1536]{1,0:T(8,128)(2,1)S(1)}, u32[]{:S(2)}, u32[]{:S(2)}) %collective-permute-start) | collective-permute-done | bytes 786464 | tf_op jit(solution)/shard_map/ppermute | solution.py:436
  85.2 0.1 fusion
  85.3 1.5 %collective-permute-start.3 = (bf16[128,1536]{1,0:T(8,128)(2,1)S(1)}, bf16[128,1536]{1,0:T(8,128)(2,1)S(1)}, u32[]{:S(2)}, u32[]{:S(2)}) collective-permute-start(bf16[128,1536]{1,0:T(8,128)(2,1)S(1)} %get-tuple-element.30), channel_id=1, source_target_pairs={{0,4},{1,3},{2,6},{3,1},{4,0},{5,7},{6,2},{7,5}} | collective-permute-start | bytes 1179656 | tf_op jit(solution)/shard_map/ppermute | solution.py:436
  86.8 16.1 %wide_grads.2 = (bf16[3072,1024]{1,0:T(8,128)(2,1)}, bf16[3072,1024]{1,0:T(8,128)(2,1)}) custom-call(bf16[2048,3072]{1,0:T(8,128)(2,1)} %x.3, bf16[2048,1024]{1,0:T(8,128)(2,1)S(1)} %get-tuple-element.23.d_gate, bf16[2048,1024]{1,0:T(8,128)(2,1)S(1)} %get-tuple-element.24.d_up), custom_call_target="tpu_custom_call" | custom-call | flops 12884901888 | bytes 20971520 | tf_op jit(solution)/shard_map/wide_grads/pallas_call | solution.py:333
  102.9 0.5 collective-permute-start.1
  103.5 0.0 collective-permute-done.5.refs_2_
  103.5 0.0 collective-permute-start.9
  103.5 1.7 %collective-permute-done.3.refs_2_ = bf16[128,1536]{1,0:T(8,128)(2,1)S(1)} collective-permute-done((bf16[128,1536]{1,0:T(8,128)(2,1)S(1)}, bf16[128,1536]{1,0:T(8,128)(2,1)S(1)}, u32[]{:S(2)}, u32[]{:S(2)}) %collective-permute-start.3) | collective-permute-done | bytes 393248 | tf_op jit(solution)/shard_map/ppermute | solution.py:436
  105.1 1.7 %collective-permute-start.6 = (bf16[256,1536]{1,0:T(8,128)(2,1)S(1)}, bf16[256,1536]{1,0:T(8,128)(2,1)S(1)}, u32[]{:S(2)}, u32[]{:S(2)}) collective-permute-start(bf16[256,1536]{1,0:T(8,128)(2,1)S(1)} %collective-permute-done.5.refs_2_), channel_id=1, source_target_pairs={{0,4},{1,3},{2,6},{3,1},{4,0},{5,7},{6,2},{7,5}} | collective-permute-start | bytes 2359304 | tf_op jit(solution)/shard_map/ppermute | solution.py:436
  106.8 0.0 collective-permute-done.10.refs_4_
  106.8 0.7 collective-permute-start.11
  107.5 16.1 %wide_grads.3 = (bf16[3072,1024]{1,0:T(8,128)(2,1)}, bf16[3072,1024]{1,0:T(8,128)(2,1)}) custom-call(bf16[2048,3072]{1,0:T(8,128)(2,1)} %x.3, bf16[2048,1024]{1,0:T(8,128)(2,1)S(1)} %get-tuple-element.23.d_gate, bf16[2048,1024]{1,0:T(8,128)(2,1)S(1)} %get-tuple-element.24.d_up, ...), custom_call_target="tpu_custom_call", output_to_operand_aliasing={{0}: (3, {}), {1}: (4, {})} | custom-call | flops 12884901888 | bytes 20971520 | tf_op jit(solution)/shard_map/wide_grads/pallas_call | solution.py:333
  123.7 0.0 collective-permute-done.1.refs_1_
  123.7 0.2 collective-permute-start.8
  123.9 0.0 collective-permute-done.9.refs_1_
  123.9 0.3 collective-permute-start.4
  124.2 0.0 collective-permute-done.6.refs_3_
  124.2 0.2 collective-permute-start.2
  124.4 0.0 collective-permute-done.12.refs_1_
  124.4 0.3 collective-permute-start.7
  124.7 10.1 %down_grad.1 = (bf16[1024,3072]{1,0:T(8,128)(2,1)}, bf16[2048,3072]{1,0:T(8,128)(2,1)}) custom-call(bf16[2048,1024]{1,0:T(8,128)(2,1)S(1)} %get-tuple-element.20.hidden, bf16[2048,3072]{1,0:T(8,128)(2,1)} %dy.3, bf16[1024,1536]{1,0:T(8,128)(2,1)S(1)} %get-tuple-element.21.block, bf16[512,1536]{1,0:T(8,128)(2,1)S(1)} %get-tuple-element.19.refs_0_, ...), custom_call_target="tpu_custom_call" | custom-call | flops 12884901888 | bytes 25165824 | tf_op jit(solution)/shard_map/down_grad/pallas_call | solution.py:383
  134.8 0.0 collective-permute-done.8.refs_0_
  134.8 0.0 collective-permute-done.11.refs_2_
  134.8 2.1 %write.3.refs_3_ = bf16[2048,3072]{1,0:T(8,128)(2,1)} custom-call(bf16[256,1536]{1,0:T(8,128)(2,1)S(1)} %collective-permute-done.8.refs_0_, bf16[256,1536]{1,0:T(8,128)(2,1)S(1)} %collective-permute-done.9.refs_1_, bf16[512,1536]{1,0:T(8,128)(2,1)S(1)} %collective-permute-done.11.refs_2_, ...), custom_call_target="tpu_custom_call", output_to_operand_aliasing={{}: (4, {})} | custom-call | flops 1000000000 | bytes 25165824 | tf_op jit(solution)/shard_map/write/pallas_call | solution.py:408
  136.9 0.0 collective-permute-done.7.refs_0_
  136.9 1.3 write.4.refs_2_
  138.2 0.0 collective-permute-done.4.refs_1_
  138.2 0.0 collective-permute-done.2.refs_0_
  138.2 1.0 write.5
Async XLA Ops:
  64.9 20.3 %collective-permute-start = (bf16[256,1536]{1,0:T(8,128)(2,1)}, bf16[256,1536]{1,0:T(8,128)(2,1)S(1)}, u32[]{:S(2)}, u32[]{:S(2)}) collective-permute-start(bf16[256,1536]{1,0:T(8,128)(2,1)} %get-tuple-element.17), channel_id=1, source_target_pairs={{0,2},{1,5},{2,0},{3,7},{4,6},{5,1},{6,4},{7,3}} | collective-permute-start | bytes 2359304 | tf_op jit(solution)/shard_map/ppermute | solution.py:436
  66.0 58.4 %collective-permute-start.12 = (bf16[512,1536]{1,0:T(8,128)(2,1)S(1)}, bf16[512,1536]{1,0:T(8,128)(2,1)S(1)}, u32[]{:S(2)}, u32[]{:S(2)}) collective-permute-start(bf16[512,1536]{1,0:T(8,128)(2,1)S(1)} %get-tuple-element.19.refs_0_), channel_id=1, source_target_pairs={{0,1},{1,0},{2,3},{3,2},{4,5},{5,4},{6,7},{7,6}} | collective-permute-start | bytes 4718600 | tf_op jit(solution)/shard_map/ppermute | solution.py:436
  66.0 40.8 %collective-permute-start.10 = (bf16[512,1536]{1,0:T(8,128)(2,1)S(1)}, bf16[512,1536]{1,0:T(8,128)(2,1)S(1)}, u32[]{:S(2)}, u32[]{:S(2)}) collective-permute-start(bf16[512,1536]{1,0:T(8,128)(2,1)S(1)} %get-tuple-element.19.refs_0_), channel_id=1, source_target_pairs={{0,4},{1,3},{2,6},{3,1},{4,0},{5,7},{6,2},{7,5}} | collective-permute-start | bytes 4718600 | tf_op jit(solution)/shard_map/ppermute | solution.py:436
  67.5 36.0 %collective-permute-start.5 = (bf16[256,1536]{1,0:T(8,128)(2,1)S(1)}, bf16[256,1536]{1,0:T(8,128)(2,1)S(1)}, u32[]{:S(2)}, u32[]{:S(2)}) collective-permute-start(bf16[256,1536]{1,0:T(8,128)(2,1)S(1)} %get-tuple-element.18), channel_id=1, source_target_pairs={{0,2},{1,5},{2,0},{3,7},{4,6},{5,1},{6,4},{7,3}} | collective-permute-start | bytes 2359304 | tf_op jit(solution)/shard_map/ppermute | solution.py:436
  85.3 19.9 %collective-permute-start.3 = (bf16[128,1536]{1,0:T(8,128)(2,1)S(1)}, bf16[128,1536]{1,0:T(8,128)(2,1)S(1)}, u32[]{:S(2)}, u32[]{:S(2)}) collective-permute-start(bf16[128,1536]{1,0:T(8,128)(2,1)S(1)} %get-tuple-element.30), channel_id=1, source_target_pairs={{0,4},{1,3},{2,6},{3,1},{4,0},{5,7},{6,2},{7,5}} | collective-permute-start | bytes 1179656 | tf_op jit(solution)/shard_map/ppermute | solution.py:436
  102.9 20.7 %collective-permute-start.1 = (bf16[128,1536]{1,0:T(8,128)(2,1)S(1)}, bf16[128,1536]{1,0:T(8,128)(2,1)S(1)}, u32[]{:S(2)}, u32[]{:S(2)}) collective-permute-start(bf16[128,1536]{1,0:T(8,128)(2,1)S(1)} %get-tuple-element.31), channel_id=1, source_target_pairs={{0,4},{1,3},{2,6},{3,1},{4,0},{5,7},{6,2},{7,5}} | collective-permute-start | bytes 1179656 | tf_op jit(solution)/shard_map/ppermute | solution.py:436
  103.5 20.4 %collective-permute-start.9 = (bf16[256,1536]{1,0:T(8,128)(2,1)S(1)}, bf16[256,1536]{1,0:T(8,128)(2,1)S(1)}, u32[]{:S(2)}, u32[]{:S(2)}) collective-permute-start(bf16[256,1536]{1,0:T(8,128)(2,1)S(1)} %collective-permute-done.refs_3_), channel_id=1, source_target_pairs={{0,1},{1,0},{2,3},{3,2},{4,5},{5,4},{6,7},{7,6}} | collective-permute-start | bytes 2359304 | tf_op jit(solution)/shard_map/ppermute | solution.py:436
  105.1 19.1 %collective-permute-start.6 = (bf16[256,1536]{1,0:T(8,128)(2,1)S(1)}, bf16[256,1536]{1,0:T(8,128)(2,1)S(1)}, u32[]{:S(2)}, u32[]{:S(2)}) collective-permute-start(bf16[256,1536]{1,0:T(8,128)(2,1)S(1)} %collective-permute-done.5.refs_2_), channel_id=1, source_target_pairs={{0,4},{1,3},{2,6},{3,1},{4,0},{5,7},{6,2},{7,5}} | collective-permute-start | bytes 2359304 | tf_op jit(solution)/shard_map/ppermute | solution.py:436
  106.8 28.0 %collective-permute-start.11 = (bf16[512,1536]{1,0:T(8,128)(2,1)S(1)}, bf16[512,1536]{1,0:T(8,128)(2,1)S(1)}, u32[]{:S(2)}, u32[]{:S(2)}) collective-permute-start(bf16[512,1536]{1,0:T(8,128)(2,1)S(1)} %collective-permute-done.10.refs_4_), channel_id=1, source_target_pairs={{0,1},{1,0},{2,3},{3,2},{4,5},{5,4},{6,7},{7,6}} | collective-permute-start | bytes 4718600 | tf_op jit(solution)/shard_map/ppermute | solution.py:436
  123.7 11.1 %collective-permute-start.8 = (bf16[256,1536]{1,0:T(8,128)(2,1)S(1)}, bf16[256,1536]{1,0:T(8,128)(2,1)S(1)}, u32[]{:S(2)}, u32[]{:S(2)}) collective-permute-start(bf16[256,1536]{1,0:T(8,128)(2,1)S(1)} %collective-permute-done.5.refs_2_), channel_id=1, source_target_pairs={{0,1},{1,0},{2,3},{3,2},{4,5},{5,4},{6,7},{7,6}} | collective-permute-start | bytes 2359304 | tf_op jit(solution)/shard_map/ppermute | solution.py:436
  123.9 14.3 %collective-permute-start.4 = (bf16[128,1536]{1,0:T(8,128)(2,1)S(1)}, bf16[128,1536]{1,0:T(8,128)(2,1)S(1)}, u32[]{:S(2)}, u32[]{:S(2)}) collective-permute-start(bf16[128,1536]{1,0:T(8,128)(2,1)S(1)} %collective-permute-done.3.refs_2_), channel_id=1, source_target_pairs={{0,1},{1,0},{2,3},{3,2},{4,5},{5,4},{6,7},{7,6}} | collective-permute-start | bytes 1179656 | tf_op jit(solution)/shard_map/ppermute | solution.py:436
  124.2 14.0 %collective-permute-start.2 = (bf16[128,1536]{1,0:T(8,128)(2,1)S(1)}, bf16[128,1536]{1,0:T(8,128)(2,1)S(1)}, u32[]{:S(2)}, u32[]{:S(2)}) collective-permute-start(bf16[128,1536]{1,0:T(8,128)(2,1)S(1)} %collective-permute-done.1.refs_1_), channel_id=1, source_target_pairs={{0,1},{1,0},{2,3},{3,2},{4,5},{5,4},{6,7},{7,6}} | collective-permute-start | bytes 1179656 | tf_op jit(solution)/shard_map/ppermute | solution.py:436
  124.4 12.5 %collective-permute-start.7 = (bf16[256,1536]{1,0:T(8,128)(2,1)S(1)}, bf16[256,1536]{1,0:T(8,128)(2,1)S(1)}, u32[]{:S(2)}, u32[]{:S(2)}) collective-permute-start(bf16[256,1536]{1,0:T(8,128)(2,1)S(1)} %collective-permute-done.6.refs_3_), channel_id=1, source_target_pairs={{0,1},{1,0},{2,3},{3,2},{4,5},{5,4},{6,7},{7,6}} | collective-permute-start | bytes 2359304 | tf_op jit(solution)/shard_map/ppermute | solution.py:436

commit v6 on v5

--- a/solution.py
+++ b/solution.py
@@ -8,11 +8,12 @@
 from jax.sharding import PartitionSpec as P
 
 
-SCATTER_MIB, WIDE_MIB, DOWN_MIB = 44, 26, 26
+SCATTER_MIB, WIDE_MIB, DOWN_MIB = 44, 24, 24
 
 BF16, F32 = jnp.bfloat16, jnp.float32
 ROWS, D, FL = 2048, 3072, 1024
 M = 256
+TAIL = 64
 U = M // 2
 HALF = D // 2
 W = 512
@@ -41,9 +42,10 @@
         flip_x = along_first * half + along_second * (1 - half)
         to_x, to_y = x + flip_x - 2 * x * flip_x, y + flip_y - 2 * y * flip_y
         cols = pl.ds(pl.multiple_of(half * HALF, HALF), HALF)
-        for i in range(0, count, U):
-            rows = pl.ds(pl.multiple_of((to_x * 2 + to_y) * 2 * M + row + i, U), U)
-            copies.append(pltpu.make_async_copy(part.at[pl.ds(i, U)], out.at[rows, cols], sem.at[k, i // U]))
+        run = TAIL if count % U else U
+        for i in range(0, count, run):
+            rows = pl.ds(pl.multiple_of((to_x * 2 + to_y) * 2 * M + row + i, run), run)
+            copies.append(pltpu.make_async_copy(part.at[pl.ds(i, run)], out.at[rows, cols], sem.at[k, i // run]))
     return copies
 
 
@@ -70,7 +72,7 @@
     shard, upper, lower, d_gate, d_up, hidden, block,
     wide, wd, inb, dgb, dub, acc, sum_own,
     sib_out, sib_in, one_out, one_in, two_out, two_in,
-    down_sem, wide_sem, in_sem,
+    down_sem, wide_sem, in_sem, half_r,
     sib_s, sib_r, one_s, one_r, two_s, two_r,
 ):
     me, core, y, x = place()
@@ -186,12 +188,12 @@
             for h in range(2):
                 sum_own[2 * (p - 6) + h, j] = chip_sum(p, j, h)
 
-    def diagonal_step(p, ready):
-        for j in range(PIECES + 1):
-            if j < PIECES:
+    def diagonal_step(p, ready, done):
+        for j in range(done, PIECES + 1):
+            if done + (done > 0) <= j < PIECES:
                 ready(0, j)
                 for_sibling(p, (j,))
-            if j:
+            if j > done:
                 ready(1, j - 1)
                 acc[j - 1] = term(own_col, j - 1)
                 to_sibling(p, j - 1).wait_recv()
@@ -206,29 +208,59 @@
         near = wd.at[:, pl.ds(k * EARLY, EARLY)]
         down_inputs.append(pltpu.make_async_copy(dy.at[pl.ds(k * FL, FL), pl.ds(0, EARLY)], near, down_sem.at[k]))
 
+    def first_piece():
+        halves = [pl.ds(i * (W // 2), W // 2) for i in range(2)]
+
+        def copy(i):
+            a, b = sib_out.at[0, 0, :, :, halves[i]], sib_in.at[0, 0, :, :, halves[i]]
+            return remote(a, b, sib_s.at[0, 0], half_r.at[i], sibling)
+
+        for i in range(2):
+            for side, base in enumerate((sib_col, own_col)):
+                if i == 0:
+                    arrived(side, 0)
+                at = pl.ds(pl.multiple_of(base + i * (W // 2), 256), W // 2)
+                part = (nt(dgb[...], wide[0, at, :]) + nt(dub[...], wide[1, at, :])).reshape(2, U, W // 2)
+                if side:
+                    acc[0, :, :, halves[i]] = part
+                else:
+                    sib_out[0, 0, :, :, halves[i]] = part.astype(BF16)
+                    copy(i).start()
+        for i in range(2):
+            copy(i).wait_recv()
+            for h in range(2):
+                total = acc[0, h, :, halves[i]] + sib_in[0, 0, h, :, halves[i]].astype(F32)
+                one_out[h, 0, :, halves[i]] = total.astype(BF16)
+                a, b = one_out.at[h, 0, :, halves[i]], one_in.at[h, 0, :, halves[i]]
+                remote(a, b, one_s, one_r.at[h, 0], first).start()
+            if i == 0:
+                arrived(0, 1)
+                for_sibling(0, (1,))
+
     inputs_here(0)
     for c in down[:2]:
         c.wait()
-    for c in slices[0, 0] + slices[0, 1]:
+    for c in slices[0, 0] + slices[1, 0]:
         c.start()
     for n in range(2):
         hidden_grads(0, 0, n)
     for c in down[2:]:
         c.wait()
-    for k in ((1, 0), (0, 2), (1, 1), (1, 2)):
+    for k in ((0, 1), (0, 2), (1, 1), (1, 2)):
         for c in slices[k]:
             c.start()
     for c in inputs(1, 1):
         c.start()
     for n in range(2, 4):
         hidden_grads(0, 0, n)
-    diagonal_step(0, arrived)
+    first_piece()
+    diagonal_step(0, arrived, 1)
     inputs_here(1)
     for c in inputs(2, 0):
         c.start()
     for n in range(FL // 256):
         hidden_grads(1, 1, n)
-    diagonal_step(1, lambda side, j: None)
+    diagonal_step(1, lambda side, j: None, 0)
 
     def step(p, carry):
         slot = p % 2
@@ -302,7 +334,7 @@
             pltpu.VMEM((M, FL), BF16), pltpu.VMEM((M, FL), BF16),
             pltpu.VMEM((PIECES, 2, U, W), F32), pltpu.VMEM((4, PIECES, U, W), F32),
             twin, twin, units(8), units(8), units(4), units(4),
-            dma((FL // 256,)), dma((2, PIECES)), dma((2,)),
+            dma((FL // 256,)), dma((2, PIECES)), dma((2,)), dma((2,)),
             dma((2, PIECES)), dma((2, PIECES)), dma, dma((8, PIECES)), dma, dma((4, PIECES)),
         ],
         compiler_params=pltpu.CompilerParams(
@@ -319,33 +351,88 @@
     return pltpu.with_memory_space_constraint(value, space)
 
 
-def wide_kernel(x, d_gate, d_up, *refs):
-    dw_gate, dw_up = refs[-2:]
-    xt = x[...].T
-    dw_gate[...] = jnp.dot(xt, d_gate[...], preferred_element_type=F32).astype(BF16)
-    dw_up[...] = jnp.dot(xt, d_up[...], preferred_element_type=F32).astype(BF16)
-
-
-def wide_grads(x, d_gate, d_up, start, count, into=(), bm=512):
+def streamed(far, near, sem, start, first, use):
+    step, count = pl.program_id(0), pl.num_programs(0)
+
+    def fetch(i):
+        cols = pl.ds(pl.multiple_of((start + i) * BN, BN), BN)
+        return pltpu.make_async_copy(far.at[:, cols], near.at[i % 2], sem.at[i % 2])
+
+    if first is None:
+
+        @pl.when(step == 0)
+        def _():
+            fetch(0).start()
+
+        fetch(step).wait()
+
+    @pl.when(step + 1 < count)
+    def _():
+        fetch(step + 1).start()
+
+    if first is None:
+        use(near.at[step % 2])
+    else:
+
+        @pl.when(step == 0)
+        def _():
+            use(first)
+
+        @pl.when(step > 0)
+        def _():
+            fetch(step).wait()
+            use(near.at[step % 2])
+
+
+def wide_kernel(start, after, given, x, d_gate, d_up, further, *refs):
+    first = refs[0] if given else None
+    dw_gate, dw_up, ahead, near, sem, ahead_sem = refs[-6:]
+    step, last = pl.program_id(0), pl.num_programs(0) - 1
+    fetch = pltpu.make_async_copy(further.at[:, pl.ds(after * BN, BN)], ahead, ahead_sem)
+
+    def use(block):
+        xt = block[...].T
+        dw_gate[...] = jnp.dot(xt, d_gate[...], preferred_element_type=F32).astype(BF16)
+        dw_up[...] = jnp.dot(xt, d_up[...], preferred_element_type=F32).astype(BF16)
+
+    streamed(x, near, sem, start, first, use)
+
+    @pl.when(step == 0)
+    def _():
+        fetch.start()
+
+    @pl.when(step == last)
+    def _():
+        fetch.wait()
+
+
+def wide_grads(x, d_gate, d_up, start, count, further, after, first=None, into=()):
     whole = pl.BlockSpec((ROWS, FL), lambda i: (0, 0), pipeline_mode=pl.Buffered(1))
-    out = pl.BlockSpec((bm, FL), lambda i: (start + i, 0))
+    block = pl.BlockSpec((ROWS, BN), lambda i: (0, 0), pipeline_mode=pl.Buffered(1))
+    out = pl.BlockSpec((BN, FL), lambda i: (start + i, 0))
     shape = jax.ShapeDtypeStruct((D, FL), BF16)
+    dma = pltpu.SemaphoreType.DMA
+    given = () if first is None else (placed(first, pltpu.VMEM),)
     return pl.pallas_call(
-        wide_kernel,
+        functools.partial(wide_kernel, start, after, bool(given)),
         grid=(count,),
-        out_shape=(shape, shape),
-        in_specs=[pl.BlockSpec((ROWS, bm), lambda i: (0, start + i)), whole, whole] + [ANY] * len(into),
-        out_specs=(out, out),
-        input_output_aliases={3 + k: k for k in range(len(into))},
+        out_shape=(shape, shape, pltpu.VMEM((ROWS, BN), BF16)),
+        in_specs=[ANY, whole, whole, ANY] + [block] * len(given) + [ANY] * len(into),
+        out_specs=(out, out, ANY),
+        scratch_shapes=[pltpu.VMEM((2, ROWS, BN), BF16), dma((2,)), dma],
+        input_output_aliases={4 + len(given) + k: k for k in range(len(into))},
         compiler_params=pltpu.CompilerParams(vmem_limit_bytes=WIDE_MIB * 2**20),
-        cost_estimate=pl.CostEstimate(flops=4 * ROWS * bm * count * FL, bytes_accessed=20 * 2**20, transcendentals=0),
+        cost_estimate=pl.CostEstimate(flops=4 * ROWS * BN * count * FL, bytes_accessed=20 * 2**20, transcendentals=0),
         name="wide_grads",
-    )(placed(x, pltpu.HBM), placed(d_gate, pltpu.VMEM), placed(d_up, pltpu.VMEM), *into)
-
-
-def down_kernel(spots, hidden, dy, block, *refs):
+    )(
+        placed(x, pltpu.HBM), placed(d_gate, pltpu.VMEM), placed(d_up, pltpu.VMEM), placed(further, pltpu.HBM),
+        *given, *into,
+    )
+
+
+def down_kernel(spots, hidden, dy, block, first, *refs):
     n = len(spots)
-    parts, (out, dx, made, part_sem, block_sem, made_sem) = refs[:n], refs[n:]
+    parts, (out, dx, made, near, part_sem, block_sem, made_sem, sem) = refs[:n], refs[n:]
     step, last = pl.program_id(0), pl.num_programs(0) - 1
 
     def save(i):
@@ -353,19 +440,22 @@
         return pltpu.make_async_copy(made.at[i % 2], out.at[:, cols], made_sem.at[i % 2])
 
     early = pltpu.make_async_copy(block, out.at[:, pl.ds(0, EARLY)], block_sem)
+
+    @pl.when(step >= 2)
+    def _():
+        save(step - 2).wait()
+
+    def use(right):
+        made[step % 2] = turned(hidden[...], right[...]).astype(BF16)
+
+    streamed(dy, near, sem, EARLY // BN, first, use)
+    save(step).start()
 
     @pl.when(step == 0)
     def _():
         early.start()
         for c in places(parts, spots, dx, part_sem):
             c.start()
-
-    @pl.when(step >= 2)
-    def _():
-        save(step - 2).wait()
-
-    made[step % 2] = turned(hidden[...], dy[...]).astype(BF16)
-    save(step).start()
 
     @pl.when(step == last)
     def _():
@@ -376,7 +466,7 @@
         save(step).wait()
 
 
-def down_grad(hidden, dy, block, parts, spots):
+def down_grad(hidden, dy, block, first, parts, spots):
     n = len(parts)
     dma = pltpu.SemaphoreType.DMA
     whole = lambda *shape: pl.BlockSpec(shape, lambda i: (0, 0), pipeline_mode=pl.Buffered(1))
@@ -384,14 +474,19 @@
         functools.partial(down_kernel, spots),
         grid=(LATE,),
         out_shape=(jax.ShapeDtypeStruct((FL, D), BF16), jax.ShapeDtypeStruct((ROWS, D), BF16)),
-        in_specs=[whole(ROWS, FL), pl.BlockSpec((ROWS, BN), lambda i: (0, i + EARLY // BN)), whole(FL, EARLY)]
-        + [ANY] * n,
+        in_specs=[whole(ROWS, FL), ANY, whole(FL, EARLY), whole(ROWS, BN)] + [ANY] * n,
         out_specs=(ANY, ANY),
-        scratch_shapes=[pltpu.VMEM((2, FL, BN), BF16), dma((n, 2 * M // U)), dma, dma((2,))],
+        scratch_shapes=[
+            pltpu.VMEM((2, FL, BN), BF16), pltpu.VMEM((2, ROWS, BN), BF16),
+            dma((n, 2 * M // U)), dma, dma((2,)), dma((2,)),
+        ],
         compiler_params=pltpu.CompilerParams(vmem_limit_bytes=DOWN_MIB * 2**20),
         cost_estimate=pl.CostEstimate(flops=2 * ROWS * D * FL, bytes_accessed=24 * 2**20, transcendentals=0),
         name="down_grad",
-    )(placed(hidden, pltpu.VMEM), placed(dy, pltpu.HBM), placed(block, pltpu.VMEM), *parts)
+    )(
+        placed(hidden, pltpu.VMEM), placed(dy, pltpu.HBM), placed(block, pltpu.VMEM), placed(first, pltpu.VMEM),
+        *parts,
+    )
 
 
 def write_kernel(spots, *refs):
@@ -441,15 +536,15 @@
         second = send(shard, SECOND)
         own_twin = send(shard, SIBLING)
         both_a = send(first_a, SECOND)
-        both_b, both_c = send(first_b[:U], SECOND), send(first_b[U:], SECOND)
+        both_b, both_c = send(first_b[: M - TAIL], SECOND), send(first_b[M - TAIL :], SECOND)
         first_a_twin, first_b_twin = send(first_a, SIBLING), send(first_b, SIBLING)
         second_twin = send(second, SIBLING)
         both_a_twin, both_b_twin = send(both_a, SIBLING), send(both_b, SIBLING)
         both_c_twin = send(both_c, SIBLING)
-        wide = wide_grads(x, d_gate, d_up, 0, 3)
-        dw_gate, dw_up = wide_grads(x, d_gate, d_up, 3, 3, wide)
+        *wide, ahead = wide_grads(x, d_gate, d_up, 0, 3, x, 3)
+        dw_gate, dw_up, ahead = wide_grads(x, d_gate, d_up, 3, 3, dy, EARLY // BN, ahead, wide)
         dw_down, dx = down_grad(
-            hidden, dy, block, (shard, own_twin, first_a, first_b, second),
+            hidden, dy, block, ahead, (shard, own_twin, first_a, first_b, second),
             ((0, 0, 0, 0, 2 * M), (1, 0, 0, 0, 2 * M), (0, 1, 0, 0, M), (0, 1, 0, M, M), (0, 0, 1, 0, 2 * M)),
         )
         dx = write(
@@ -457,10 +552,12 @@
             ((1, 1, 0, 0, M), (1, 1, 0, M, M), (1, 0, 1, 0, 2 * M), (0, 1, 1, 0, M)),
             dx,
         )
+        dx = write((both_a_twin, both_b), ((1, 1, 1, 0, M), (0, 1, 1, M, M - TAIL)), dx)
         dx = write(
-            (both_a_twin, both_b, both_c), ((1, 1, 1, 0, M), (0, 1, 1, M, U), (0, 1, 1, M + U, U)), dx
+            (both_b_twin, both_c, both_c_twin),
+            ((1, 1, 1, M, M - TAIL), (0, 1, 1, 2 * M - TAIL, TAIL), (1, 1, 1, 2 * M - TAIL, TAIL)),
+            dx,
         )
-        dx = write((both_b_twin, both_c_twin), ((1, 1, 1, M, U), (1, 1, 1, M + U, U)), dx)
         return dx, dw_gate, dw_up, dw_down
 
     tokens, columns, rows = P("dp", None), P(None, "tp"), P("tp", None)

time: 140 us -> 137 us (0.979)
  waiting for transfers between devices: 18.4 us -> 16.5 us
    ppermute x13, waiting for transfers between devices: 18.4 us -> 16.5 us  [send(): return lax.ppermute(value, 'tp', perm)]
  transfers between devices with their start and end apart: 13 -> 13, of which waited for: 2 -> 2; matrix products, arithmetic and copies ran while one was open for 0% -> 0% of each run, Pallas kernels for 33% -> 32%
where the time goes in v6:
time: 137 us; the launch traced here: 136 us
  Pallas kernels  110 us (80%)
  waiting for transfers between devices  16.5 us (12%)
  starting transfers between devices  9.34 us (7%)
    pallas_call x1, Pallas kernels, scatter(): pl.pallas_call(scatter_kernel, out_shape=(pltpu.VMEM((2 * M, HALF), BF16)...  64.3 us
    pallas_call x2, Pallas kernels, wide_grads(): pl.pallas_call(functools.partial(wide_kernel, start, after, bool(given)),...  31.8 us
    ppermute x13, waiting for transfers between devices, send(): return lax.ppermute(value, 'tp', perm)  16.5 us
    ppermute x13, starting transfers between devices, send(): return lax.ppermute(value, 'tp', perm)  9.34 us
    pallas_call x1, Pallas kernels, down_grad(): pl.pallas_call(functools.partial(down_kernel, spots), grid=(LATE,), out_s...  9.24 us
    pallas_call x3, Pallas kernels, write(): pl.pallas_call(functools.partial(write_kernel, spots), out_shape=jax.Shap...  4.31 us
  transfers between devices with their start and end apart: 13, of which 2 were waited for; matrix products, arithmetic and copies ran while one was open for 0% of the time, Pallas kernels for 32%

profile of v6, /device:TPU:0, one launch (start us, length us, event | category | flops | bytes accessed | tf_op | source)
XLA Modules:
  0.0 136.4 jit_solution(4897413814023543410)
XLA Ops:
  0.6 64.3 %scatter.1 = (bf16[512,1536]{1,0:T(8,128)(2,1)S(1)}, bf16[256,1536]{1,0:T(8,128)(2,1)}, bf16[256,1536]{1,0:T(8,128)(2,1)S(1)}, bf16[2048,1024]{1,0:T(8,128)(2,1)...) custom-call(bf16[2048,3072]{1,0:T(8,128)(2,1)} %dy.3, ...), custom_call_target="tpu_custom_call" | custom-call | flops 38654705664 | bytes 62914560 | tf_op jit(solution)/shard_map/scatter/pallas_call | solution.py:327
  64.9 1.8 %collective-permute-start = (bf16[256,1536]{1,0:T(8,128)(2,1)S(1)}, bf16[256,1536]{1,0:T(8,128)(2,1)S(1)}, u32[]{:S(2)}, u32[]{:S(2)}) collective-permute-start(bf16[256,1536]{1,0:T(8,128)(2,1)S(1)} %get-tuple-element.19), channel_id=1, source_target_pairs={{0,2},{1,5},{2,0},{3,7},{4,6},{5,1},{6,4},{7,3}} | collective-permute-start | bytes 2359304 | tf_op jit(solution)/shard_map/ppermute | solution.py:531
  66.7 1.5 %collective-permute-start.10 = (bf16[512,1536]{1,0:T(8,128)(2,1)S(1)}, bf16[512,1536]{1,0:T(8,128)(2,1)S(1)}, u32[]{:S(2)}, u32[]{:S(2)}) collective-permute-start(bf16[512,1536]{1,0:T(8,128)(2,1)S(1)} %get-tuple-element.21.refs_0_), channel_id=1, source_target_pairs={{0,4},{1,3},{2,6},{3,1},{4,0},{5,7},{6,2},{7,5}} | collective-permute-start | bytes 4718600 | tf_op jit(solution)/shard_map/ppermute | solution.py:531
  68.2 0.0 collective-permute-start.12
  68.2 0.5 collective-permute-start.5
  68.7 16.0 %collective-permute-done.refs_3_ = bf16[256,1536]{1,0:T(8,128)(2,1)S(1)} collective-permute-done((bf16[256,1536]{1,0:T(8,128)(2,1)S(1)}, bf16[256,1536]{1,0:T(8,128)(2,1)S(1)}, u32[]{:S(2)}, u32[]{:S(2)}) %collective-permute-start) | collective-permute-done | bytes 786464 | tf_op jit(solution)/shard_map/ppermute | solution.py:531
  84.7 2.4 %collective-permute-start.3 = (bf16[64,1536]{1,0:T(8,128)(2,1)S(1)}, bf16[64,1536]{1,0:T(8,128)(2,1)S(1)}, u32[]{:S(2)}, u32[]{:S(2)}) collective-permute-start(bf16[64,1536]{1,0:T(8,128)(2,1)S(1)} %slice.9), channel_id=1, source_target_pairs={{0,4},{1,3},{2,6},{3,1},{4,0},{5,7},{6,2},{7,5}} | collective-permute-start | bytes 589832 | tf_op jit(solution)/shard_map/ppermute | solution.py:531
  87.2 16.6 %wide_grads.2 = (bf16[3072,1024]{1,0:T(8,128)(2,1)}, bf16[3072,1024]{1,0:T(8,128)(2,1)}, bf16[2048,512]{1,0:T(8,128)(2,1)S(1)}) custom-call(bf16[2048,3072]{1,0:T(8,128)(2,1)} %x.3, bf16[2048,1024]{1,0:T(8,128)(2,1)S(1)} %get-tuple-element.24.d_gate, bf16[2048,1024]{1,0:T(8,128)(2,1)S(1)} %get-tuple-element.25.d_up, bf16[2048,3072]{1,0:T(8,128)(2,1)} %x.3), custom_call_target="tpu_custom_call" | custom-call | flops 12884901888 | bytes 20971520 | tf_op jit(solution)/shard_map/wide_grads/pallas_call | solution.py:416
  103.8 0.1 collective-permute-start.1
  103.8 0.0 collective-permute-done.5.refs_2_
  103.8 0.0 collective-permute-start.9
  103.8 0.0 collective-permute-done.3.refs_1_
  103.9 2.0 %collective-permute-start.6 = (bf16[256,1536]{1,0:T(8,128)(2,1)S(1)}, bf16[256,1536]{1,0:T(8,128)(2,1)S(1)}, u32[]{:S(2)}, u32[]{:S(2)}) collective-permute-start(bf16[256,1536]{1,0:T(8,128)(2,1)S(1)} %collective-permute-done.5.refs_2_), channel_id=1, source_target_pairs={{0,4},{1,3},{2,6},{3,1},{4,0},{5,7},{6,2},{7,5}} | collective-permute-start | bytes 2359304 | tf_op jit(solution)/shard_map/ppermute | solution.py:531
  105.8 0.0 collective-permute-done.10.refs_4_
  105.8 0.0 collective-permute-start.11
  105.8 15.2 %wide_grads.3 = (bf16[3072,1024]{1,0:T(8,128)(2,1)}, bf16[3072,1024]{1,0:T(8,128)(2,1)}, bf16[2048,512]{1,0:T(8,128)(2,1)S(1)}) custom-call(bf16[2048,3072]{1,0:T(8,128)(2,1)} %x.3, bf16[2048,1024]{1,0:T(8,128)(2,1)S(1)} %get-tuple-element.24.d_gate, bf16[2048,1024]{1,0:T(8,128)(2,1)S(1)} %get-tuple-element.25.d_up, ...), custom_call_target="tpu_custom_call", output_to_operand_aliasing={{0}: (5, {}), {1}: (6, {})} | custom-call | flops 12884901888 | bytes 20971520 | tf_op jit(solution)/shard_map/wide_grads/pallas_call | solution.py:416
  121.1 0.0 collective-permute-done.1.refs_1_
  121.1 0.3 collective-permute-start.8
  121.4 0.0 collective-permute-done.12.refs_1_
  121.4 0.3 collective-permute-start.4
  121.6 0.5 collective-permute-done.6.refs_3_
  122.1 0.0 collective-permute-start.2
  122.1 0.0 collective-permute-done.9.refs_1_
  122.1 0.5 collective-permute-start.7
  122.6 9.2 %down_grad.1 = (bf16[1024,3072]{1,0:T(8,128)(2,1)}, bf16[2048,3072]{1,0:T(8,128)(2,1)}) custom-call(bf16[2048,1024]{1,0:T(8,128)(2,1)S(1)} %get-tuple-element.22.hidden, bf16[2048,3072]{1,0:T(8,128)(2,1)} %dy.3, bf16[1024,1536]{1,0:T(8,128)(2,1)S(1)} %get-tuple-element.23.block, bf16[2048,512]{1,0:T(8,128)(2,1)S(1)} %get-tuple-element.29.first, ...), custom_call_target="tpu_custom_call" | custom-call | flops 12884901888 | bytes 25165824 | tf_op jit(solution)/shard_map/down_grad/pallas_call | solution.py:473
  131.9 0.0 collective-permute-done.8.refs_0_
  131.9 0.0 collective-permute-done.11.refs_2_
  131.9 2.1 %write.3.refs_2_ = bf16[2048,3072]{1,0:T(8,128)(2,1)} custom-call(bf16[256,1536]{1,0:T(8,128)(2,1)S(1)} %collective-permute-done.8.refs_0_, bf16[256,1536]{1,0:T(8,128)(2,1)S(1)} %collective-permute-done.9.refs_1_, bf16[512,1536]{1,0:T(8,128)(2,1)S(1)} %collective-permute-done.11.refs_2_, ...), custom_call_target="tpu_custom_call", output_to_operand_aliasing={{}: (4, {})} | custom-call | flops 1000000000 | bytes 25165824 | tf_op jit(solution)/shard_map/write/pallas_call | solution.py:503
  134.0 0.0 collective-permute-done.7.refs_0_
  134.0 1.2 write.4.refs_3_
  135.1 0.0 collective-permute-done.4.refs_2_
  135.2 0.0 collective-permute-done.2.refs_0_
  135.2 1.1 write.5
  (2 shorter events, 0.1 us)
Async XLA Ops:
  64.9 19.8 %collective-permute-start = (bf16[256,1536]{1,0:T(8,128)(2,1)S(1)}, bf16[256,1536]{1,0:T(8,128)(2,1)S(1)}, u32[]{:S(2)}, u32[]{:S(2)}) collective-permute-start(bf16[256,1536]{1,0:T(8,128)(2,1)S(1)} %get-tuple-element.19), channel_id=1, source_target_pairs={{0,2},{1,5},{2,0},{3,7},{4,6},{5,1},{6,4},{7,3}} | collective-permute-start | bytes 2359304 | tf_op jit(solution)/shard_map/ppermute | solution.py:531
  66.7 39.1 %collective-permute-start.10 = (bf16[512,1536]{1,0:T(8,128)(2,1)S(1)}, bf16[512,1536]{1,0:T(8,128)(2,1)S(1)}, u32[]{:S(2)}, u32[]{:S(2)}) collective-permute-start(bf16[512,1536]{1,0:T(8,128)(2,1)S(1)} %get-tuple-element.21.refs_0_), channel_id=1, source_target_pairs={{0,4},{1,3},{2,6},{3,1},{4,0},{5,7},{6,2},{7,5}} | collective-permute-start | bytes 4718600 | tf_op jit(solution)/shard_map/ppermute | solution.py:531
  68.2 53.2 %collective-permute-start.12 = (bf16[512,1536]{1,0:T(8,128)(2,1)S(1)}, bf16[512,1536]{1,0:T(8,128)(2,1)S(1)}, u32[]{:S(2)}, u32[]{:S(2)}) collective-permute-start(bf16[512,1536]{1,0:T(8,128)(2,1)S(1)} %get-tuple-element.21.refs_0_), channel_id=1, source_target_pairs={{0,1},{1,0},{2,3},{3,2},{4,5},{5,4},{6,7},{7,6}} | collective-permute-start | bytes 4718600 | tf_op jit(solution)/shard_map/ppermute | solution.py:531
  68.2 35.6 %collective-permute-start.5 = (bf16[256,1536]{1,0:T(8,128)(2,1)}, bf16[256,1536]{1,0:T(8,128)(2,1)S(1)}, u32[]{:S(2)}, u32[]{:S(2)}) collective-permute-start(bf16[256,1536]{1,0:T(8,128)(2,1)} %get-tuple-element.20), channel_id=1, source_target_pairs={{0,2},{1,5},{2,0},{3,7},{4,6},{5,1},{6,4},{7,3}} | collective-permute-start | bytes 2359304 | tf_op jit(solution)/shard_map/ppermute | solution.py:531
  84.7 19.1 %collective-permute-start.3 = (bf16[64,1536]{1,0:T(8,128)(2,1)S(1)}, bf16[64,1536]{1,0:T(8,128)(2,1)S(1)}, u32[]{:S(2)}, u32[]{:S(2)}) collective-permute-start(bf16[64,1536]{1,0:T(8,128)(2,1)S(1)} %slice.9), channel_id=1, source_target_pairs={{0,4},{1,3},{2,6},{3,1},{4,0},{5,7},{6,2},{7,5}} | collective-permute-start | bytes 589832 | tf_op jit(solution)/shard_map/ppermute | solution.py:531
  103.8 17.3 %collective-permute-start.1 = (bf16[192,1536]{1,0:T(8,128)(2,1)S(1)}, bf16[192,1536]{1,0:T(8,128)(2,1)S(1)}, u32[]{:S(2)}, u32[]{:S(2)}) collective-permute-start(bf16[192,1536]{1,0:T(8,128)(2,1)S(1)} %slice.8), channel_id=1, source_target_pairs={{0,4},{1,3},{2,6},{3,1},{4,0},{5,7},{6,2},{7,5}} | collective-permute-start | bytes 1769480 | tf_op jit(solution)/shard_map/ppermute | solution.py:531
  103.8 18.3 %collective-permute-start.9 = (bf16[256,1536]{1,0:T(8,128)(2,1)S(1)}, bf16[256,1536]{1,0:T(8,128)(2,1)S(1)}, u32[]{:S(2)}, u32[]{:S(2)}) collective-permute-start(bf16[256,1536]{1,0:T(8,128)(2,1)S(1)} %collective-permute-done.refs_3_), channel_id=1, source_target_pairs={{0,1},{1,0},{2,3},{3,2},{4,5},{5,4},{6,7},{7,6}} | collective-permute-start | bytes 2359304 | tf_op jit(solution)/shard_map/ppermute | solution.py:531
  103.9 18.2 %collective-permute-start.6 = (bf16[256,1536]{1,0:T(8,128)(2,1)S(1)}, bf16[256,1536]{1,0:T(8,128)(2,1)S(1)}, u32[]{:S(2)}, u32[]{:S(2)}) collective-permute-start(bf16[256,1536]{1,0:T(8,128)(2,1)S(1)} %collective-permute-done.5.refs_2_), channel_id=1, source_target_pairs={{0,4},{1,3},{2,6},{3,1},{4,0},{5,7},{6,2},{7,5}} | collective-permute-start | bytes 2359304 | tf_op jit(solution)/shard_map/ppermute | solution.py:531
  105.8 26.0 %collective-permute-start.11 = (bf16[512,1536]{1,0:T(8,128)(2,1)S(1)}, bf16[512,1536]{1,0:T(8,128)(2,1)S(1)}, u32[]{:S(2)}, u32[]{:S(2)}) collective-permute-start(bf16[512,1536]{1,0:T(8,128)(2,1)S(1)} %collective-permute-done.10.refs_4_), channel_id=1, source_target_pairs={{0,1},{1,0},{2,3},{3,2},{4,5},{5,4},{6,7},{7,6}} | collective-permute-start | bytes 4718600 | tf_op jit(solution)/shard_map/ppermute | solution.py:531
  121.1 10.8 %collective-permute-start.8 = (bf16[256,1536]{1,0:T(8,128)(2,1)S(1)}, bf16[256,1536]{1,0:T(8,128)(2,1)S(1)}, u32[]{:S(2)}, u32[]{:S(2)}) collective-permute-start(bf16[256,1536]{1,0:T(8,128)(2,1)S(1)} %collective-permute-done.5.refs_2_), channel_id=1, source_target_pairs={{0,1},{1,0},{2,3},{3,2},{4,5},{5,4},{6,7},{7,6}} | collective-permute-start | bytes 2359304 | tf_op jit(solution)/shard_map/ppermute | solution.py:531
  121.4 13.8 %collective-permute-start.4 = (bf16[64,1536]{1,0:T(8,128)(2,1)S(1)}, bf16[64,1536]{1,0:T(8,128)(2,1)S(1)}, u32[]{:S(2)}, u32[]{:S(2)}) collective-permute-start(bf16[64,1536]{1,0:T(8,128)(2,1)S(1)} %collective-permute-done.3.refs_1_), channel_id=1, source_target_pairs={{0,1},{1,0},{2,3},{3,2},{4,5},{5,4},{6,7},{7,6}} | collective-permute-start | bytes 589832 | tf_op jit(solution)/shard_map/ppermute | solution.py:531
  122.1 13.1 %collective-permute-start.2 = (bf16[192,1536]{1,0:T(8,128)(2,1)S(1)}, bf16[192,1536]{1,0:T(8,128)(2,1)S(1)}, u32[]{:S(2)}, u32[]{:S(2)}) collective-permute-start(bf16[192,1536]{1,0:T(8,128)(2,1)S(1)} %collective-permute-done.1.refs_1_), channel_id=1, source_target_pairs={{0,1},{1,0},{2,3},{3,2},{4,5},{5,4},{6,7},{7,6}} | collective-permute-start | bytes 1769480 | tf_op jit(solution)/shard_map/ppermute | solution.py:531
  122.1 11.9 %collective-permute-start.7 = (bf16[256,1536]{1,0:T(8,128)(2,1)S(1)}, bf16[256,1536]{1,0:T(8,128)(2,1)S(1)}, u32[]{:S(2)}, u32[]{:S(2)}) collective-permute-start(bf16[256,1536]{1,0:T(8,128)(2,1)S(1)} %collective-permute-done.6.refs_3_), channel_id=1, source_target_pairs={{0,1},{1,0},{2,3},{3,2},{4,5},{5,4},{6,7},{7,6}} | collective-permute-start | bytes 2359304 | tf_op jit(solution)/shard_map/ppermute | solution.py:531

commit v7 on v6

--- a/solution.py
+++ b/solution.py
@@ -121,10 +121,13 @@
         return remote(sib_out.at[p % 2, j], sib_in.at[p % 2, j], sib_s.at[p % 2, j], sib_r.at[p % 2, j], sibling)
 
     def to_first(k, j):
-        return remote(one_out.at[k, j], one_in.at[k, j], one_s, one_r.at[k, j], first)
+        return remote(one_out.at[k, j], one_in.at[k, j], one_s, one_r.at[k], first)
+
+    def unit_here(into, sems, k):
+        pltpu.make_async_copy(into.at[k], into.at[k], sems.at[k]).wait()
 
     def to_second(k, j):
-        return remote(two_out.at[k, j], two_in.at[k, j], two_s, two_r.at[k, j], second)
+        return remote(two_out.at[k, j], two_in.at[k, j], two_s, two_r.at[k], second)
 
     for c in inputs(0, 0) + down[:2]:
         c.start()
@@ -177,8 +180,8 @@
             to_sibling(p, j).wait_recv()
             one_out[4 + q, j] = chip_sum(p, j, core).astype(BF16)
             to_first(4 + q, j).start()
-        for j in range(PIECES):
-            to_first(q, j).wait_recv()
+        unit_here(one_in, one_r, q)
+        for j in range(PIECES):
             two_out[q, j] = (chip_sum(p, j, 1 - core) + one_in[q, j].astype(F32)).astype(BF16)
             to_second(q, j).start()
 
@@ -232,7 +235,7 @@
                 total = acc[0, h, :, halves[i]] + sib_in[0, 0, h, :, halves[i]].astype(F32)
                 one_out[h, 0, :, halves[i]] = total.astype(BF16)
                 a, b = one_out.at[h, 0, :, halves[i]], one_in.at[h, 0, :, halves[i]]
-                remote(a, b, one_s, one_r.at[h, 0], first).start()
+                remote(a, b, one_s, one_r.at[h], first).start()
             if i == 0:
                 arrived(0, 1)
                 for_sibling(0, (1,))
@@ -274,7 +277,7 @@
         for n in range(FL // 256):
             hidden_grads(p, slot, n)
 
-        @pl.when(jnp.logical_and(p >= 4, p < 7))
+        @pl.when(jnp.logical_and(p >= 5, p < 7))
         def _():
             send_middle(p - 1)
 
@@ -290,9 +293,9 @@
         for j in range(PIECES):
             acc[j] = term(own_col, j)
 
-        @pl.when(p == 2)
-        def _():
-            send_middle(2)
+        @pl.when(p < 4)
+        def _():
+            send_middle(p)
 
         return carry
 
@@ -306,17 +309,17 @@
         block[:, pl.ds(n, 256)] = turned(hidden[...], right).astype(BF16)
 
     for q in range(4):
-        for j in range(PIECES):
-            to_first(4 + q, j).wait_recv()
-            to_second(q, j).wait_recv()
+        unit_here(one_in, one_r, 4 + q)
+        unit_here(two_in, two_r, q)
+        for j in range(PIECES):
             total = sum_own[q, j] + one_in[4 + q, j].astype(F32) + two_in[q, j].astype(F32)
             for to, row in ((upper, lower)[q // 2], q % 2), (shard, q):
                 to[pl.ds(row * U, U), pl.ds(j * W, W)] = total.astype(BF16)
     for p in (STEPS - 2, STEPS - 1):
         for j in range(PIECES):
             to_sibling(p, j).wait_send()
-    remote(one_out, one_in, one_s, one_r.at[0, 0], first).wait_send()
-    remote(two_out, two_in, two_s, two_r.at[0, 0], second).wait_send()
+    remote(one_out, one_in, one_s, one_r.at[0], first).wait_send()
+    remote(two_out, two_in, two_s, two_r.at[0], second).wait_send()
 
 
 def scatter(dy, gate, up, w_gate, w_up, w_down):
@@ -335,7 +338,7 @@
             pltpu.VMEM((PIECES, 2, U, W), F32), pltpu.VMEM((4, PIECES, U, W), F32),
             twin, twin, units(8), units(8), units(4), units(4),
             dma((FL // 256,)), dma((2, PIECES)), dma((2,)), dma((2,)),
-            dma((2, PIECES)), dma((2, PIECES)), dma, dma((8, PIECES)), dma, dma((4, PIECES)),
+            dma((2, PIECES)), dma((2, PIECES)), dma, dma((8,)), dma, dma((4,)),
         ],
         compiler_params=pltpu.CompilerParams(
             collective_id=0, has_side_effects=True, vmem_limit_bytes=SCATTER_MIB * 2**20
@@ -553,11 +556,8 @@
             dx,
         )
         dx = write((both_a_twin, both_b), ((1, 1, 1, 0, M), (0, 1, 1, M, M - TAIL)), dx)
-        dx = write(
-            (both_b_twin, both_c, both_c_twin),
-            ((1, 1, 1, M, M - TAIL), (0, 1, 1, 2 * M - TAIL, TAIL), (1, 1, 1, 2 * M - TAIL, TAIL)),
-            dx,
-        )
+        dx = write((both_b_twin, both_c), ((1, 1, 1, M, M - TAIL), (0, 1, 1, 2 * M - TAIL, TAIL)), dx)
+        dx = write((both_c_twin,), ((1, 1, 1, 2 * M - TAIL, TAIL),), dx)
         return dx, dw_gate, dw_up, dw_down
 
     tokens, columns, rows = P("dp", None), P(None, "tp"), P("tp", None)

time: 137 us -> 137 us (level)
    pallas_call x3 -> x4, Pallas kernels: 4.31 us -> 4.92 us  [write(): pl.pallas_call(functools.partial(write_kernel, spots), out_shape=jax.Shap...]
  transfers between devices with their start and end apart: 13 -> 13, of which waited for: 2 -> 2; matrix products, arithmetic and copies ran while one was open for 0% -> 0% of each run, Pallas kernels for 32% -> 33%
where the time goes in v7:
time: 137 us; the launch traced here: 136 us
  Pallas kernels  110 us (80%)
  waiting for transfers between devices  16.6 us (12%)
  starting transfers between devices  8.68 us (6%)
    pallas_call x1, Pallas kernels, scatter(): pl.pallas_call(scatter_kernel, out_shape=(pltpu.VMEM((2 * M, HALF), BF16)...  64.1 us
    pallas_call x2, Pallas kernels, wide_grads(): pl.pallas_call(functools.partial(wide_kernel, start, after, bool(given)),...  31.8 us
    ppermute x13, waiting for transfers between devices, send(): return lax.ppermute(value, 'tp', perm)  16.6 us
    pallas_call x1, Pallas kernels, down_grad(): pl.pallas_call(functools.partial(down_kernel, spots), grid=(LATE,), out_s...  9.24 us
    ppermute x13, starting transfers between devices, send(): return lax.ppermute(value, 'tp', perm)  8.68 us
    pallas_call x4, Pallas kernels, write(): pl.pallas_call(functools.partial(write_kernel, spots), out_shape=jax.Shap...  4.92 us
  transfers between devices with their start and end apart: 13, of which 2 were waited for; matrix products, arithmetic and copies ran while one was open for 0% of the time, Pallas kernels for 33%

profile of v7, /device:TPU:0, one launch (start us, length us, event | category | flops | bytes accessed | tf_op | source)
XLA Modules:
  0.0 136.3 jit_solution(3700157278703519098)
XLA Ops:
  0.6 64.1 %scatter.1 = (bf16[512,1536]{1,0:T(8,128)(2,1)S(1)}, bf16[256,1536]{1,0:T(8,128)(2,1)}, bf16[256,1536]{1,0:T(8,128)(2,1)S(1)}, bf16[2048,1024]{1,0:T(8,128)(2,1)...) custom-call(bf16[2048,3072]{1,0:T(8,128)(2,1)} %dy.3, ...), custom_call_target="tpu_custom_call" | custom-call | flops 38654705664 | bytes 62914560 | tf_op jit(solution)/shard_map/scatter/pallas_call | solution.py:330
  64.8 1.6 %collective-permute-start.10 = (bf16[512,1536]{1,0:T(8,128)(2,1)S(1)}, bf16[512,1536]{1,0:T(8,128)(2,1)S(1)}, u32[]{:S(2)}, u32[]{:S(2)}) collective-permute-start(bf16[512,1536]{1,0:T(8,128)(2,1)S(1)} %get-tuple-element.21.refs_0_), channel_id=1, source_target_pairs={{0,4},{1,3},{2,6},{3,1},{4,0},{5,7},{6,2},{7,5}} | collective-permute-start | bytes 4718600 | tf_op jit(solution)/shard_map/ppermute | solution.py:534
  66.4 0.1 collective-permute-start.12
  66.5 1.4 %collective-permute-start = (bf16[256,1536]{1,0:T(8,128)(2,1)S(1)}, bf16[256,1536]{1,0:T(8,128)(2,1)S(1)}, u32[]{:S(2)}, u32[]{:S(2)}) collective-permute-start(bf16[256,1536]{1,0:T(8,128)(2,1)S(1)} %get-tuple-element.19), channel_id=1, source_target_pairs={{0,2},{1,5},{2,0},{3,7},{4,6},{5,1},{6,4},{7,3}} | collective-permute-start | bytes 2359304 | tf_op jit(solution)/shard_map/ppermute | solution.py:534
  68.0 0.6 collective-permute-start.5
  68.6 16.6 %wide_grads.2 = (bf16[3072,1024]{1,0:T(8,128)(2,1)}, bf16[3072,1024]{1,0:T(8,128)(2,1)}, bf16[2048,512]{1,0:T(8,128)(2,1)S(1)}) custom-call(bf16[2048,3072]{1,0:T(8,128)(2,1)} %x.3, bf16[2048,1024]{1,0:T(8,128)(2,1)S(1)} %get-tuple-element.24.d_gate, bf16[2048,1024]{1,0:T(8,128)(2,1)S(1)} %get-tuple-element.25.d_up, bf16[2048,3072]{1,0:T(8,128)(2,1)} %x.3), custom_call_target="tpu_custom_call" | custom-call | flops 12884901888 | bytes 20971520 | tf_op jit(solution)/shard_map/wide_grads/pallas_call | solution.py:419
  85.1 1.8 %collective-permute-done.refs_3_ = bf16[256,1536]{1,0:T(8,128)(2,1)S(1)} collective-permute-done((bf16[256,1536]{1,0:T(8,128)(2,1)S(1)}, bf16[256,1536]{1,0:T(8,128)(2,1)S(1)}, u32[]{:S(2)}, u32[]{:S(2)}) %collective-permute-start) | collective-permute-done | bytes 786464 | tf_op jit(solution)/shard_map/ppermute | solution.py:534
  87.0 1.5 %collective-permute-start.3 = (bf16[192,1536]{1,0:T(8,128)(2,1)S(1)}, bf16[192,1536]{1,0:T(8,128)(2,1)S(1)}, u32[]{:S(2)}, u32[]{:S(2)}) collective-permute-start(bf16[192,1536]{1,0:T(8,128)(2,1)S(1)} %slice.9), channel_id=1, source_target_pairs={{0,4},{1,3},{2,6},{3,1},{4,0},{5,7},{6,2},{7,5}} | collective-permute-start | bytes 1769480 | tf_op jit(solution)/shard_map/ppermute | solution.py:534
  88.5 0.6 collective-permute-start.1
  89.1 14.7 %collective-permute-done.5.refs_2_ = bf16[256,1536]{1,0:T(8,128)(2,1)S(1)} collective-permute-done((bf16[256,1536]{1,0:T(8,128)(2,1)}, bf16[256,1536]{1,0:T(8,128)(2,1)S(1)}, u32[]{:S(2)}, u32[]{:S(2)}) %collective-permute-start.5) | collective-permute-done | bytes 786464 | tf_op jit(solution)/shard_map/ppermute | solution.py:534
  103.8 1.5 %collective-permute-start.6 = (bf16[256,1536]{1,0:T(8,128)(2,1)S(1)}, bf16[256,1536]{1,0:T(8,128)(2,1)S(1)}, u32[]{:S(2)}, u32[]{:S(2)}) collective-permute-start(bf16[256,1536]{1,0:T(8,128)(2,1)S(1)} %collective-permute-done.5.refs_2_), channel_id=1, source_target_pairs={{0,4},{1,3},{2,6},{3,1},{4,0},{5,7},{6,2},{7,5}} | collective-permute-start | bytes 2359304 | tf_op jit(solution)/shard_map/ppermute | solution.py:534
  105.3 0.0 collective-permute-done.10.refs_4_
  105.3 0.0 collective-permute-start.11
  105.3 15.2 %wide_grads.3 = (bf16[3072,1024]{1,0:T(8,128)(2,1)}, bf16[3072,1024]{1,0:T(8,128)(2,1)}, bf16[2048,512]{1,0:T(8,128)(2,1)S(1)}) custom-call(bf16[2048,3072]{1,0:T(8,128)(2,1)} %x.3, bf16[2048,1024]{1,0:T(8,128)(2,1)S(1)} %get-tuple-element.24.d_gate, bf16[2048,1024]{1,0:T(8,128)(2,1)S(1)} %get-tuple-element.25.d_up, ...), custom_call_target="tpu_custom_call", output_to_operand_aliasing={{0}: (5, {}), {1}: (6, {})} | custom-call | flops 12884901888 | bytes 20971520 | tf_op jit(solution)/shard_map/wide_grads/pallas_call | solution.py:419
  120.6 0.0 collective-permute-done.1.refs_1_
  120.6 0.3 collective-permute-start.9
  120.9 0.0 collective-permute-done.3.refs_1_
  120.9 0.3 collective-permute-start.8
  121.1 0.0 collective-permute-done.12.refs_1_
  121.1 0.3 collective-permute-start.4
  121.4 0.0 collective-permute-done.6.refs_3_
  121.4 0.3 collective-permute-start.7
  121.6 9.2 %down_grad.1 = (bf16[1024,3072]{1,0:T(8,128)(2,1)}, bf16[2048,3072]{1,0:T(8,128)(2,1)}) custom-call(bf16[2048,1024]{1,0:T(8,128)(2,1)S(1)} %get-tuple-element.22.hidden, bf16[2048,3072]{1,0:T(8,128)(2,1)} %dy.3, bf16[1024,1536]{1,0:T(8,128)(2,1)S(1)} %get-tuple-element.23.block, bf16[2048,512]{1,0:T(8,128)(2,1)S(1)} %get-tuple-element.29.first, ...), custom_call_target="tpu_custom_call" | custom-call | flops 12884901888 | bytes 25165824 | tf_op jit(solution)/shard_map/down_grad/pallas_call | solution.py:476
  130.9 0.0 collective-permute-done.9.refs_1_
  130.9 0.3 collective-permute-start.2
  131.2 0.0 collective-permute-done.8.refs_0_
  131.2 0.0 collective-permute-done.11.refs_2_
  131.2 2.0 %write.4.refs_2_ = bf16[2048,3072]{1,0:T(8,128)(2,1)} custom-call(bf16[256,1536]{1,0:T(8,128)(2,1)S(1)} %collective-permute-done.8.refs_0_, bf16[256,1536]{1,0:T(8,128)(2,1)S(1)} %collective-permute-done.9.refs_1_, bf16[512,1536]{1,0:T(8,128)(2,1)S(1)} %collective-permute-done.11.refs_2_, ...), custom_call_target="tpu_custom_call", output_to_operand_aliasing={{}: (4, {})} | custom-call | flops 1000000000 | bytes 25165824 | tf_op jit(solution)/shard_map/write/pallas_call | solution.py:506
  133.2 0.0 collective-permute-done.7.refs_0_
  133.2 1.2 write.5.refs_2_
  134.4 0.0 collective-permute-done.4.refs_0_
  134.4 1.0 write.6.refs_1_
  135.4 0.0 collective-permute-done.2.refs_0_
  135.4 0.7 write.7
  (2 shorter events, 0.1 us)
Async XLA Ops:
  64.8 40.5 %collective-permute-start.10 = (bf16[512,1536]{1,0:T(8,128)(2,1)S(1)}, bf16[512,1536]{1,0:T(8,128)(2,1)S(1)}, u32[]{:S(2)}, u32[]{:S(2)}) collective-permute-start(bf16[512,1536]{1,0:T(8,128)(2,1)S(1)} %get-tuple-element.21.refs_0_), channel_id=1, source_target_pairs={{0,4},{1,3},{2,6},{3,1},{4,0},{5,7},{6,2},{7,5}} | collective-permute-start | bytes 4718600 | tf_op jit(solution)/shard_map/ppermute | solution.py:534
  66.4 54.7 %collective-permute-start.12 = (bf16[512,1536]{1,0:T(8,128)(2,1)S(1)}, bf16[512,1536]{1,0:T(8,128)(2,1)S(1)}, u32[]{:S(2)}, u32[]{:S(2)}) collective-permute-start(bf16[512,1536]{1,0:T(8,128)(2,1)S(1)} %get-tuple-element.21.refs_0_), channel_id=1, source_target_pairs={{0,1},{1,0},{2,3},{3,2},{4,5},{5,4},{6,7},{7,6}} | collective-permute-start | bytes 4718600 | tf_op jit(solution)/shard_map/ppermute | solution.py:534
  66.5 20.4 %collective-permute-start = (bf16[256,1536]{1,0:T(8,128)(2,1)S(1)}, bf16[256,1536]{1,0:T(8,128)(2,1)S(1)}, u32[]{:S(2)}, u32[]{:S(2)}) collective-permute-start(bf16[256,1536]{1,0:T(8,128)(2,1)S(1)} %get-tuple-element.19), channel_id=1, source_target_pairs={{0,2},{1,5},{2,0},{3,7},{4,6},{5,1},{6,4},{7,3}} | collective-permute-start | bytes 2359304 | tf_op jit(solution)/shard_map/ppermute | solution.py:534
  68.0 35.9 %collective-permute-start.5 = (bf16[256,1536]{1,0:T(8,128)(2,1)}, bf16[256,1536]{1,0:T(8,128)(2,1)S(1)}, u32[]{:S(2)}, u32[]{:S(2)}) collective-permute-start(bf16[256,1536]{1,0:T(8,128)(2,1)} %get-tuple-element.20), channel_id=1, source_target_pairs={{0,2},{1,5},{2,0},{3,7},{4,6},{5,1},{6,4},{7,3}} | collective-permute-start | bytes 2359304 | tf_op jit(solution)/shard_map/ppermute | solution.py:534
  87.0 33.8 %collective-permute-start.3 = (bf16[192,1536]{1,0:T(8,128)(2,1)S(1)}, bf16[192,1536]{1,0:T(8,128)(2,1)S(1)}, u32[]{:S(2)}, u32[]{:S(2)}) collective-permute-start(bf16[192,1536]{1,0:T(8,128)(2,1)S(1)} %slice.9), channel_id=1, source_target_pairs={{0,4},{1,3},{2,6},{3,1},{4,0},{5,7},{6,2},{7,5}} | collective-permute-start | bytes 1769480 | tf_op jit(solution)/shard_map/ppermute | solution.py:534
  88.5 32.0 %collective-permute-start.1 = (bf16[64,1536]{1,0:T(8,128)(2,1)S(1)}, bf16[64,1536]{1,0:T(8,128)(2,1)S(1)}, u32[]{:S(2)}, u32[]{:S(2)}) collective-permute-start(bf16[64,1536]{1,0:T(8,128)(2,1)S(1)} %slice.8), channel_id=1, source_target_pairs={{0,4},{1,3},{2,6},{3,1},{4,0},{5,7},{6,2},{7,5}} | collective-permute-start | bytes 589832 | tf_op jit(solution)/shard_map/ppermute | solution.py:534
  103.8 17.6 %collective-permute-start.6 = (bf16[256,1536]{1,0:T(8,128)(2,1)S(1)}, bf16[256,1536]{1,0:T(8,128)(2,1)S(1)}, u32[]{:S(2)}, u32[]{:S(2)}) collective-permute-start(bf16[256,1536]{1,0:T(8,128)(2,1)S(1)} %collective-permute-done.5.refs_2_), channel_id=1, source_target_pairs={{0,4},{1,3},{2,6},{3,1},{4,0},{5,7},{6,2},{7,5}} | collective-permute-start | bytes 2359304 | tf_op jit(solution)/shard_map/ppermute | solution.py:534
  105.3 25.9 %collective-permute-start.11 = (bf16[512,1536]{1,0:T(8,128)(2,1)S(1)}, bf16[512,1536]{1,0:T(8,128)(2,1)S(1)}, u32[]{:S(2)}, u32[]{:S(2)}) collective-permute-start(bf16[512,1536]{1,0:T(8,128)(2,1)S(1)} %collective-permute-done.10.refs_4_), channel_id=1, source_target_pairs={{0,1},{1,0},{2,3},{3,2},{4,5},{5,4},{6,7},{7,6}} | collective-permute-start | bytes 4718600 | tf_op jit(solution)/shard_map/ppermute | solution.py:534
  120.6 10.3 %collective-permute-start.9 = (bf16[256,1536]{1,0:T(8,128)(2,1)S(1)}, bf16[256,1536]{1,0:T(8,128)(2,1)S(1)}, u32[]{:S(2)}, u32[]{:S(2)}) collective-permute-start(bf16[256,1536]{1,0:T(8,128)(2,1)S(1)} %collective-permute-done.refs_3_), channel_id=1, source_target_pairs={{0,1},{1,0},{2,3},{3,2},{4,5},{5,4},{6,7},{7,6}} | collective-permute-start | bytes 2359304 | tf_op jit(solution)/shard_map/ppermute | solution.py:534
  120.9 10.3 %collective-permute-start.8 = (bf16[256,1536]{1,0:T(8,128)(2,1)S(1)}, bf16[256,1536]{1,0:T(8,128)(2,1)S(1)}, u32[]{:S(2)}, u32[]{:S(2)}) collective-permute-start(bf16[256,1536]{1,0:T(8,128)(2,1)S(1)} %collective-permute-done.5.refs_2_), channel_id=1, source_target_pairs={{0,1},{1,0},{2,3},{3,2},{4,5},{5,4},{6,7},{7,6}} | collective-permute-start | bytes 2359304 | tf_op jit(solution)/shard_map/ppermute | solution.py:534
  121.1 13.3 %collective-permute-start.4 = (bf16[192,1536]{1,0:T(8,128)(2,1)S(1)}, bf16[192,1536]{1,0:T(8,128)(2,1)S(1)}, u32[]{:S(2)}, u32[]{:S(2)}) collective-permute-start(bf16[192,1536]{1,0:T(8,128)(2,1)S(1)} %collective-permute-done.3.refs_1_), channel_id=1, source_target_pairs={{0,1},{1,0},{2,3},{3,2},{4,5},{5,4},{6,7},{7,6}} | collective-permute-start | bytes 1769480 | tf_op jit(solution)/shard_map/ppermute | solution.py:534
  121.4 11.9 %collective-permute-start.7 = (bf16[256,1536]{1,0:T(8,128)(2,1)S(1)}, bf16[256,1536]{1,0:T(8,128)(2,1)S(1)}, u32[]{:S(2)}, u32[]{:S(2)}) collective-permute-start(bf16[256,1536]{1,0:T(8,128)(2,1)S(1)} %collective-permute-done.6.refs_3_), channel_id=1, source_target_pairs={{0,1},{1,0},{2,3},{3,2},{4,5},{5,4},{6,7},{7,6}} | collective-permute-start | bytes 2359304 | tf_op jit(solution)/shard_map/ppermute | solution.py:534
  130.9 4.5 %collective-permute-start.2 = (bf16[64,1536]{1,0:T(8,128)(2,1)S(1)}, bf16[64,1536]{1,0:T(8,128)(2,1)S(1)}, u32[]{:S(2)}, u32[]{:S(2)}) collective-permute-start(bf16[64,1536]{1,0:T(8,128)(2,1)S(1)} %collective-permute-done.1.refs_1_), channel_id=1, source_target_pairs={{0,1},{1,0},{2,3},{3,2},{4,5},{5,4},{6,7},{7,6}} | collective-permute-start | bytes 589832 | tf_op jit(solution)/shard_map/ppermute | solution.py:534

commit v8 on v7

--- a/solution.py
+++ b/solution.py
@@ -118,10 +118,13 @@
         )
 
     def to_sibling(p, j):
-        return remote(sib_out.at[p % 2, j], sib_in.at[p % 2, j], sib_s.at[p % 2, j], sib_r.at[p % 2, j], sibling)
+        return remote(sib_out.at[p % 2, j], sib_in.at[p % 2, j], sib_s.at[p % 2], sib_r.at[p % 2, j], sibling)
 
     def to_first(k, j):
         return remote(one_out.at[k, j], one_in.at[k, j], one_s, one_r.at[k], first)
+
+    def sent(p):
+        remote(sib_out.at[p % 2], sib_in.at[p % 2], sib_s.at[p % 2], sib_r.at[0, 0], sibling).wait_send()
 
     def unit_here(into, sems, k):
         pltpu.make_async_copy(into.at[k], into.at[k], sems.at[k]).wait()
@@ -216,7 +219,7 @@
 
         def copy(i):
             a, b = sib_out.at[0, 0, :, :, halves[i]], sib_in.at[0, 0, :, :, halves[i]]
-            return remote(a, b, sib_s.at[0, 0], half_r.at[i], sibling)
+            return remote(a, b, sib_s.at[0], half_r.at[i], sibling)
 
         for i in range(2):
             for side, base in enumerate((sib_col, own_col)):
@@ -287,8 +290,7 @@
                 c.start()
             keep_own(6)
 
-        for j in range(PIECES):
-            to_sibling(p, j).wait_send()
+        sent(p)
         for_sibling(p, range(PIECES))
         for j in range(PIECES):
             acc[j] = term(own_col, j)
@@ -316,8 +318,7 @@
             for to, row in ((upper, lower)[q // 2], q % 2), (shard, q):
                 to[pl.ds(row * U, U), pl.ds(j * W, W)] = total.astype(BF16)
     for p in (STEPS - 2, STEPS - 1):
-        for j in range(PIECES):
-            to_sibling(p, j).wait_send()
+        sent(p)
     remote(one_out, one_in, one_s, one_r.at[0], first).wait_send()
     remote(two_out, two_in, two_s, two_r.at[0], second).wait_send()
 
@@ -338,7 +339,7 @@
             pltpu.VMEM((PIECES, 2, U, W), F32), pltpu.VMEM((4, PIECES, U, W), F32),
             twin, twin, units(8), units(8), units(4), units(4),
             dma((FL // 256,)), dma((2, PIECES)), dma((2,)), dma((2,)),
-            dma((2, PIECES)), dma((2, PIECES)), dma, dma((8,)), dma, dma((4,)),
+            dma((2,)), dma((2, PIECES)), dma, dma((8,)), dma, dma((4,)),
         ],
         compiler_params=pltpu.CompilerParams(
             collective_id=0, has_side_effects=True, vmem_limit_bytes=SCATTER_MIB * 2**20

time: 137 us -> 136 us (level)
  no operation moved by 1% of the time
where the time goes in v8:
time: 136 us
  Pallas kernels  110 us (81%)
  waiting for transfers between devices  16.6 us (12%)
  starting transfers between devices  8.64 us (6%)
    pallas_call x1, Pallas kernels, scatter(): pl.pallas_call(scatter_kernel, out_shape=(pltpu.VMEM((2 * M, HALF), BF16)...  64.1 us
    pallas_call x2, Pallas kernels, wide_grads(): pl.pallas_call(functools.partial(wide_kernel, start, after, bool(given)),...  31.8 us
    ppermute x13, waiting for transfers between devices, send(): return lax.ppermute(value, 'tp', perm)  16.6 us
    pallas_call x1, Pallas kernels, down_grad(): pl.pallas_call(functools.partial(down_kernel, spots), grid=(LATE,), out_s...  9.24 us
    ppermute x13, starting transfers between devices, send(): return lax.ppermute(value, 'tp', perm)  8.64 us
    pallas_call x4, Pallas kernels, write(): pl.pallas_call(functools.partial(write_kernel, spots), out_shape=jax.Shap...  4.92 us
  transfers between devices with their start and end apart: 13, of which 2 were waited for; matrix products, arithmetic and copies ran while one was open for 0% of the time, Pallas kernels for 33%

profile of v8, /device:TPU:0, one launch (start us, length us, event | category | flops | bytes accessed | tf_op | source)
XLA Modules:
  0.0 136.2 jit_solution(10837508578842222888)
XLA Ops:
  0.6 64.1 %scatter.1 = (bf16[512,1536]{1,0:T(8,128)(2,1)S(1)}, bf16[256,1536]{1,0:T(8,128)(2,1)}, bf16[256,1536]{1,0:T(8,128)(2,1)S(1)}, bf16[2048,1024]{1,0:T(8,128)(2,1)...) custom-call(bf16[2048,3072]{1,0:T(8,128)(2,1)} %dy.3, ...), custom_call_target="tpu_custom_call" | custom-call | flops 38654705664 | bytes 62914560 | tf_op jit(solution)/shard_map/scatter/pallas_call | solution.py:331
  64.7 1.6 %collective-permute-start.10 = (bf16[512,1536]{1,0:T(8,128)(2,1)S(1)}, bf16[512,1536]{1,0:T(8,128)(2,1)S(1)}, u32[]{:S(2)}, u32[]{:S(2)}) collective-permute-start(bf16[512,1536]{1,0:T(8,128)(2,1)S(1)} %get-tuple-element.21.refs_0_), channel_id=1, source_target_pairs={{0,4},{1,3},{2,6},{3,1},{4,0},{5,7},{6,2},{7,5}} | collective-permute-start | bytes 4718600 | tf_op jit(solution)/shard_map/ppermute | solution.py:535
  66.4 0.1 collective-permute-start.12
  66.5 1.4 %collective-permute-start = (bf16[256,1536]{1,0:T(8,128)(2,1)S(1)}, bf16[256,1536]{1,0:T(8,128)(2,1)S(1)}, u32[]{:S(2)}, u32[]{:S(2)}) collective-permute-start(bf16[256,1536]{1,0:T(8,128)(2,1)S(1)} %get-tuple-element.19), channel_id=1, source_target_pairs={{0,2},{1,5},{2,0},{3,7},{4,6},{5,1},{6,4},{7,3}} | collective-permute-start | bytes 2359304 | tf_op jit(solution)/shard_map/ppermute | solution.py:535
  67.9 0.6 collective-permute-start.5
  68.5 16.6 %wide_grads.2 = (bf16[3072,1024]{1,0:T(8,128)(2,1)}, bf16[3072,1024]{1,0:T(8,128)(2,1)}, bf16[2048,512]{1,0:T(8,128)(2,1)S(1)}) custom-call(bf16[2048,3072]{1,0:T(8,128)(2,1)} %x.3, bf16[2048,1024]{1,0:T(8,128)(2,1)S(1)} %get-tuple-element.24.d_gate, bf16[2048,1024]{1,0:T(8,128)(2,1)S(1)} %get-tuple-element.25.d_up, bf16[2048,3072]{1,0:T(8,128)(2,1)} %x.3), custom_call_target="tpu_custom_call" | custom-call | flops 12884901888 | bytes 20971520 | tf_op jit(solution)/shard_map/wide_grads/pallas_call | solution.py:420
  85.1 1.8 %collective-permute-done.refs_3_ = bf16[256,1536]{1,0:T(8,128)(2,1)S(1)} collective-permute-done((bf16[256,1536]{1,0:T(8,128)(2,1)S(1)}, bf16[256,1536]{1,0:T(8,128)(2,1)S(1)}, u32[]{:S(2)}, u32[]{:S(2)}) %collective-permute-start) | collective-permute-done | bytes 786464 | tf_op jit(solution)/shard_map/ppermute | solution.py:535
  86.9 1.5 %collective-permute-start.3 = (bf16[192,1536]{1,0:T(8,128)(2,1)S(1)}, bf16[192,1536]{1,0:T(8,128)(2,1)S(1)}, u32[]{:S(2)}, u32[]{:S(2)}) collective-permute-start(bf16[192,1536]{1,0:T(8,128)(2,1)S(1)} %slice.9), channel_id=1, source_target_pairs={{0,4},{1,3},{2,6},{3,1},{4,0},{5,7},{6,2},{7,5}} | collective-permute-start | bytes 1769480 | tf_op jit(solution)/shard_map/ppermute | solution.py:535
  88.5 0.6 collective-permute-start.1
  89.0 14.7 %collective-permute-done.5.refs_2_ = bf16[256,1536]{1,0:T(8,128)(2,1)S(1)} collective-permute-done((bf16[256,1536]{1,0:T(8,128)(2,1)}, bf16[256,1536]{1,0:T(8,128)(2,1)S(1)}, u32[]{:S(2)}, u32[]{:S(2)}) %collective-permute-start.5) | collective-permute-done | bytes 786464 | tf_op jit(solution)/shard_map/ppermute | solution.py:535
  103.8 1.5 %collective-permute-start.6 = (bf16[256,1536]{1,0:T(8,128)(2,1)S(1)}, bf16[256,1536]{1,0:T(8,128)(2,1)S(1)}, u32[]{:S(2)}, u32[]{:S(2)}) collective-permute-start(bf16[256,1536]{1,0:T(8,128)(2,1)S(1)} %collective-permute-done.5.refs_2_), channel_id=1, source_target_pairs={{0,4},{1,3},{2,6},{3,1},{4,0},{5,7},{6,2},{7,5}} | collective-permute-start | bytes 2359304 | tf_op jit(solution)/shard_map/ppermute | solution.py:535
  105.2 0.0 collective-permute-done.10.refs_4_
  105.2 0.0 collective-permute-start.11
  105.2 15.2 %wide_grads.3 = (bf16[3072,1024]{1,0:T(8,128)(2,1)}, bf16[3072,1024]{1,0:T(8,128)(2,1)}, bf16[2048,512]{1,0:T(8,128)(2,1)S(1)}) custom-call(bf16[2048,3072]{1,0:T(8,128)(2,1)} %x.3, bf16[2048,1024]{1,0:T(8,128)(2,1)S(1)} %get-tuple-element.24.d_gate, bf16[2048,1024]{1,0:T(8,128)(2,1)S(1)} %get-tuple-element.25.d_up, ...), custom_call_target="tpu_custom_call", output_to_operand_aliasing={{0}: (5, {}), {1}: (6, {})} | custom-call | flops 12884901888 | bytes 20971520 | tf_op jit(solution)/shard_map/wide_grads/pallas_call | solution.py:420
  120.5 0.0 collective-permute-done.1.refs_1_
  120.5 0.3 collective-permute-start.9
  120.8 0.0 collective-permute-done.3.refs_1_
  120.8 0.3 collective-permute-start.8
  121.0 0.0 collective-permute-done.12.refs_1_
  121.0 0.3 collective-permute-start.4
  121.3 0.0 collective-permute-done.6.refs_3_
  121.3 0.3 collective-permute-start.7
  121.5 9.2 %down_grad.1 = (bf16[1024,3072]{1,0:T(8,128)(2,1)}, bf16[2048,3072]{1,0:T(8,128)(2,1)}) custom-call(bf16[2048,1024]{1,0:T(8,128)(2,1)S(1)} %get-tuple-element.22.hidden, bf16[2048,3072]{1,0:T(8,128)(2,1)} %dy.3, bf16[1024,1536]{1,0:T(8,128)(2,1)S(1)} %get-tuple-element.23.block, bf16[2048,512]{1,0:T(8,128)(2,1)S(1)} %get-tuple-element.29.first, ...), custom_call_target="tpu_custom_call" | custom-call | flops 12884901888 | bytes 25165824 | tf_op jit(solution)/shard_map/down_grad/pallas_call | solution.py:477
  130.8 0.0 collective-permute-done.9.refs_1_
  130.8 0.3 collective-permute-start.2
  131.1 0.0 collective-permute-done.8.refs_0_
  131.1 0.0 collective-permute-done.11.refs_2_
  131.1 2.0 %write.4.refs_2_ = bf16[2048,3072]{1,0:T(8,128)(2,1)} custom-call(bf16[256,1536]{1,0:T(8,128)(2,1)S(1)} %collective-permute-done.8.refs_0_, bf16[256,1536]{1,0:T(8,128)(2,1)S(1)} %collective-permute-done.9.refs_1_, bf16[512,1536]{1,0:T(8,128)(2,1)S(1)} %collective-permute-done.11.refs_2_, ...), custom_call_target="tpu_custom_call", output_to_operand_aliasing={{}: (4, {})} | custom-call | flops 1000000000 | bytes 25165824 | tf_op jit(solution)/shard_map/write/pallas_call | solution.py:507
  133.1 0.0 collective-permute-done.7.refs_0_
  133.2 1.2 write.5.refs_2_
  134.3 0.0 collective-permute-done.4.refs_0_
  134.3 1.0 write.6.refs_1_
  135.3 0.0 collective-permute-done.2.refs_0_
  135.3 0.7 write.7
  (2 shorter events, 0.1 us)
Async XLA Ops:
  64.7 40.5 %collective-permute-start.10 = (bf16[512,1536]{1,0:T(8,128)(2,1)S(1)}, bf16[512,1536]{1,0:T(8,128)(2,1)S(1)}, u32[]{:S(2)}, u32[]{:S(2)}) collective-permute-start(bf16[512,1536]{1,0:T(8,128)(2,1)S(1)} %get-tuple-element.21.refs_0_), channel_id=1, source_target_pairs={{0,4},{1,3},{2,6},{3,1},{4,0},{5,7},{6,2},{7,5}} | collective-permute-start | bytes 4718600 | tf_op jit(solution)/shard_map/ppermute | solution.py:535
  66.4 54.7 %collective-permute-start.12 = (bf16[512,1536]{1,0:T(8,128)(2,1)S(1)}, bf16[512,1536]{1,0:T(8,128)(2,1)S(1)}, u32[]{:S(2)}, u32[]{:S(2)}) collective-permute-start(bf16[512,1536]{1,0:T(8,128)(2,1)S(1)} %get-tuple-element.21.refs_0_), channel_id=1, source_target_pairs={{0,1},{1,0},{2,3},{3,2},{4,5},{5,4},{6,7},{7,6}} | collective-permute-start | bytes 4718600 | tf_op jit(solution)/shard_map/ppermute | solution.py:535
  66.5 20.4 %collective-permute-start = (bf16[256,1536]{1,0:T(8,128)(2,1)S(1)}, bf16[256,1536]{1,0:T(8,128)(2,1)S(1)}, u32[]{:S(2)}, u32[]{:S(2)}) collective-permute-start(bf16[256,1536]{1,0:T(8,128)(2,1)S(1)} %get-tuple-element.19), channel_id=1, source_target_pairs={{0,2},{1,5},{2,0},{3,7},{4,6},{5,1},{6,4},{7,3}} | collective-permute-start | bytes 2359304 | tf_op jit(solution)/shard_map/ppermute | solution.py:535
  67.9 35.9 %collective-permute-start.5 = (bf16[256,1536]{1,0:T(8,128)(2,1)}, bf16[256,1536]{1,0:T(8,128)(2,1)S(1)}, u32[]{:S(2)}, u32[]{:S(2)}) collective-permute-start(bf16[256,1536]{1,0:T(8,128)(2,1)} %get-tuple-element.20), channel_id=1, source_target_pairs={{0,2},{1,5},{2,0},{3,7},{4,6},{5,1},{6,4},{7,3}} | collective-permute-start | bytes 2359304 | tf_op jit(solution)/shard_map/ppermute | solution.py:535
  86.9 33.8 %collective-permute-start.3 = (bf16[192,1536]{1,0:T(8,128)(2,1)S(1)}, bf16[192,1536]{1,0:T(8,128)(2,1)S(1)}, u32[]{:S(2)}, u32[]{:S(2)}) collective-permute-start(bf16[192,1536]{1,0:T(8,128)(2,1)S(1)} %slice.9), channel_id=1, source_target_pairs={{0,4},{1,3},{2,6},{3,1},{4,0},{5,7},{6,2},{7,5}} | collective-permute-start | bytes 1769480 | tf_op jit(solution)/shard_map/ppermute | solution.py:535
  88.5 32.0 %collective-permute-start.1 = (bf16[64,1536]{1,0:T(8,128)(2,1)S(1)}, bf16[64,1536]{1,0:T(8,128)(2,1)S(1)}, u32[]{:S(2)}, u32[]{:S(2)}) collective-permute-start(bf16[64,1536]{1,0:T(8,128)(2,1)S(1)} %slice.8), channel_id=1, source_target_pairs={{0,4},{1,3},{2,6},{3,1},{4,0},{5,7},{6,2},{7,5}} | collective-permute-start | bytes 589832 | tf_op jit(solution)/shard_map/ppermute | solution.py:535
  103.8 17.5 %collective-permute-start.6 = (bf16[256,1536]{1,0:T(8,128)(2,1)S(1)}, bf16[256,1536]{1,0:T(8,128)(2,1)S(1)}, u32[]{:S(2)}, u32[]{:S(2)}) collective-permute-start(bf16[256,1536]{1,0:T(8,128)(2,1)S(1)} %collective-permute-done.5.refs_2_), channel_id=1, source_target_pairs={{0,4},{1,3},{2,6},{3,1},{4,0},{5,7},{6,2},{7,5}} | collective-permute-start | bytes 2359304 | tf_op jit(solution)/shard_map/ppermute | solution.py:535
  105.2 25.9 %collective-permute-start.11 = (bf16[512,1536]{1,0:T(8,128)(2,1)S(1)}, bf16[512,1536]{1,0:T(8,128)(2,1)S(1)}, u32[]{:S(2)}, u32[]{:S(2)}) collective-permute-start(bf16[512,1536]{1,0:T(8,128)(2,1)S(1)} %collective-permute-done.10.refs_4_), channel_id=1, source_target_pairs={{0,1},{1,0},{2,3},{3,2},{4,5},{5,4},{6,7},{7,6}} | collective-permute-start | bytes 4718600 | tf_op jit(solution)/shard_map/ppermute | solution.py:535
  120.5 10.3 %collective-permute-start.9 = (bf16[256,1536]{1,0:T(8,128)(2,1)S(1)}, bf16[256,1536]{1,0:T(8,128)(2,1)S(1)}, u32[]{:S(2)}, u32[]{:S(2)}) collective-permute-start(bf16[256,1536]{1,0:T(8,128)(2,1)S(1)} %collective-permute-done.refs_3_), channel_id=1, source_target_pairs={{0,1},{1,0},{2,3},{3,2},{4,5},{5,4},{6,7},{7,6}} | collective-permute-start | bytes 2359304 | tf_op jit(solution)/shard_map/ppermute | solution.py:535
  120.8 10.3 %collective-permute-start.8 = (bf16[256,1536]{1,0:T(8,128)(2,1)S(1)}, bf16[256,1536]{1,0:T(8,128)(2,1)S(1)}, u32[]{:S(2)}, u32[]{:S(2)}) collective-permute-start(bf16[256,1536]{1,0:T(8,128)(2,1)S(1)} %collective-permute-done.5.refs_2_), channel_id=1, source_target_pairs={{0,1},{1,0},{2,3},{3,2},{4,5},{5,4},{6,7},{7,6}} | collective-permute-start | bytes 2359304 | tf_op jit(solution)/shard_map/ppermute | solution.py:535
  121.0 13.3 %collective-permute-start.4 = (bf16[192,1536]{1,0:T(8,128)(2,1)S(1)}, bf16[192,1536]{1,0:T(8,128)(2,1)S(1)}, u32[]{:S(2)}, u32[]{:S(2)}) collective-permute-start(bf16[192,1536]{1,0:T(8,128)(2,1)S(1)} %collective-permute-done.3.refs_1_), channel_id=1, source_target_pairs={{0,1},{1,0},{2,3},{3,2},{4,5},{5,4},{6,7},{7,6}} | collective-permute-start | bytes 1769480 | tf_op jit(solution)/shard_map/ppermute | solution.py:535
  121.3 11.9 %collective-permute-start.7 = (bf16[256,1536]{1,0:T(8,128)(2,1)S(1)}, bf16[256,1536]{1,0:T(8,128)(2,1)S(1)}, u32[]{:S(2)}, u32[]{:S(2)}) collective-permute-start(bf16[256,1536]{1,0:T(8,128)(2,1)S(1)} %collective-permute-done.6.refs_3_), channel_id=1, source_target_pairs={{0,1},{1,0},{2,3},{3,2},{4,5},{5,4},{6,7},{7,6}} | collective-permute-start | bytes 2359304 | tf_op jit(solution)/shard_map/ppermute | solution.py:535
  130.8 4.5 %collective-permute-start.2 = (bf16[64,1536]{1,0:T(8,128)(2,1)S(1)}, bf16[64,1536]{1,0:T(8,128)(2,1)S(1)}, u32[]{:S(2)}, u32[]{:S(2)}) collective-permute-start(bf16[64,1536]{1,0:T(8,128)(2,1)S(1)} %collective-permute-done.1.refs_1_), channel_id=1, source_target_pairs={{0,1},{1,0},{2,3},{3,2},{4,5},{5,4},{6,7},{7,6}} | collective-permute-start | bytes 589832 | tf_op jit(solution)/shard_map/ppermute | solution.py:535
